TPU v7x, 256 devices: a whole 4x4x8 slice. The times are simulated.
256 devices in a mesh: rep: 32 (over x, y, core), head: 8 (over z).
Axes of the slice: x: 4, y: 4, z: 8, core: 2. Of those that a mesh axis runs over, the one named last changes fastest.
Arguments:
- ssd_x: bfloat16 [8192, 8192], P('rep', 'head'), may hold values from -6 to 6
- gate_z: bfloat16 [8192, 8192], P('rep', 'head'), may hold values from -6 to 6
- group_b: bfloat16 [8192, 1024], P('rep', 'head'), may hold values from -6 to 6
- group_c: bfloat16 [8192, 1024], P('rep', 'head'), may hold values from -0.5 to 0.5
- step_dt: bfloat16 [8192, 128], P('rep', 'head'), may hold values from 0.5 to 2
- queries: bfloat16 [8192, 8192], P('rep', 'head'), may hold values from -8 to 8
- tail_kv: bfloat16 [8192, 2048], P('rep', 'head'), may hold values from -6 to 6
- ckpt_state: bfloat16 [512, 128, 64, 128], P('rep', 'head'), may hold values from -6 to 6
- kv_pool: bfloat16 [8192, 16, 2048], P('rep', None, 'head'), may hold values from -8 to 8
- w_out: bfloat16 [8192, 4096], P('head', 'rep'), may hold values from -0.125 to 0.125
- decay_rate: float32 [128], P('head'), may hold values from 0.002 to 2
- skip_d: float32 [128], P('head'), may hold values from 0.5 to 1.5
- norm_gain: float32 [8192], P('head'), may hold values from 0.5 to 1.5
- owner: int32 [512], replicated, may hold values from 0 to 31, as said below
- slot: int32 [512], replicated, may hold values from 0 to 15, as said below
- page_table: int32 [512, 16], replicated, may hold values from 0 to 255, as said below
- hit_len: int32 [512], replicated, may hold values from 2 to 256, as said below
- tail_len: int32 [512], replicated, may hold values from 1 to 16, as said below
Outputs:
- ssd_out: bfloat16 [8192, 8192], P('rep', 'head')
- attn_proj: bfloat16 [8192, 4096], P('rep', 'head')
- final_state: bfloat16 [512, 128, 64, 128], P('rep', 'head')
Inputs may be any that keep to these rules, and one draw needn't show every extreme that they name: Every replica owns exactly 16 requests, and no two requests of one replica share an owner. `slot`: the requests of one owner have distinct slots. `page_table`: each of an owner's 256 pages belongs to exactly one of its requests. `hit_len`: some request has exactly 256. `tail_len`: some request has exactly 16.
All inputs are finite; a program needn't handle non-finite values.
Results may differ from a plain program's by a relative error of at most 0.0057.
Values may be sent and summed in bfloat16 or wider, within the bound.
No kernel may reach another device: no remote copies, remote signals or barrier semaphores. Data moves between devices by JAX's collectives and lax.ppermute only.
A program may use at most 192 MiB of HBM per device.

v0:
```python
import math

import jax
import jax.numpy as jnp
from jax import lax
from jax.experimental import pallas as pl
from jax.experimental.pallas import tpu as pltpu
from jax.sharding import PartitionSpec as P


TAIL = 16
STATE = 128
QH = 8
DH = 128
REQ = 16
REPS = 32
HEADS = 16
HD = 64
PAGES = 16
CACHE = 256
TOK = REQ * TAIL
WIDTH = HEADS * HD
QW = QH * DH + 2 * DH
NHEAD = 8
NEAR = (0, -1, 1, 2)
SIZES = (14, 2)
STARTS = (0, 14)
STEPS = (2, 4)
CHUNKS = len(SIZES)
ROOM = 4 * TAIL * DH // (HD * STATE)

f32 = jnp.float32
bf16 = jnp.bfloat16
SMEM = pl.BlockSpec(memory_space=pltpu.SMEM)
VMEM = pl.BlockSpec(memory_space=pltpu.VMEM)
ANY = pl.BlockSpec(memory_space=pl.ANY)
NT = (((1,), (1,)), ((), ()))


def dot(a, b):
    return jnp.dot(a, b, preferred_element_type=f32)


def split2(v):
    hi = v.astype(bf16)
    return hi, (v - hi.astype(f32)).astype(bf16)


def split3(v):
    hi = v.astype(bf16)
    rest = v - hi.astype(f32)
    mid = rest.astype(bf16)
    return hi, mid, (rest - mid.astype(f32)).astype(bf16)


def sds(shape, dtype):
    return jax.ShapeDtypeStruct(shape, dtype)


def params(**kw):
    return pltpu.CompilerParams(**kw)


def pack_q_body(me, owner, q, kv, out, sem):
    base = me[0] * REQ
    for j in range(REQ):
        o = owner[base + j]
        rows = pl.ds(j * TAIL, TAIL)
        pltpu.make_async_copy(q.at[rows], out.at[o, :, pl.ds(0, QH * DH)], sem.at[0]).start()
        pltpu.make_async_copy(kv.at[rows], out.at[o, :, pl.ds(QH * DH, 2 * DH)], sem.at[1]).start()
    pltpu.make_async_copy(q, q, sem.at[0]).wait()
    pltpu.make_async_copy(kv, kv, sem.at[1]).wait()


def pack_q(me, owner, q, kv):
    return pl.pallas_call(
        pack_q_body,
        out_shape=sds((REPS, TAIL, QW), bf16),
        in_specs=[SMEM, SMEM, VMEM, VMEM],
        out_specs=ANY,
        scratch_shapes=[pltpu.SemaphoreType.DMA((2,))],
        name="pack_q",
    )(me, owner, q, kv)


def pack_s_body(me, owner, slot, ckpt, *rest):
    outs = rest[:CHUNKS]
    req, buf, come, go = rest[CHUNKS:]
    mine = me[0]
    for s in range(REQ):
        pltpu.make_async_copy(ckpt.at[s], buf.at[s], come.at[s]).start()

    def home(h, carry):
        s = jnp.int32(0)
        g = jnp.int32(0)
        for j in range(REQ):
            hit = owner[h * REQ + j] == mine
            s = jnp.where(hit, slot[h * REQ + j] + 1, s)
            g = jnp.where(hit, h * REQ + j, g)

        @pl.when(s > 0)
        def _():
            req[s - 1] = g

        return carry

    lax.fori_loop(0, REPS, home, 0)
    for s in range(REQ):
        pltpu.make_async_copy(ckpt.at[s], buf.at[s], come.at[s]).wait()
        for c in range(CHUNKS):
            pltpu.make_async_copy(
                buf.at[s, pl.ds(STARTS[c], SIZES[c])],
                outs[c].at[req[s] // REQ, pl.ds(0, SIZES[c])],
                go.at[c],
            ).start()
    for c in range(CHUNKS):
        part = buf.at[:, pl.ds(STARTS[c], SIZES[c])]
        pltpu.make_async_copy(part, part, go.at[c]).wait()


def pack_s(me, owner, slot, ckpt):
    depth = [n + (ROOM if c == CHUNKS - 1 else 0) for c, n in enumerate(SIZES)]
    out = pl.pallas_call(
        pack_s_body,
        out_shape=[sds((REPS, n, HD, STATE), bf16) for n in depth] + [sds((REQ,), jnp.int32)],
        in_specs=[SMEM, SMEM, SMEM, ANY],
        out_specs=[ANY] * CHUNKS + [SMEM],
        scratch_shapes=[
            pltpu.VMEM((REQ, HEADS, HD, STATE), bf16),
            pltpu.SemaphoreType.DMA((REQ,)),
            pltpu.SemaphoreType.DMA((CHUNKS,)),
        ],
        name="pack_s",
    )(me, owner, slot, ckpt)
    return out[:CHUNKS], out[CHUNKS]


def attend_body(req, pages, hit, tail, qin, pool, out):
    row = lax.broadcasted_iota(jnp.int32, (QH * TAIL, CACHE + DH), 0) & (TAIL - 1)
    col = lax.broadcasted_iota(jnp.int32, (QH * TAIL, CACHE + DH), 1)
    late = col - CACHE
    causal = (late >= 0) & (late <= row)
    time = lax.broadcasted_iota(jnp.int32, (QH * TAIL, DH), 0) & (TAIL - 1)
    pad = jnp.zeros((DH - TAIL, DH), bf16)
    scale = 1.0 / math.sqrt(DH)

    def one(s, carry):
        g = req[s]
        q = qin[g // REQ]
        rows = jnp.concatenate([q[:, a * DH : (a + 1) * DH] for a in range(QH)], axis=0)
        held = [pool[pages[g * PAGES + i]] for i in range(PAGES)]
        keys = jnp.concatenate(
            [p[:, :DH] for p in held] + [q[:, QH * DH : QH * DH + DH], pad], axis=0
        )
        vals = jnp.concatenate([p[:, DH:] for p in held] + [q[:, QH * DH + DH :], pad], axis=0)
        scores = lax.dot_general(rows, keys, NT, preferred_element_type=f32) * scale
        visible = (col < hit[g]) | (causal & (late < tail[g]))
        scores = jnp.where(visible, scores, -1e30)
        top = jnp.max(scores, axis=1, keepdims=True)
        expo = jnp.where(visible, jnp.exp(scores - top), 0.0)
        weights = (expo / jnp.sum(expo, axis=1, keepdims=True)).astype(bf16)
        res = dot(weights, vals)
        res = jnp.where(time < tail[g], res, 0.0).astype(bf16)
        for a in range(QH):
            out[pl.ds(pl.multiple_of(s * TAIL, TAIL), TAIL), a * DH : (a + 1) * DH] = res[
                a * TAIL : (a + 1) * TAIL
            ]
        return carry

    lax.fori_loop(0, REQ, one, 0, unroll=2)


def attend(req, pages, hit, tail, qin, pool):
    return pl.pallas_call(
        attend_body,
        out_shape=sds((TOK, QH * DH), bf16),
        in_specs=[SMEM, SMEM, SMEM, SMEM, VMEM, VMEM],
        out_specs=VMEM,
        cost_estimate=pl.CostEstimate(
            flops=8_000_000_000, transcendentals=0, bytes_accessed=4_000_000
        ),
        name="attend",
    )(req, pages, hit, tail, qin, pool)


def spot(k, i):
    base = jnp.int32(12)
    for dist, start in ((1, 16), (2, 0), (3, 20), (5, 28), (6, 6), (7, 24)):
        base = jnp.where(k == dist, start, base)
    base = jnp.where(k == 4, jnp.where(i < 2, 4, 8), base)
    return base + i


def project_body(me, head, attn, a_near, b_near, a_far, b_far, out):
    x = me[0] // 8
    y = (me[0] // 2) & 3
    par = me[0] & 1
    step = pl.program_id(0)
    off = jnp.where(step == 3, 2, jnp.where(step == 1, -1, jnp.where(step == 2, 1, 0)))
    cy = (y + off) & 3
    half = QH * DH // 2
    for far, (wa, wb) in enumerate(((a_near, b_near), (a_far, b_far))):
        core = 1 - par if far else par
        for d in (0, 2):
            res = dot(attn[:, :half], jnp.concatenate([wa[0, d], wa[0, d + 1]], axis=1)) + dot(
                attn[:, half:], jnp.concatenate([wb[d, 0], wb[d + 1, 0]], axis=1)
            )
            res = res.astype(bf16)
            for k in range(2):
                col = ((x + NEAR[d + k]) & 3) * 8 + cy * 2 + core
                out[spot(((col // 4) - head[0]) & (NHEAD - 1), col & 3)] = res[
                    :, k * DH : (k + 1) * DH
                ]


def project(me, head, attn, a_near, b_near, a_far, b_far):
    half = QH * DH // 2
    wa = pl.BlockSpec((1, 4, half, DH), lambda i: (i, 0, 0, 0))
    wb = pl.BlockSpec((4, 1, half, DH), lambda i: (0, i, 0, 0))
    return pl.pallas_call(
        project_body,
        grid=(4,),
        out_shape=sds((4 * NHEAD, TOK, DH), bf16),
        in_specs=[SMEM, SMEM, pl.BlockSpec((TOK, QH * DH), lambda i: (0, 0)), wa, wb, wa, wb],
        out_specs=pl.BlockSpec((4 * NHEAD, TOK, DH), lambda i: (0, 0, 0)),
        compiler_params=params(dimension_semantics=("arbitrary",)),
        cost_estimate=pl.CostEstimate(
            flops=8_000_000_000, transcendentals=0, bytes_accessed=11_000_000
        ),
        name="project",
    )(me, head, attn, a_near, b_near, a_far, b_far)


def relay_body(terms, up, down, one, three, seven, five):
    def add(a, b):
        return (a.astype(f32) + b.astype(f32)).astype(bf16)

    one[...] = add(terms[16:20], up[0:4])
    three[0:2] = add(terms[20:22], up[4:6])
    three[2:4] = terms[22:24]
    seven[...] = add(terms[24:28], down[0:4])
    five[0:2] = terms[28:30]
    five[2:4] = add(terms[30:32], down[4:6])


def relay(terms, up, down):
    return pl.pallas_call(
        relay_body,
        out_shape=[sds((4, TOK, DH), bf16)] * 4,
        in_specs=[VMEM] * 3,
        out_specs=[VMEM] * 4,
        cost_estimate=pl.CostEstimate(
            flops=1_000_000_000, transcendentals=0, bytes_accessed=3_000_000
        ),
        name="relay",
    )(terms, up, down)


def total_body(req, terms, *rest):
    parts = rest[:4]
    out, tmp, sem = rest[5:]
    for i in range(4):
        acc = terms[12 + i].astype(f32)
        for p in parts:
            acc = acc + p[i].astype(f32)
        acc = acc.astype(bf16)
        for s in range(REQ):
            tmp[s, i * TAIL : (i + 1) * TAIL, :] = acc[s * TAIL : (s + 1) * TAIL]
    for s in range(REQ):
        pltpu.make_async_copy(tmp.at[s], out.at[req[s] // REQ, SIZES[-1]], sem.at[0]).start()
    pltpu.make_async_copy(tmp, tmp, sem.at[0]).wait()


def total(req, terms, parts, packed):
    return pl.pallas_call(
        total_body,
        out_shape=sds(packed.shape, bf16),
        in_specs=[SMEM] + [VMEM] * 5 + [ANY],
        out_specs=ANY,
        input_output_aliases={6: 0},
        scratch_shapes=[pltpu.VMEM((REQ, 4 * TAIL, DH), bf16), pltpu.SemaphoreType.DMA((1,))],
        cost_estimate=pl.CostEstimate(
            flops=1_000_000_000, transcendentals=0, bytes_accessed=3_000_000
        ),
        name="total",
    )(req, terms, *parts, packed)


def prepare_body(
    me, tail, x_ref, z_ref, b_ref, c_ref, dt_ref, rate, skip, base_ref, ecx_ref, xt_ref, dl_ref, tmp
):
    first = me[0] * REQ
    req16 = lax.broadcasted_iota(jnp.int32, (TOK, HEADS), 0) // TAIL
    tim16 = lax.broadcasted_iota(jnp.int32, (TOK, HEADS), 0) & (TAIL - 1)
    limit = jnp.zeros((TOK, HEADS), jnp.int32)
    for j in range(REQ):
        limit = jnp.where(req16 == j, tail[first + j], limit)
    live = (tim16 < limit).astype(f32)
    wdt = dt_ref[...].astype(f32) * live
    decay = -rate[...] * wdt
    r = lax.broadcasted_iota(jnp.int32, (TOK, TOK), 0)
    u = lax.broadcasted_iota(jnp.int32, (TOK, TOK), 1)
    same = (r // TAIL) == (u // TAIL)
    tri = same & (u <= r)
    trib = tri.astype(f32).astype(bf16)
    allb = same.astype(f32).astype(bf16)
    pieces = split3(decay)
    cum = dot(trib, pieces[0]) + dot(trib, pieces[1]) + dot(trib, pieces[2])
    last = dot(allb, pieces[0]) + dot(allb, pieces[1]) + dot(allb, pieces[2])
    tmp[...] = jnp.exp(last)
    dl_ref[...] = tmp[pl.ds(0, REQ, stride=TAIL), :]
    er = lax.broadcasted_iota(jnp.int32, (HEADS, WIDTH), 0)
    ec = lax.broadcasted_iota(jnp.int32, (HEADS, WIDTH), 1)
    onehot = ((ec // HD) == er).astype(f32).astype(bf16)

    def widen(v):
        a, b, c = split3(v)
        return dot(a, onehot) + dot(b, onehot) + dot(c, onehot)

    x = x_ref[...].astype(f32)
    hi, lo = split2(widen(jnp.exp(-cum) * wdt) * x)
    cb = jnp.where(
        tri, lax.dot_general(c_ref[...], b_ref[...], NT, preferred_element_type=f32), 0.0
    )
    chi, clo = split2(cb)
    within = dot(chi, hi) + dot(chi, lo) + dot(clo, hi)
    z = z_ref[...].astype(f32)
    gate = z / (1.0 + jnp.exp(-z))
    ecx = widen(jnp.exp(cum) * live)
    base_ref[...] = (ecx * within + widen(skip[...] * live) * x) * gate
    ecx_ref[...] = ecx * gate
    hi, lo = split2(widen(jnp.exp(last - cum) * wdt) * x)
    for k in range(2):
        rows = slice(k * 128, (k + 1) * 128)
        xt_ref[k, :, :128] = hi[rows].T
        xt_ref[k, :, 128:] = lo[rows].T


def prepare(me, tail, x, z, b, c, dt, rate, skip):
    return pl.pallas_call(
        prepare_body,
        out_shape=[
            sds((TOK, WIDTH), f32),
            sds((TOK, WIDTH), f32),
            sds((2, WIDTH, 256), bf16),
            sds((REQ, HEADS), f32),
        ],
        in_specs=[SMEM, SMEM] + [VMEM] * 7,
        out_specs=[VMEM] * 4,
        scratch_shapes=[pltpu.VMEM((TOK, HEADS), f32)],
        cost_estimate=pl.CostEstimate(
            flops=8_000_000_000, transcendentals=0, bytes_accessed=5_000_000
        ),
        name="prepare",
    )(me, tail, x, z, b, c, dt, rate, skip)


def scan_body(chunk, *refs):
    refs = list(refs)
    heads = SIZES[chunk]
    count = STEPS[chunk]
    width = heads * HD
    final_chunk = chunk == CHUNKS - 1
    dl = refs[2]
    held = refs[3 : 3 + count]
    b_ref, c_ref, xt, base, ecx = refs[3 + count : 8 + count]
    refs = refs[8 + count :]
    prev = []
    if chunk > 0:
        prev = refs[1 : 1 + chunk]
        refs = refs[1 + chunk :]
    if final_chunk:
        gain, fin, out, proj = refs
    else:
        fin, gated_ref = refs
    i = pl.program_id(0)
    states = [s[0, :heads].reshape(width, STATE) for s in held]
    seen = jnp.concatenate(
        [
            lax.dot_general(
                c_ref[k * TAIL : (k + 1) * TAIL, :], states[k], NT, preferred_element_type=f32
            )
            for k in range(count)
        ],
        axis=0,
    )
    gated = base[...] + ecx[...] * seen
    if final_chunk:
        parts = [p[...] for p in prev] + [gated]
        energy = sum(jnp.sum(p * p, axis=1, keepdims=True) for p in parts)
        denom = jnp.sqrt(energy / WIDTH + 1e-5)
        for c in range(CHUNKS):
            cols = slice(STARTS[c] * HD, (STARTS[c] + SIZES[c]) * HD)
            out[:, cols] = (parts[c] / denom * gain[:, cols]).astype(bf16)
        for k, s in enumerate(held):
            for c in range(4):
                proj[k * TAIL : (k + 1) * TAIL, c * DH : (c + 1) * DH] = s[
                    0, heads, c * TAIL : (c + 1) * TAIL, :
                ]
    else:
        gated_ref[...] = gated
    who = lax.broadcasted_iota(jnp.int32, (128, STATE), 0) // TAIL
    rows = b_ref[...].astype(f32)
    at = (count * i) & 7
    mine = jnp.concatenate(
        [jnp.where(who == at + k, rows, 0.0).astype(bf16) for k in range(count)], axis=1
    )
    update = dot(xt[0], jnp.concatenate([mine, mine], axis=0))
    for k in range(count):
        for e in range(heads):
            rr = slice(e * HD, (e + 1) * HD)
            fin[k, e] = (
                dl[count * i + k, STARTS[chunk] + e] * states[k][rr].astype(f32)
                + update[rr, k * STATE : (k + 1) * STATE]
            ).astype(bf16)


def scan(chunk, me, owner, dl, got, b, c, xt, base, ecx, fin, prev, gain):
    final_chunk = chunk == CHUNKS - 1
    heads = SIZES[chunk]
    count = STEPS[chunk]
    width = heads * HD
    at = STARTS[chunk] // heads
    rows = count * TAIL

    def held(k):
        return pl.BlockSpec(
            (1,) + got.shape[1:], lambda i, m, o: (o[m[0] * REQ + count * i + k], 0, 0, 0)
        )

    def span(w, col=0):
        return pl.BlockSpec((rows, w), lambda i, m, o: (i, col))

    in_specs = [SMEM] + [held(k) for k in range(count)]
    in_specs += [
        pl.BlockSpec((128, STATE), lambda i, m, o: (i * count // 8, 0)),
        span(STATE),
        pl.BlockSpec((1, width, 256), lambda i, m, o: (i * count // 8, at, 0)),
        span(width, at),
        span(width, at),
    ]
    args = [dl] + [got] * count + [b, c, xt, base, ecx]
    alias = {}
    if chunk > 0:
        alias = {2 + len(args): 0}
        in_specs += [ANY] + [span(p.shape[1]) for p in prev]
        args += [fin] + prev
    out_specs = [pl.BlockSpec((count, heads, HD, STATE), lambda i, m, o: (i, at, 0, 0))]
    out_shape = [sds((REQ, HEADS, HD, STATE), bf16)]
    if final_chunk:
        in_specs.append(pl.BlockSpec((1, WIDTH), lambda i, m, o: (0, 0)))
        args.append(gain)
        out_specs += [span(WIDTH), span(4 * DH)]
        out_shape += [sds((TOK, WIDTH), bf16), sds((TOK, 4 * DH), bf16)]
    else:
        out_specs += [span(width)]
        out_shape += [sds((TOK, width), f32)]

    def body(*refs):
        scan_body(chunk, *refs)

    return pl.pallas_call(
        body,
        grid_spec=pltpu.PrefetchScalarGridSpec(
            num_scalar_prefetch=2,
            grid=(REQ // count,),
            in_specs=in_specs,
            out_specs=out_specs,
        ),
        out_shape=out_shape,
        input_output_aliases=alias,
        compiler_params=params(dimension_semantics=("arbitrary",)),
        cost_estimate=pl.CostEstimate(
            flops=4_000_000_000, transcendentals=0, bytes_accessed=8_000_000
        ),
    )(me, owner, *args)


def exchange(x, axis):
    return lax.all_to_all(x, axis, split_axis=0, concat_axis=0, tiled=True)


def place(x, y, core):
    return (x & 3) * 8 + (y & 3) * 2 + core


def hop(v, axis, by):
    dx, dy = (by, 0) if axis == "x" else (0, by)
    pairs = [
        (place(x, y, c), place(x + dx, y + dy, c))
        for x in range(4)
        for y in range(4)
        for c in range(2)
    ]
    return lax.ppermute(v, "rep", pairs)


def ring(v, axis):
    return jnp.stack([v, hop(v, axis, 1), hop(v, axis, -1), hop(v, axis, 2)])


def sides(v, axis):
    return hop(v, axis, 1), hop(v, axis, -1)


def across(v, axis, left, right):
    n = v.shape[0] // 2
    far = jnp.concatenate([hop(right[:n], axis, -1), hop(left[n:], axis, 1)], axis=0)
    return jnp.stack([v, left, right, far])


def turn(v, by):
    return lax.ppermute(v, "head", [(z, (z + by) % NHEAD) for z in range(NHEAD)])


def step(
    ssd_x,
    gate_z,
    group_b,
    group_c,
    step_dt,
    queries,
    tail_kv,
    ckpt_state,
    kv_pool,
    w_out,
    decay_rate,
    skip_d,
    norm_gain,
    owner,
    slot,
    page_table,
    hit_len,
    tail_len,
):
    me = lax.axis_index("rep").astype(jnp.int32).reshape(1)
    head = lax.axis_index("head").astype(jnp.int32).reshape(1)
    swap = [(r, r ^ 1) for r in range(REPS)]
    half = w_out.shape[0] // 2
    queued = pack_q(me, owner, queries, tail_kv)
    asked = exchange(queued, "rep")
    w_out = lax.optimization_barrier((w_out, queued))[0]
    a_half = ring(w_out[:half], "x")
    b_half = ring(w_out[half:], "y")
    a_side = sides(a_half, "y")
    b_side = sides(b_half, "x")
    a_near = across(a_half, "y", *a_side)
    b_near = across(b_half, "x", *b_side)
    a_far = lax.ppermute(a_near, "rep", swap)
    b_far = lax.ppermute(b_near, "rep", swap)
    packed, req = pack_s(me, owner, slot, ckpt_state)
    first = lax.optimization_barrier((packed[0], asked, a_near, b_near))[0]
    got = exchange(first, "rep")
    attn = attend(req, page_table.reshape(-1), hit_len, tail_len, asked, kv_pool)
    terms = project(me, head, attn, a_near, b_near, a_far, b_far)
    one, three, seven, five = relay(terms, turn(terms[0:6], 1), turn(terms[6:12], -1))
    parts = [turn(one, 1), turn(three, 3), turn(seven, -1), turn(five, -3)]
    base, ecx, xt, dl = prepare(
        me,
        tail_len,
        ssd_x,
        gate_z,
        group_b,
        group_c,
        step_dt,
        decay_rate.reshape(1, -1),
        skip_d.reshape(1, -1),
    )
    gain = norm_gain.reshape(1, -1)
    last = exchange(total(req, terms, parts, packed[1]), "rep")
    fin, rows = scan(0, me, owner, dl, got, group_b, group_c, xt, base, ecx, None, [], gain)
    fin, out, projected = scan(
        1, me, owner, dl, last, group_b, group_c, xt, base, ecx, fin, [rows], gain
    )
    return out, projected, fin


def solution(mesh):
    return jax.shard_map(
        step,
        mesh=mesh,
        in_specs=(
            P("rep", "head"),
            P("rep", "head"),
            P("rep", "head"),
            P("rep", "head"),
            P("rep", "head"),
            P("rep", "head"),
            P("rep", "head"),
            P("rep", "head", None, None),
            P("rep", None, "head"),
            P("head", "rep"),
            P("head"),
            P("head"),
            P("head"),
            P(),
            P(),
            P(),
            P(),
            P(),
        ),
        out_specs=(P("rep", "head"), P("rep", "head"), P("rep", "head", None, None)),
        check_vma=False,
    )
```

profile of v0, /device:TPU:1, one launch (start us, length us, event | category | flops | bytes accessed | tf_op | source)
XLA Modules:
  0.0 211.6 jit_solution(16390651987233266050)
XLA Ops:
  0.6 2.0 pack_q.1
  2.7 2.2 %collective-permute-start.7 = (bf16[512,128]{1,0:T(8,128)(2,1)S(1)}, bf16[512,128]{1,0:T(8,128)(2,1)S(1)}, u32[]{:S(2)}, u32[]{:S(2)}) collective-permute-start(bf16[512,128]{1,0:T(8,128)(2,1)S(1)} %get-tuple-element.47), channel_id=1, source_target_pairs={{0,16},{8,24},{16,32},{24,40},{32,48},{40,56},{48,0},{56,8},{64,80... | collective-permute-start | bytes 393224 | tf_op jit(solution)/shard_map/ppermute | solution.py:495
  4.9 1.5 collective-permute-start.8
  6.4 1.6 collective-permute-start.9
  9.2 1.5 collective-permute-start.1
  10.7 1.5 collective-permute-start.2
  13.7 3.1 %collective-permute-start.11 = (bf16[4,512,128]{2,1,0:T(8,128)(2,1)}, bf16[4,512,128]{2,1,0:T(8,128)(2,1)S(1)}, u32[]{:S(2)}, u32[]{:S(2)}) collective-permute-start(bf16[4,512,128]{2,1,0:T(8,128)(2,1)} %get-tuple-element.42), channel_id=1, source_target_pairs={{0,192},{8,200},{16,208},{24,216},{32,224},{40,232},{48,240},{56,2... | collective-permute-start | bytes 1572872 | tf_op jit(solution)/shard_map/ppermute | solution.py:495
  19.7 8.8 %all-to-all-start = ((bf16[32,16,1280]{2,1,0:T(8,128)(2,1)}), bf16[32,16,1280]{2,1,0:T(8,128)(2,1)}, u32[]{:S(2)}, u32[]{:S(2)}) async-start(bf16[32,16,1280]{2,1,0:T(8,128)(2,1)} %pack_q.1), calls=%async_computation | async-start | bytes 2621440 | tf_op jit(solution)/shard_map/all_to_all | solution.py:480
  28.6 2.7 %collective-permute-start.12 = (bf16[2,512,128]{2,1,0:T(8,128)(2,1)S(1)}, bf16[2,512,128]{2,1,0:T(8,128)(2,1)}, u32[]{:S(2)}, u32[]{:S(2)}) collective-permute-start(bf16[2,512,128]{2,1,0:T(8,128)(2,1)S(1)} %slice.34), channel_id=1, source_target_pairs={{0,192},{8,200},{16,208},{24,216},{32,224},{40,232},{48,240},{56,2... | collective-permute-start | bytes 786440 | tf_op jit(solution)/shard_map/ppermute | solution.py:495
  32.9 2.4 %collective-permute-start.5 = (bf16[2,512,128]{2,1,0:T(8,128)(2,1)}, bf16[2,512,128]{2,1,0:T(8,128)(2,1)}, u32[]{:S(2)}, u32[]{:S(2)}) collective-permute-start(bf16[2,512,128]{2,1,0:T(8,128)(2,1)} %slice.32), channel_id=1, source_target_pairs={{0,48},{8,56},{16,0},{24,8},{32,16},{40,24},{48,32},{56,40},{64,11... | collective-permute-start | bytes 786440 | tf_op jit(solution)/shard_map/ppermute | solution.py:495
  36.1 4.5 %pack_s.1 = (bf16[32,14,64,128]{3,2,1,0:T(8,128)(2,1)}, bf16[32,3,64,128]{3,2,1,0:T(8,128)(2,1)}, s32[16]{0:T(128)}) custom-call(s32[1]{0:T(128)} %bitcast.me.refs_0_, s32[512]{0:T(512)} %refs_1_.3, s32[512]{0:T(512)} %slot.1, bf16[16,16,64,128]{3,2,1,0:T(8,128)(2,1)} %ckpt.1), custom_call_target="tpu_custom_call" | custom-call | tf_op jit(solution)/shard_map/pack_s/pallas_call | solution.py:123
  40.7 9.7 %collective-permute-done.12 = bf16[2,512,128]{2,1,0:T(8,128)(2,1)} collective-permute-done((bf16[2,512,128]{2,1,0:T(8,128)(2,1)S(1)}, bf16[2,512,128]{2,1,0:T(8,128)(2,1)}, u32[]{:S(2)}, u32[]{:S(2)}) %collective-permute-start.12) | collective-permute-done | bytes 262176 | tf_op jit(solution)/shard_map/ppermute | solution.py:495
  50.4 1.3 collective-permute-done.13
  55.1 1.6 pad_maximum_fusion.a_near
  56.7 11.2 %all-to-all-start.2 = ((bf16[32,14,64,128]{3,2,1,0:T(8,128)(2,1)}), bf16[32,14,64,128]{3,2,1,0:T(8,128)(2,1)}, u32[]{:S(2)}, u32[]{:S(2)}) async-start(bf16[32,14,64,128]{3,2,1,0:T(8,128)(2,1)} %get-tuple-element.33), calls=%async_computation.2 | async-start | bytes 14680064 | tf_op jit(solution)/shard_map/all_to_all | solution.py:480
  69.4 9.5 %attend.1.attn = bf16[256,1024]{1,0:T(8,128)(2,1)} custom-call(s32[16]{0:T(128)} %get-tuple-element.22.req, s32[8192]{0:T(1024)} %reshape.28.pages, s32[512]{0:T(512)} %hit.1, s32[512]{0:T(512)} %tail.3, bf16[32,16,1280]{2,1,0:T(8,128)(2,1)} %all-to-all-done.qin, bf16[256,16,256]{2,1,0:T(8,128)(2,1)} %pool.1), custom_call_target="tpu_custom_call" | custom-call | flops 8000000000 | bytes 4000000 | tf_op jit(solution)/shard_map/attend/pallas_call | solution.py:174
  78.9 6.9 %project.1.terms = bf16[32,256,128]{2,1,0:T(8,128)(2,1)} custom-call(s32[1]{0:T(128)} %bitcast.me.refs_0_, s32[1]{0:T(128)} %bitcast.3.head, bf16[256,1024]{1,0:T(8,128)(2,1)} %attend.1.attn, bf16[4,4,512,128]{3,2,1,0:T(8,128)(2,1)} %pad_maximum_fusion.a_near, bf16[4,4,512,128]{3,2,1,0:T(8,128)(2,1)} %copy-done, ...), custom_call_target="tpu_custom_call" | custom-call | flops 8000000000 | bytes 11000000 | tf_op jit(solution)/shard_map/project/pallas_call | solution.py:220
  87.0 1.7 collective-permute-start.16
  88.7 4.0 %collective-permute-start.17 = (bf16[6,256,128]{2,1,0:T(8,128)(2,1)S(1)}, bf16[6,256,128]{2,1,0:T(8,128)(2,1)S(1)}, u32[]{:S(2)}, u32[]{:S(2)}) collective-permute-start(bf16[6,256,128]{2,1,0:T(8,128)(2,1)S(1)} %get-tuple-element.39), channel_id=1, source_target_pairs={{0,7},{1,0},{2,1},{3,2},{4,3},{5,4},{6,5},{7,6},{8,15},{9,8},{10,9... | collective-permute-start | bytes 1179656 | tf_op jit(solution)/shard_map/ppermute | solution.py:513
  92.8 9.2 %collective-permute-done.16.up = bf16[6,256,128]{2,1,0:T(8,128)(2,1)S(1)} collective-permute-done((bf16[6,256,128]{2,1,0:T(8,128)(2,1)S(1)}, bf16[6,256,128]{2,1,0:T(8,128)(2,1)S(1)}, u32[]{:S(2)}, u32[]{:S(2)}) %collective-permute-start.16) | collective-permute-done | bytes 393248 | tf_op jit(solution)/shard_map/ppermute | solution.py:513
  103.5 2.7 %relay.1 = (bf16[4,256,128]{2,1,0:T(8,128)(2,1)}, bf16[4,256,128]{2,1,0:T(8,128)(2,1)}, bf16[4,256,128]{2,1,0:T(8,128)(2,1)}, bf16[4,256,128]{2,1,0:T(8,128)(2,1)}) custom-call(bf16[32,256,128]{2,1,0:T(8,128)(2,1)} %project.1.terms, bf16[6,256,128]{2,1,0:T(8,128)(2,1)} %copy-done.17, bf16[6,256,128]{2,1,0:T(8,128)(2,1)} %copy-done.18), custom_call_target="tpu_custom_call" | custom-call | flops 1000000000 | bytes 3000000 | tf_op jit(solution)/shard_map/relay/pallas_call | solution.py:247
  106.2 4.0 %collective-permute-start.19 = (bf16[4,256,128]{2,1,0:T(8,128)(2,1)}, bf16[4,256,128]{2,1,0:T(8,128)(2,1)S(1)}, u32[]{:S(2)}, u32[]{:S(2)}) collective-permute-start(bf16[4,256,128]{2,1,0:T(8,128)(2,1)} %get-tuple-element.25), channel_id=1, source_target_pairs={{0,3},{1,4},{2,5},{3,6},{4,7},{5,0},{6,1},{7,2},{8,11},{9,12},{10,... | collective-permute-start | bytes 786440 | tf_op jit(solution)/shard_map/ppermute | solution.py:513
  110.2 1.7 collective-permute-start.20
  112.1 2.8 %collective-permute-done.18.rest_0_ = bf16[4,256,128]{2,1,0:T(8,128)(2,1)S(1)} collective-permute-done((bf16[4,256,128]{2,1,0:T(8,128)(2,1)}, bf16[4,256,128]{2,1,0:T(8,128)(2,1)S(1)}, u32[]{:S(2)}, u32[]{:S(2)}) %collective-permute-start.18) | collective-permute-done | bytes 262176 | tf_op jit(solution)/shard_map/ppermute | solution.py:513
  115.0 16.0 %collective-permute-done.19.rest_1_ = bf16[4,256,128]{2,1,0:T(8,128)(2,1)S(1)} collective-permute-done((bf16[4,256,128]{2,1,0:T(8,128)(2,1)}, bf16[4,256,128]{2,1,0:T(8,128)(2,1)S(1)}, u32[]{:S(2)}, u32[]{:S(2)}) %collective-permute-start.19) | collective-permute-done | bytes 262176 | tf_op jit(solution)/shard_map/ppermute | solution.py:513
  131.8 2.7 %total.1 = bf16[32,3,64,128]{3,2,1,0:T(8,128)(2,1)} custom-call(s32[16]{0:T(128)} %get-tuple-element.22.req, bf16[32,256,128]{2,1,0:T(8,128)(2,1)} %project.1.terms, bf16[4,256,128]{2,1,0:T(8,128)(2,1)} %copy-done.11, bf16[4,256,128]{2,1,0:T(8,128)(2,1)} %copy-done.12, bf16[4,256,128]{2,1,0:T(8,128)(2,1)} %copy-done.13, ...), custom_call_target="tpu_custom_call", output_to_operand_aliasing={{}: (6, {})} | custom-call | flops 1000000000 | bytes 3000000 | tf_op jit(solution)/shard_map/total/pallas_call | solution.py:275
  134.6 24.2 %all-to-all-done.2.refs_3_.refs_4_ = bf16[32,14,64,128]{3,2,1,0:T(8,128)(2,1)} async-done(((bf16[32,14,64,128]{3,2,1,0:T(8,128)(2,1)}), bf16[32,14,64,128]{3,2,1,0:T(8,128)(2,1)}, u32[]{:S(2)}, u32[]{:S(2)}) %all-to-all-start.2) | async-done | bytes 7340064 | tf_op jit(solution)/shard_map/all_to_all | solution.py:480
  158.8 23.8 %all-to-all-start.1 = ((bf16[32,3,64,128]{3,2,1,0:T(8,128)(2,1)}), bf16[32,3,64,128]{3,2,1,0:T(8,128)(2,1)S(1)}, u32[]{:S(2)}, u32[]{:S(2)}) async-start(bf16[32,3,64,128]{3,2,1,0:T(8,128)(2,1)} %total.1), calls=%async_computation.1 | async-start | bytes 3145728 | tf_op jit(solution)/shard_map/all_to_all | solution.py:480
  183.3 5.2 %prepare.1 = (f32[256,1024]{1,0:T(8,128)}, f32[256,1024]{1,0:T(8,128)}, bf16[2,1024,256]{2,1,0:T(8,128)(2,1)}, f32[16,16]{1,0:T(8,128)}) custom-call(s32[1]{0:T(128)} %bitcast.me.refs_0_, s32[512]{0:T(512)} %tail.3, bf16[256,1024]{1,0:T(8,128)(2,1)} %x_ref.1, bf16[256,1024]{1,0:T(8,128)(2,1)} %z_ref.1, bf16[256,128]{1,0:T(8,128)(2,1)} %refs_7_.1, ...), custom_call_target="tpu_custom_call" | custom-call | flops 8000000000 | bytes 5000000 | tf_op jit(solution)/shard_map/prepare/pallas_call | solution.py:340
  188.5 9.7 %shard_map.193 = (bf16[16,16,64,128]{3,2,1,0:T(8,128)(2,1)}, f32[256,896]{1,0:T(8,128)}) custom-call(s32[1]{0:T(128)} %bitcast.me.refs_0_, s32[512]{0:T(512)} %refs_1_.3, f32[16,16]{1,0:T(8,128)} %get-tuple-element.21.refs_2_, bf16[32,14,64,128]{3,2,1,0:T(8,128)(2,1)} %all-to-all-done.2.refs_3_.refs_4_, ...), custom_call_target="tpu_custom_call" | custom-call | flops 4000000000 | bytes 8000000 | tf_op jit(solution)/shard_map/pallas_call | solution.py:462
  198.2 7.1 %all-to-all-done.1.refs_3_.refs_4_.refs_5_.refs_6_ = bf16[32,3,64,128]{3,2,1,0:T(8,128)(2,1)S(1)} async-done(((bf16[32,3,64,128]{3,2,1,0:T(8,128)(2,1)}), bf16[32,3,64,128]{3,2,1,0:T(8,128)(2,1)S(1)}, u32[]{:S(2)}, u32[]{:S(2)}) %all-to-all-start.1) | async-done | bytes 1572896 | tf_op jit(solution)/shard_map/all_to_all | solution.py:480
  206.4 5.1 %shard_map.194 = (bf16[16,16,64,128]{3,2,1,0:T(8,128)(2,1)}, bf16[256,1024]{1,0:T(8,128)(2,1)}, bf16[256,512]{1,0:T(8,128)(2,1)}) custom-call(s32[1]{0:T(128)} %bitcast.me.refs_0_, s32[512]{0:T(512)} %refs_1_.3, f32[16,16]{1,0:T(8,128)} %get-tuple-element.21.refs_2_, bf16[32,3,64,128]{3,2,1,0:T(8,128)(2,1)} %copy-done.1, ...), custom_call_target="tpu_custom_call", output_to_operand_aliasing={{0}: (12, {})} | custom-call | flops 4000000000 | bytes 8000000 | tf_op jit(solution)/shard_map/pallas_call | solution.py:462
  (80 shorter events, 18.6 us)
Async XLA Ops:
  2.7 8.0 %collective-permute-start.7 = (bf16[512,128]{1,0:T(8,128)(2,1)S(1)}, bf16[512,128]{1,0:T(8,128)(2,1)S(1)}, u32[]{:S(2)}, u32[]{:S(2)}) collective-permute-start(bf16[512,128]{1,0:T(8,128)(2,1)S(1)} %get-tuple-element.47), channel_id=1, source_target_pairs={{0,16},{8,24},{16,32},{24,40},{32,48},{40,56},{48,0},{56,8},{64,80... | collective-permute-start | bytes 393224 | tf_op jit(solution)/shard_map/ppermute | solution.py:495
  4.9 7.3 %collective-permute-start.8 = (bf16[512,128]{1,0:T(8,128)(2,1)S(1)}, bf16[512,128]{1,0:T(8,128)(2,1)S(1)}, u32[]{:S(2)}, u32[]{:S(2)}) collective-permute-start(bf16[512,128]{1,0:T(8,128)(2,1)S(1)} %get-tuple-element.47), channel_id=1, source_target_pairs={{0,48},{8,56},{16,0},{24,8},{32,16},{40,24},{48,32},{56,40},{64,11... | collective-permute-start | bytes 393224 | tf_op jit(solution)/shard_map/ppermute | solution.py:495
  6.4 6.4 %collective-permute-start.9 = (bf16[512,128]{1,0:T(8,128)(2,1)S(1)}, bf16[512,128]{1,0:T(8,128)(2,1)S(1)}, u32[]{:S(2)}, u32[]{:S(2)}) collective-permute-start(bf16[512,128]{1,0:T(8,128)(2,1)S(1)} %get-tuple-element.47), channel_id=1, source_target_pairs={{0,32},{8,40},{16,48},{24,56},{32,0},{40,8},{48,16},{56,24},{64,96... | collective-permute-start | bytes 393224 | tf_op jit(solution)/shard_map/ppermute | solution.py:495
  8.0 8.8 %collective-permute-start = (bf16[512,128]{1,0:T(8,128)(2,1)S(1)}, bf16[512,128]{1,0:T(8,128)(2,1)S(1)}, u32[]{:S(2)}, u32[]{:S(2)}) collective-permute-start(bf16[512,128]{1,0:T(8,128)(2,1)S(1)} %get-tuple-element.48), channel_id=1, source_target_pairs={{0,64},{8,72},{16,80},{24,88},{32,96},{40,104},{48,112},{56,120},{... | collective-permute-start | bytes 393224 | tf_op jit(solution)/shard_map/ppermute | solution.py:495
  9.2 7.6 %collective-permute-start.1 = (bf16[512,128]{1,0:T(8,128)(2,1)S(1)}, bf16[512,128]{1,0:T(8,128)(2,1)S(1)}, u32[]{:S(2)}, u32[]{:S(2)}) collective-permute-start(bf16[512,128]{1,0:T(8,128)(2,1)S(1)} %get-tuple-element.48), channel_id=1, source_target_pairs={{0,192},{8,200},{16,208},{24,216},{32,224},{40,232},{48,240},{56,2... | collective-permute-start | bytes 393224 | tf_op jit(solution)/shard_map/ppermute | solution.py:495
  10.7 6.7 %collective-permute-start.2 = (bf16[512,128]{1,0:T(8,128)(2,1)S(1)}, bf16[512,128]{1,0:T(8,128)(2,1)S(1)}, u32[]{:S(2)}, u32[]{:S(2)}) collective-permute-start(bf16[512,128]{1,0:T(8,128)(2,1)S(1)} %get-tuple-element.48), channel_id=1, source_target_pairs={{0,128},{8,136},{16,144},{24,152},{32,160},{40,168},{48,176},{56,1... | collective-permute-start | bytes 393224 | tf_op jit(solution)/shard_map/ppermute | solution.py:495
  13.7 14.9 %collective-permute-start.11 = (bf16[4,512,128]{2,1,0:T(8,128)(2,1)}, bf16[4,512,128]{2,1,0:T(8,128)(2,1)S(1)}, u32[]{:S(2)}, u32[]{:S(2)}) collective-permute-start(bf16[4,512,128]{2,1,0:T(8,128)(2,1)} %get-tuple-element.42), channel_id=1, source_target_pairs={{0,192},{8,200},{16,208},{24,216},{32,224},{40,232},{48,240},{56,2... | collective-permute-start | bytes 1572872 | tf_op jit(solution)/shard_map/ppermute | solution.py:495
  16.8 14.5 %collective-permute-start.10 = (bf16[4,512,128]{2,1,0:T(8,128)(2,1)}, bf16[4,512,128]{2,1,0:T(8,128)(2,1)S(1)}, u32[]{:S(2)}, u32[]{:S(2)}) collective-permute-start(bf16[4,512,128]{2,1,0:T(8,128)(2,1)} %get-tuple-element.42), channel_id=1, source_target_pairs={{0,64},{8,72},{16,80},{24,88},{32,96},{40,104},{48,112},{56,120},{... | collective-permute-start | bytes 1572872 | tf_op jit(solution)/shard_map/ppermute | solution.py:495
  18.3 13.8 %collective-permute-start.4 = (bf16[4,512,128]{2,1,0:T(8,128)(2,1)}, bf16[4,512,128]{2,1,0:T(8,128)(2,1)S(1)}, u32[]{:S(2)}, u32[]{:S(2)}) collective-permute-start(bf16[4,512,128]{2,1,0:T(8,128)(2,1)} %get-tuple-element.44), channel_id=1, source_target_pairs={{0,48},{8,56},{16,0},{24,8},{32,16},{40,24},{48,32},{56,40},{64,11... | collective-permute-start | bytes 1572872 | tf_op jit(solution)/shard_map/ppermute | solution.py:495
  19.4 15.9 %collective-permute-start.3 = (bf16[4,512,128]{2,1,0:T(8,128)(2,1)}, bf16[4,512,128]{2,1,0:T(8,128)(2,1)S(1)}, u32[]{:S(2)}, u32[]{:S(2)}) collective-permute-start(bf16[4,512,128]{2,1,0:T(8,128)(2,1)} %get-tuple-element.44), channel_id=1, source_target_pairs={{0,16},{8,24},{16,32},{24,40},{32,48},{40,56},{48,0},{56,8},{64,80... | collective-permute-start | bytes 1572872 | tf_op jit(solution)/shard_map/ppermute | solution.py:495
  19.7 36.9 %all-to-all-start = ((bf16[32,16,1280]{2,1,0:T(8,128)(2,1)}), bf16[32,16,1280]{2,1,0:T(8,128)(2,1)}, u32[]{:S(2)}, u32[]{:S(2)}) async-start(bf16[32,16,1280]{2,1,0:T(8,128)(2,1)} %pack_q.1), calls=%async_computation | async-start | bytes 2621440 | tf_op jit(solution)/shard_map/all_to_all | solution.py:480
  28.6 12.1 %copy-start.2 = (bf16[4,512,128]{2,1,0:T(8,128)(2,1)}, bf16[4,512,128]{2,1,0:T(8,128)(2,1)S(1)}, u32[]{:S(2)}) copy-start(bf16[4,512,128]{2,1,0:T(8,128)(2,1)S(1)} %collective-permute-done.11) | copy-start | bytes 1572868
  28.6 21.8 %collective-permute-start.12 = (bf16[2,512,128]{2,1,0:T(8,128)(2,1)S(1)}, bf16[2,512,128]{2,1,0:T(8,128)(2,1)}, u32[]{:S(2)}, u32[]{:S(2)}) collective-permute-start(bf16[2,512,128]{2,1,0:T(8,128)(2,1)S(1)} %slice.34), channel_id=1, source_target_pairs={{0,192},{8,200},{16,208},{24,216},{32,224},{40,232},{48,240},{56,2... | collective-permute-start | bytes 786440 | tf_op jit(solution)/shard_map/ppermute | solution.py:495
  31.3 9.3 %copy-start.4 = (bf16[4,512,128]{2,1,0:T(8,128)(2,1)}, bf16[4,512,128]{2,1,0:T(8,128)(2,1)S(1)}, u32[]{:S(2)}) copy-start(bf16[4,512,128]{2,1,0:T(8,128)(2,1)S(1)} %collective-permute-done.10) | copy-start | bytes 1572868
  32.1 19.6 %collective-permute-start.13 = (bf16[2,512,128]{2,1,0:T(8,128)(2,1)}, bf16[2,512,128]{2,1,0:T(8,128)(2,1)}, u32[]{:S(2)}, u32[]{:S(2)}) collective-permute-start(bf16[2,512,128]{2,1,0:T(8,128)(2,1)} %slice.35), channel_id=1, source_target_pairs={{0,64},{8,72},{16,80},{24,88},{32,96},{40,104},{48,112},{56,120},{... | collective-permute-start | bytes 786440 | tf_op jit(solution)/shard_map/ppermute | solution.py:495
  32.1 8.6 %copy-start.6 = (bf16[4,512,128]{2,1,0:T(8,128)(2,1)}, bf16[4,512,128]{2,1,0:T(8,128)(2,1)S(1)}, u32[]{:S(2)}) copy-start(bf16[4,512,128]{2,1,0:T(8,128)(2,1)S(1)} %collective-permute-done.4) | copy-start | bytes 1572868
  32.9 19.9 %collective-permute-start.5 = (bf16[2,512,128]{2,1,0:T(8,128)(2,1)}, bf16[2,512,128]{2,1,0:T(8,128)(2,1)}, u32[]{:S(2)}, u32[]{:S(2)}) collective-permute-start(bf16[2,512,128]{2,1,0:T(8,128)(2,1)} %slice.32), channel_id=1, source_target_pairs={{0,48},{8,56},{16,0},{24,8},{32,16},{40,24},{48,32},{56,40},{64,11... | collective-permute-start | bytes 786440 | tf_op jit(solution)/shard_map/ppermute | solution.py:495
  36.1 16.7 %collective-permute-start.6 = (bf16[2,512,128]{2,1,0:T(8,128)(2,1)}, bf16[2,512,128]{2,1,0:T(8,128)(2,1)}, u32[]{:S(2)}, u32[]{:S(2)}) collective-permute-start(bf16[2,512,128]{2,1,0:T(8,128)(2,1)} %slice.33), channel_id=1, source_target_pairs={{0,16},{8,24},{16,32},{24,40},{32,48},{40,56},{48,0},{56,8},{64,80... | collective-permute-start | bytes 786440 | tf_op jit(solution)/shard_map/ppermute | solution.py:495
  54.2 13.7 %copy-start = (bf16[4,4,512,128]{3,2,1,0:T(8,128)(2,1)}, bf16[4,4,512,128]{3,2,1,0:T(8,128)(2,1)S(1)}, u32[]{:S(2)}) copy-start(bf16[4,4,512,128]{3,2,1,0:T(8,128)(2,1)S(1)} %pad_maximum_fusion.1.b_near) | copy-start | bytes 6291460
  56.7 11.8 %copy-start.15 = (s32[512,16]{0,1:T(8,128)S(1)}, s32[512,16]{0,1:T(8,128)}, u32[]{:S(2)}) copy-start(s32[512,16]{0,1:T(8,128)} %param.33) | copy-start | bytes 98308
  56.7 102.1 %all-to-all-start.2 = ((bf16[32,14,64,128]{3,2,1,0:T(8,128)(2,1)}), bf16[32,14,64,128]{3,2,1,0:T(8,128)(2,1)}, u32[]{:S(2)}, u32[]{:S(2)}) async-start(bf16[32,14,64,128]{3,2,1,0:T(8,128)(2,1)} %get-tuple-element.33), calls=%async_computation.2 | async-start | bytes 14680064 | tf_op jit(solution)/shard_map/all_to_all | solution.py:480
  67.9 11.0 %collective-permute-start.15 = (bf16[4,4,512,128]{3,2,1,0:T(8,128)(2,1)S(1)}, bf16[4,4,512,128]{3,2,1,0:T(8,128)(2,1)}, u32[]{:S(2)}, u32[]{:S(2)}) collective-permute-start(bf16[4,4,512,128]{3,2,1,0:T(8,128)(2,1)S(1)} %pad_maximum_fusion.1.b_near), channel_id=1, source_target_pairs={{0,8},{8,0},{16,24},{24,16},{32,40},{40,32},{48,56},{56,48},{64,72... | collective-permute-start | bytes 6291464 | tf_op jit(solution)/shard_map/ppermute | solution.py:550
  68.3 10.6 %collective-permute-start.14 = (bf16[4,4,512,128]{3,2,1,0:T(8,128)(2,1)}, bf16[4,4,512,128]{3,2,1,0:T(8,128)(2,1)}, u32[]{:S(2)}, u32[]{:S(2)}) collective-permute-start(bf16[4,4,512,128]{3,2,1,0:T(8,128)(2,1)} %pad_maximum_fusion.a_near), channel_id=1, source_target_pairs={{0,8},{8,0},{16,24},{24,16},{32,40},{40,32},{48,56},{56,48},{64,72... | collective-permute-start | bytes 6291464 | tf_op jit(solution)/shard_map/ppermute | solution.py:549
  87.0 15.0 %collective-permute-start.16 = (bf16[6,256,128]{2,1,0:T(8,128)(2,1)S(1)}, bf16[6,256,128]{2,1,0:T(8,128)(2,1)S(1)}, u32[]{:S(2)}, u32[]{:S(2)}) collective-permute-start(bf16[6,256,128]{2,1,0:T(8,128)(2,1)S(1)} %get-tuple-element.40), channel_id=1, source_target_pairs={{0,1},{1,2},{2,3},{3,4},{4,5},{5,6},{6,7},{7,0},{8,9},{9,10},{10,1... | collective-permute-start | bytes 1179656 | tf_op jit(solution)/shard_map/ppermute | solution.py:513
  88.7 13.2 %collective-permute-start.17 = (bf16[6,256,128]{2,1,0:T(8,128)(2,1)S(1)}, bf16[6,256,128]{2,1,0:T(8,128)(2,1)S(1)}, u32[]{:S(2)}, u32[]{:S(2)}) collective-permute-start(bf16[6,256,128]{2,1,0:T(8,128)(2,1)S(1)} %get-tuple-element.39), channel_id=1, source_target_pairs={{0,7},{1,0},{2,1},{3,2},{4,3},{5,4},{6,5},{7,6},{8,15},{9,8},{10,9... | collective-permute-start | bytes 1179656 | tf_op jit(solution)/shard_map/ppermute | solution.py:513
  106.2 8.8 %collective-permute-start.18 = (bf16[4,256,128]{2,1,0:T(8,128)(2,1)}, bf16[4,256,128]{2,1,0:T(8,128)(2,1)S(1)}, u32[]{:S(2)}, u32[]{:S(2)}) collective-permute-start(bf16[4,256,128]{2,1,0:T(8,128)(2,1)} %get-tuple-element.24), channel_id=1, source_target_pairs={{0,1},{1,2},{2,3},{3,4},{4,5},{5,6},{6,7},{7,0},{8,9},{9,10},{10,1... | collective-permute-start | bytes 786440 | tf_op jit(solution)/shard_map/ppermute | solution.py:513
  106.2 24.8 %collective-permute-start.19 = (bf16[4,256,128]{2,1,0:T(8,128)(2,1)}, bf16[4,256,128]{2,1,0:T(8,128)(2,1)S(1)}, u32[]{:S(2)}, u32[]{:S(2)}) collective-permute-start(bf16[4,256,128]{2,1,0:T(8,128)(2,1)} %get-tuple-element.25), channel_id=1, source_target_pairs={{0,3},{1,4},{2,5},{3,6},{4,7},{5,0},{6,1},{7,2},{8,11},{9,12},{10,... | collective-permute-start | bytes 786440 | tf_op jit(solution)/shard_map/ppermute | solution.py:513
  110.2 20.8 %collective-permute-start.20 = (bf16[4,256,128]{2,1,0:T(8,128)(2,1)}, bf16[4,256,128]{2,1,0:T(8,128)(2,1)S(1)}, u32[]{:S(2)}, u32[]{:S(2)}) collective-permute-start(bf16[4,256,128]{2,1,0:T(8,128)(2,1)} %get-tuple-element.26), channel_id=1, source_target_pairs={{0,7},{1,0},{2,1},{3,2},{4,3},{5,4},{6,5},{7,6},{8,15},{9,8},{10,9... | collective-permute-start | bytes 786440 | tf_op jit(solution)/shard_map/ppermute | solution.py:513
  111.8 19.1 %collective-permute-start.21 = (bf16[4,256,128]{2,1,0:T(8,128)(2,1)}, bf16[4,256,128]{2,1,0:T(8,128)(2,1)S(1)}, u32[]{:S(2)}, u32[]{:S(2)}) collective-permute-start(bf16[4,256,128]{2,1,0:T(8,128)(2,1)} %get-tuple-element.27), channel_id=1, source_target_pairs={{0,5},{1,6},{2,7},{3,0},{4,1},{5,2},{6,3},{7,4},{8,13},{9,14},{10,... | collective-permute-start | bytes 786440 | tf_op jit(solution)/shard_map/ppermute | solution.py:513
  114.9 16.0 %copy-start.11 = (bf16[4,256,128]{2,1,0:T(8,128)(2,1)}, bf16[4,256,128]{2,1,0:T(8,128)(2,1)S(1)}, u32[]{:S(2)}) copy-start(bf16[4,256,128]{2,1,0:T(8,128)(2,1)S(1)} %collective-permute-done.18.rest_0_) | copy-start | bytes 786436
  134.5 48.0 %copy-start.16 = (bf16[256,16]{0,1:T(8,128)(2,1)S(1)}, bf16[256,16]{0,1:T(8,128)(2,1)}, u32[]{:S(2)}) copy-start(bf16[256,16]{0,1:T(8,128)(2,1)} %param.22) | copy-start | bytes 24580
  158.8 46.5 %all-to-all-start.1 = ((bf16[32,3,64,128]{3,2,1,0:T(8,128)(2,1)}), bf16[32,3,64,128]{3,2,1,0:T(8,128)(2,1)S(1)}, u32[]{:S(2)}, u32[]{:S(2)}) async-start(bf16[32,3,64,128]{3,2,1,0:T(8,128)(2,1)} %total.1), calls=%async_computation.1 | async-start | bytes 3145728 | tf_op jit(solution)/shard_map/all_to_all | solution.py:480
  (12 other events, 21.5 us)
where the time goes:
time: 213 us; the launch traced here: 212 us
  starting transfers between devices  75.4 us (35%)
  waiting for transfers between devices  71.5 us (34%)
  Pallas kernels  48.3 us (23%)
  local copies, waits for them, and re-layouts  9.62 us (5%)
  other arithmetic  5.76 us (3%)
    all_to_all x3, starting transfers between devices, exchange(): return lax.all_to_all(x, axis, split_axis=0, concat_axis=0, tiled=True)  43.8 us
    all_to_all x3, waiting for transfers between devices, exchange(): return lax.all_to_all(x, axis, split_axis=0, concat_axis=0, tiled=True)  31.3 us
    ppermute x6, waiting for transfers between devices, turn(): lax.ppermute(v, 'head', [(z, (z + by) % NHEAD) for z in range(NHEAD)])  28.1 us
    ppermute x14, starting transfers between devices, hop(): return lax.ppermute(v, 'rep', pairs)  19.2 us
    pallas_call x2, Pallas kernels, scan(): pl.pallas_call(body, grid_spec=pltpu.PrefetchScalarGridSpec(num_scalar_pr...  14.8 us
    ppermute x14, waiting for transfers between devices, hop(): return lax.ppermute(v, 'rep', pairs)  12.2 us
    ppermute x6, starting transfers between devices, turn(): lax.ppermute(v, 'head', [(z, (z + by) % NHEAD) for z in range(NHEAD)])  11.7 us
    pallas_call x1, Pallas kernels, attend(): pl.pallas_call(attend_body, out_shape=sds((TOK, QH * DH), bf16), in_specs...  9.51 us
  transfers between devices with their start and end apart: 25, of which 9 were waited for; matrix products, arithmetic and copies ran while one was open for 5% of the time, Pallas kernels for 19%

commit v1 on v0

--- a/solution.py
+++ b/solution.py
@@ -20,14 +20,17 @@
 CACHE = 256
 TOK = REQ * TAIL
 WIDTH = HEADS * HD
-QW = QH * DH + 2 * DH
 NHEAD = 8
 NEAR = (0, -1, 1, 2)
 SIZES = (14, 2)
 STARTS = (0, 14)
 STEPS = (2, 4)
 CHUNKS = len(SIZES)
-ROOM = 4 * TAIL * DH // (HD * STATE)
+EARLY = 2 * HD
+MOST = 12 * HD
+LAST = 2 * HD
+SLAB = 4 * TAIL
+ASK = (QH + 2) * TAIL
 
 f32 = jnp.float32
 bf16 = jnp.bfloat16
@@ -61,35 +64,7 @@
     return pltpu.CompilerParams(**kw)
 
 
-def pack_q_body(me, owner, q, kv, out, sem):
-    base = me[0] * REQ
-    for j in range(REQ):
-        o = owner[base + j]
-        rows = pl.ds(j * TAIL, TAIL)
-        pltpu.make_async_copy(q.at[rows], out.at[o, :, pl.ds(0, QH * DH)], sem.at[0]).start()
-        pltpu.make_async_copy(kv.at[rows], out.at[o, :, pl.ds(QH * DH, 2 * DH)], sem.at[1]).start()
-    pltpu.make_async_copy(q, q, sem.at[0]).wait()
-    pltpu.make_async_copy(kv, kv, sem.at[1]).wait()
-
-
-def pack_q(me, owner, q, kv):
-    return pl.pallas_call(
-        pack_q_body,
-        out_shape=sds((REPS, TAIL, QW), bf16),
-        in_specs=[SMEM, SMEM, VMEM, VMEM],
-        out_specs=ANY,
-        scratch_shapes=[pltpu.SemaphoreType.DMA((2,))],
-        name="pack_q",
-    )(me, owner, q, kv)
-
-
-def pack_s_body(me, owner, slot, ckpt, *rest):
-    outs = rest[:CHUNKS]
-    req, buf, come, go = rest[CHUNKS:]
-    mine = me[0]
-    for s in range(REQ):
-        pltpu.make_async_copy(ckpt.at[s], buf.at[s], come.at[s]).start()
-
+def serve(owner, slot, mine, req, base):
     def home(h, carry):
         s = jnp.int32(0)
         g = jnp.int32(0)
@@ -100,39 +75,85 @@
 
         @pl.when(s > 0)
         def _():
-            req[s - 1] = g
+            req[base + s - 1] = g
 
         return carry
 
     lax.fori_loop(0, REPS, home, 0)
+
+
+def pack_first_body(me, owner, slot, q, kv, ckpt, out, req, buf, tmp, come, go):
+    for s in range(REQ):
+        pltpu.make_async_copy(ckpt.at[s, pl.ds(MOST, EARLY)], buf.at[s], come.at[s]).start()
+    first = me[0] * REQ
+    for j in range(REQ):
+        rows = slice(j * TAIL, (j + 1) * TAIL)
+        for a in range(QH):
+            tmp[j, a * TAIL : (a + 1) * TAIL, :] = q[rows, a * DH : (a + 1) * DH]
+        for a in range(2):
+            tmp[j, (QH + a) * TAIL : (QH + a + 1) * TAIL, :] = kv[rows, a * DH : (a + 1) * DH]
+        pltpu.make_async_copy(
+            tmp.at[j], out.at[owner[first + j], pl.ds(EARLY, ASK)], go.at[0]
+        ).start()
+    serve(owner, slot, me[0], req, 0)
+    for s in range(REQ):
+        pltpu.make_async_copy(ckpt.at[s, pl.ds(MOST, EARLY)], buf.at[s], come.at[s]).wait()
+        pltpu.make_async_copy(buf.at[s], out.at[req[s] // REQ, pl.ds(0, EARLY)], go.at[1]).start()
+    pltpu.make_async_copy(tmp, tmp, go.at[0]).wait()
+    pltpu.make_async_copy(buf, buf, go.at[1]).wait()
+
+
+def pack_first(me, owner, slot, q, kv, ckpt):
+    return pl.pallas_call(
+        pack_first_body,
+        out_shape=[sds((REPS, EARLY + ASK, STATE), bf16), sds((REQ,), jnp.int32)],
+        in_specs=[SMEM, SMEM, SMEM, VMEM, VMEM, ANY],
+        out_specs=[ANY, SMEM],
+        scratch_shapes=[
+            pltpu.VMEM((REQ, EARLY, STATE), bf16),
+            pltpu.VMEM((REQ, ASK, DH), bf16),
+            pltpu.SemaphoreType.DMA((REQ,)),
+            pltpu.SemaphoreType.DMA((2,)),
+        ],
+        name="pack_first",
+    )(me, owner, slot, q, kv, ckpt)
+
+
+def pack_s_body(me, owner, slot, req, ckpt, most, last, both, buf, come, go):
+    for s in range(REQ):
+        pltpu.make_async_copy(ckpt.at[s], buf.at[s], come.at[s]).start()
     for s in range(REQ):
         pltpu.make_async_copy(ckpt.at[s], buf.at[s], come.at[s]).wait()
-        for c in range(CHUNKS):
-            pltpu.make_async_copy(
-                buf.at[s, pl.ds(STARTS[c], SIZES[c])],
-                outs[c].at[req[s] // REQ, pl.ds(0, SIZES[c])],
-                go.at[c],
-            ).start()
-    for c in range(CHUNKS):
-        part = buf.at[:, pl.ds(STARTS[c], SIZES[c])]
-        pltpu.make_async_copy(part, part, go.at[c]).wait()
-
-
-def pack_s(me, owner, slot, ckpt):
-    depth = [n + (ROOM if c == CHUNKS - 1 else 0) for c, n in enumerate(SIZES)]
-    out = pl.pallas_call(
+        home = req[s] // REQ
+        pltpu.make_async_copy(buf.at[s, pl.ds(0, MOST)], most.at[home], go.at[0]).start()
+        pltpu.make_async_copy(
+            buf.at[s, pl.ds(MOST + EARLY, LAST)], last.at[home, pl.ds(0, LAST)], go.at[1]
+        ).start()
+    par = me[0] & 1
+    for s in range(REQ):
+        both[par * REQ + s] = req[s]
+    serve(owner, slot, me[0] + 1 - 2 * par, both, (1 - par) * REQ)
+    for k, part in enumerate((buf.at[:, pl.ds(0, MOST)], buf.at[:, pl.ds(MOST + EARLY, LAST)])):
+        pltpu.make_async_copy(part, part, go.at[k]).wait()
+
+
+def pack_s(me, owner, slot, req, ckpt):
+    return pl.pallas_call(
         pack_s_body,
-        out_shape=[sds((REPS, n, HD, STATE), bf16) for n in depth] + [sds((REQ,), jnp.int32)],
-        in_specs=[SMEM, SMEM, SMEM, ANY],
-        out_specs=[ANY] * CHUNKS + [SMEM],
+        out_shape=[
+            sds((REPS, MOST, STATE), bf16),
+            sds((REPS, LAST + SLAB, STATE), bf16),
+            sds((2 * REQ,), jnp.int32),
+        ],
+        in_specs=[SMEM, SMEM, SMEM, SMEM, ANY],
+        out_specs=[ANY, ANY, SMEM],
         scratch_shapes=[
-            pltpu.VMEM((REQ, HEADS, HD, STATE), bf16),
+            pltpu.VMEM((REQ, WIDTH, STATE), bf16),
             pltpu.SemaphoreType.DMA((REQ,)),
-            pltpu.SemaphoreType.DMA((CHUNKS,)),
+            pltpu.SemaphoreType.DMA((2,)),
         ],
         name="pack_s",
-    )(me, owner, slot, ckpt)
-    return out[:CHUNKS], out[CHUNKS]
+    )(me, owner, slot, req, ckpt)
 
 
 def attend_body(req, pages, hit, tail, qin, pool, out):
@@ -146,13 +167,13 @@
 
     def one(s, carry):
         g = req[s]
-        q = qin[g // REQ]
-        rows = jnp.concatenate([q[:, a * DH : (a + 1) * DH] for a in range(QH)], axis=0)
+        ask = qin[g // REQ]
+        rows = ask[EARLY : EARLY + QH * TAIL]
         held = [pool[pages[g * PAGES + i]] for i in range(PAGES)]
         keys = jnp.concatenate(
-            [p[:, :DH] for p in held] + [q[:, QH * DH : QH * DH + DH], pad], axis=0
+            [p[:, :DH] for p in held] + [ask[EARLY + ASK - 2 * TAIL : EARLY + ASK - TAIL], pad], axis=0
         )
-        vals = jnp.concatenate([p[:, DH:] for p in held] + [q[:, QH * DH + DH :], pad], axis=0)
+        vals = jnp.concatenate([p[:, DH:] for p in held] + [ask[EARLY + ASK - TAIL :], pad], axis=0)
         scores = lax.dot_general(rows, keys, NT, preferred_element_type=f32) * scale
         visible = (col < hit[g]) | (causal & (late < tail[g]))
         scores = jnp.where(visible, scores, -1e30)
@@ -191,44 +212,41 @@
     return base + i
 
 
-def project_body(me, head, attn, a_near, b_near, a_far, b_far, out):
+def project_body(me, head, mine, other, *rest):
+    a_ring, b_ring, out = rest[:5], rest[5:10], rest[10]
     x = me[0] // 8
     y = (me[0] // 2) & 3
     par = me[0] & 1
-    step = pl.program_id(0)
-    off = jnp.where(step == 3, 2, jnp.where(step == 1, -1, jnp.where(step == 2, 1, 0)))
-    cy = (y + off) & 3
     half = QH * DH // 2
-    for far, (wa, wb) in enumerate(((a_near, b_near), (a_far, b_far))):
-        core = 1 - par if far else par
-        for d in (0, 2):
-            res = dot(attn[:, :half], jnp.concatenate([wa[0, d], wa[0, d + 1]], axis=1)) + dot(
-                attn[:, half:], jnp.concatenate([wb[d, 0], wb[d + 1, 0]], axis=1)
-            )
-            res = res.astype(bf16)
-            for k in range(2):
-                col = ((x + NEAR[d + k]) & 3) * 8 + cy * 2 + core
-                out[spot(((col // 4) - head[0]) & (NHEAD - 1), col & 3)] = res[
-                    :, k * DH : (k + 1) * DH
-                ]
-
-
-def project(me, head, attn, a_near, b_near, a_far, b_far):
-    half = QH * DH // 2
-    wa = pl.BlockSpec((1, 4, half, DH), lambda i: (i, 0, 0, 0))
-    wb = pl.BlockSpec((4, 1, half, DH), lambda i: (0, i, 0, 0))
+
+    def block(ring, outer, inner):
+        if outer < 3:
+            return ring[outer][inner]
+        return ring[3 + inner // 2][inner % 2]
+
+    for dy in range(4):
+        for dx in (0, 2):
+            top = jnp.concatenate([block(a_ring, dy, dx), block(a_ring, dy, dx + 1)], axis=1)
+            low = jnp.concatenate([block(b_ring, dx, dy), block(b_ring, dx + 1, dy)], axis=1)
+            for attn, core in ((mine, par), (other, 1 - par)):
+                res = (dot(attn[:, :half], top) + dot(attn[:, half:], low)).astype(bf16)
+                for k in range(2):
+                    pair = ((x + NEAR[dx + k]) & 3) * 4 + ((y + NEAR[dy]) & 3)
+                    dist = ((pair // 2) - head[0]) & (NHEAD - 1)
+                    out[spot(dist, 2 * (pair & 1) + core)] = res[:, k * DH : (k + 1) * DH]
+
+
+def project(me, head, mine, other, a_ring, b_ring):
     return pl.pallas_call(
         project_body,
-        grid=(4,),
         out_shape=sds((4 * NHEAD, TOK, DH), bf16),
-        in_specs=[SMEM, SMEM, pl.BlockSpec((TOK, QH * DH), lambda i: (0, 0)), wa, wb, wa, wb],
-        out_specs=pl.BlockSpec((4 * NHEAD, TOK, DH), lambda i: (0, 0, 0)),
-        compiler_params=params(dimension_semantics=("arbitrary",)),
+        in_specs=[SMEM, SMEM] + [VMEM] * 12,
+        out_specs=VMEM,
         cost_estimate=pl.CostEstimate(
             flops=8_000_000_000, transcendentals=0, bytes_accessed=11_000_000
         ),
         name="project",
-    )(me, head, attn, a_near, b_near, a_far, b_far)
+    )(me, head, mine, other, *a_ring, *b_ring)
 
 
 def relay_body(terms, up, down, one, three, seven, five):
@@ -256,34 +274,38 @@
     )(terms, up, down)
 
 
-def total_body(req, terms, *rest):
+def total_body(both, terms, *rest):
     parts = rest[:4]
     out, tmp, sem = rest[5:]
-    for i in range(4):
-        acc = terms[12 + i].astype(f32)
+    for u in range(4):
+        acc = terms[12 + u].astype(f32)
         for p in parts:
-            acc = acc + p[i].astype(f32)
+            acc = acc + p[u].astype(f32)
         acc = acc.astype(bf16)
+        i, core = u // 2, u % 2
         for s in range(REQ):
-            tmp[s, i * TAIL : (i + 1) * TAIL, :] = acc[s * TAIL : (s + 1) * TAIL]
-    for s in range(REQ):
-        pltpu.make_async_copy(tmp.at[s], out.at[req[s] // REQ, SIZES[-1]], sem.at[0]).start()
+            tmp[core * REQ + s, i * TAIL : (i + 1) * TAIL, :] = acc[s * TAIL : (s + 1) * TAIL]
+    for s in range(2 * REQ):
+        at = LAST + (s // REQ) * 2 * TAIL
+        pltpu.make_async_copy(
+            tmp.at[s], out.at[both[s] // REQ, pl.ds(at, 2 * TAIL)], sem.at[0]
+        ).start()
     pltpu.make_async_copy(tmp, tmp, sem.at[0]).wait()
 
 
-def total(req, terms, parts, packed):
+def total(both, terms, parts, packed):
     return pl.pallas_call(
         total_body,
         out_shape=sds(packed.shape, bf16),
         in_specs=[SMEM] + [VMEM] * 5 + [ANY],
         out_specs=ANY,
         input_output_aliases={6: 0},
-        scratch_shapes=[pltpu.VMEM((REQ, 4 * TAIL, DH), bf16), pltpu.SemaphoreType.DMA((1,))],
+        scratch_shapes=[pltpu.VMEM((2 * REQ, 2 * TAIL, DH), bf16), pltpu.SemaphoreType.DMA((1,))],
         cost_estimate=pl.CostEstimate(
             flops=1_000_000_000, transcendentals=0, bytes_accessed=3_000_000
         ),
         name="total",
-    )(req, terms, *parts, packed)
+    )(both, terms, *parts, packed)
 
 
 def prepare_body(
@@ -359,12 +381,13 @@
     refs = list(refs)
     heads = SIZES[chunk]
     count = STEPS[chunk]
-    width = heads * HD
     final_chunk = chunk == CHUNKS - 1
-    dl = refs[2]
-    held = refs[3 : 3 + count]
-    b_ref, c_ref, xt, base, ecx = refs[3 + count : 8 + count]
-    refs = refs[8 + count :]
+    me, owner, dl = refs[:3]
+    per = 3 if final_chunk else 2
+    held = [refs[3 + per * k : 3 + per * (k + 1)] for k in range(count)]
+    refs = refs[3 + per * count :]
+    b_ref, c_ref, xt, base, ecx = refs[:5]
+    refs = refs[5:]
     prev = []
     if chunk > 0:
         prev = refs[1 : 1 + chunk]
@@ -374,7 +397,10 @@
     else:
         fin, gated_ref = refs
     i = pl.program_id(0)
-    states = [s[0, :heads].reshape(width, STATE) for s in held]
+    if final_chunk:
+        states = [h[0][0] for h in held]
+    else:
+        states = [jnp.concatenate([h[0][0], h[1][0]], axis=0) for h in held]
     seen = jnp.concatenate(
         [
             lax.dot_general(
@@ -392,11 +418,16 @@
         for c in range(CHUNKS):
             cols = slice(STARTS[c] * HD, (STARTS[c] + SIZES[c]) * HD)
             out[:, cols] = (parts[c] / denom * gain[:, cols]).astype(bf16)
-        for k, s in enumerate(held):
+        for k in range(count):
+            upper = (owner[me[0] * REQ + count * i + k] & 1) == 1
             for c in range(4):
-                proj[k * TAIL : (k + 1) * TAIL, c * DH : (c + 1) * DH] = s[
-                    0, heads, c * TAIL : (c + 1) * TAIL, :
-                ]
+                slab = held[k][1 + c % 2]
+                at = (c // 2) * TAIL
+                proj[k * TAIL : (k + 1) * TAIL, c * DH : (c + 1) * DH] = jnp.where(
+                    upper,
+                    slab[0, 2 * TAIL + at : 3 * TAIL + at, :],
+                    slab[0, at : TAIL + at, :],
+                )
     else:
         gated_ref[...] = gated
     who = lax.broadcasted_iota(jnp.int32, (128, STATE), 0) // TAIL
@@ -423,15 +454,30 @@
     at = STARTS[chunk] // heads
     rows = count * TAIL
 
+    def who(i, m, o, k):
+        return o[m[0] * REQ + count * i + k]
+
     def held(k):
-        return pl.BlockSpec(
-            (1,) + got.shape[1:], lambda i, m, o: (o[m[0] * REQ + count * i + k], 0, 0, 0)
-        )
+        if final_chunk:
+            return [
+                pl.BlockSpec((1, LAST, STATE), lambda i, m, o: (who(i, m, o, k), 0, 0)),
+                pl.BlockSpec(
+                    (1, SLAB, STATE), lambda i, m, o: (who(i, m, o, k) // 2 * 2, LAST // SLAB, 0)
+                ),
+                pl.BlockSpec(
+                    (1, SLAB, STATE),
+                    lambda i, m, o: (who(i, m, o, k) // 2 * 2 + 1, LAST // SLAB, 0),
+                ),
+            ]
+        return [
+            pl.BlockSpec((1, MOST, STATE), lambda i, m, o: (who(i, m, o, k), 0, 0)),
+            pl.BlockSpec((1, EARLY, STATE), lambda i, m, o: (who(i, m, o, k), 0, 0)),
+        ]
 
     def span(w, col=0):
         return pl.BlockSpec((rows, w), lambda i, m, o: (i, col))
 
-    in_specs = [SMEM] + [held(k) for k in range(count)]
+    in_specs = [SMEM] + [spec for k in range(count) for spec in held(k)]
     in_specs += [
         pl.BlockSpec((128, STATE), lambda i, m, o: (i * count // 8, 0)),
         span(STATE),
@@ -439,7 +485,7 @@
         span(width, at),
         span(width, at),
     ]
-    args = [dl] + [got] * count + [b, c, xt, base, ecx]
+    args = [dl] + list(got) * count + [b, c, xt, base, ecx]
     alias = {}
     if chunk > 0:
         alias = {2 + len(args): 0}
@@ -505,8 +551,7 @@
 
 def across(v, axis, left, right):
     n = v.shape[0] // 2
-    far = jnp.concatenate([hop(right[:n], axis, -1), hop(left[n:], axis, 1)], axis=0)
-    return jnp.stack([v, left, right, far])
+    return v, left, right, hop(right[:n], axis, -1), hop(left[n:], axis, 1)
 
 
 def turn(v, by):
@@ -537,22 +582,21 @@
     head = lax.axis_index("head").astype(jnp.int32).reshape(1)
     swap = [(r, r ^ 1) for r in range(REPS)]
     half = w_out.shape[0] // 2
-    queued = pack_q(me, owner, queries, tail_kv)
+    ckpt = ckpt_state.reshape(REQ, WIDTH, STATE)
+    queued, req = pack_first(me, owner, slot, queries, tail_kv, ckpt)
     asked = exchange(queued, "rep")
-    w_out = lax.optimization_barrier((w_out, queued))[0]
     a_half = ring(w_out[:half], "x")
     b_half = ring(w_out[half:], "y")
     a_side = sides(a_half, "y")
     b_side = sides(b_half, "x")
-    a_near = across(a_half, "y", *a_side)
-    b_near = across(b_half, "x", *b_side)
-    a_far = lax.ppermute(a_near, "rep", swap)
-    b_far = lax.ppermute(b_near, "rep", swap)
-    packed, req = pack_s(me, owner, slot, ckpt_state)
-    first = lax.optimization_barrier((packed[0], asked, a_near, b_near))[0]
-    got = exchange(first, "rep")
+    a_ring = across(a_half, "y", *a_side)
+    b_ring = across(b_half, "x", *b_side)
+    most, packed, both = pack_s(me, owner, slot, req, ckpt)
+    most = lax.optimization_barrier((most, asked, a_ring[3], a_ring[4], b_ring[3], b_ring[4]))[0]
+    got = exchange(most, "rep")
     attn = attend(req, page_table.reshape(-1), hit_len, tail_len, asked, kv_pool)
-    terms = project(me, head, attn, a_near, b_near, a_far, b_far)
+    other = lax.ppermute(attn, "rep", swap)
+    terms = project(me, head, attn, other, a_ring, b_ring)
     one, three, seven, five = relay(terms, turn(terms[0:6], 1), turn(terms[6:12], -1))
     parts = [turn(one, 1), turn(three, 3), turn(seven, -1), turn(five, -3)]
     base, ecx, xt, dl = prepare(
@@ -567,10 +611,12 @@
         skip_d.reshape(1, -1),
     )
     gain = norm_gain.reshape(1, -1)
-    last = exchange(total(req, terms, parts, packed[1]), "rep")
-    fin, rows = scan(0, me, owner, dl, got, group_b, group_c, xt, base, ecx, None, [], gain)
+    last = exchange(total(both, terms, parts, packed), "rep")
+    fin, rows = scan(
+        0, me, owner, dl, (got, asked), group_b, group_c, xt, base, ecx, None, [], gain
+    )
     fin, out, projected = scan(
-        1, me, owner, dl, last, group_b, group_c, xt, base, ecx, fin, [rows], gain
+        1, me, owner, dl, (last,) * 3, group_b, group_c, xt, base, ecx, fin, [rows], gain
     )
     return out, projected, fin
 

time: 213 us -> 207 us (0.972)
  starting transfers between devices: 75.4 us -> 60.8 us
  waiting for transfers between devices: 71.5 us -> 82.9 us
  other arithmetic: 5.76 us -> 0.14 us
  Pallas kernels: 48.3 us -> 50.9 us
    ppermute x14, waiting for transfers between devices: 12.2 us -> 36.3 us  [hop(): return lax.ppermute(v, 'rep', pairs)]
    all_to_all x3, waiting for transfers between devices: 31.3 us -> 17.4 us  [exchange(): return lax.all_to_all(x, axis, split_axis=0, concat_axis=0, tiled=True)]
    all_to_all x3, starting transfers between devices: 43.8 us -> 31.5 us  [exchange(): return lax.all_to_all(x, axis, split_axis=0, concat_axis=0, tiled=True)]
    another operation x6 -> x2, other arithmetic: 5.76 us -> 0.14 us  [ring(): return jnp.stack([v, hop(v, axis, 1), hop(v, axis, -1), hop(v, axis, 2)])]
    unnamed x40 -> x38, local copies, waits for them, and re-layouts: 5.29 us -> 5.69 us
  transfers between devices with their start and end apart: 25 -> 24, of which waited for: 9 -> 12; matrix products, arithmetic and copies ran while one was open for 5% -> 3% of each run, Pallas kernels for 19% -> 20%
where the time goes in v1:
time: 207 us; the launch traced here: 206 us
  waiting for transfers between devices  82.9 us (40%)
  starting transfers between devices  60.8 us (29%)
  Pallas kernels  50.9 us (25%)
  local copies, waits for them, and re-layouts  10.7 us (5%)
    ppermute x14, waiting for transfers between devices, hop(): return lax.ppermute(v, 'rep', pairs)  36.3 us
    all_to_all x3, starting transfers between devices, exchange(): return lax.all_to_all(x, axis, split_axis=0, concat_axis=0, tiled=True)  31.5 us
    ppermute x6, waiting for transfers between devices, turn(): lax.ppermute(v, 'head', [(z, (z + by) % NHEAD) for z in range(NHEAD)])  27.4 us
    all_to_all x3, waiting for transfers between devices, exchange(): return lax.all_to_all(x, axis, split_axis=0, concat_axis=0, tiled=True)  17.4 us
    ppermute x14, starting transfers between devices, hop(): return lax.ppermute(v, 'rep', pairs)  17.4 us
    pallas_call x2, Pallas kernels, scan(): pl.pallas_call(body, grid_spec=pltpu.PrefetchScalarGridSpec(num_scalar_pr...  15.5 us
    ppermute x6, starting transfers between devices, turn(): lax.ppermute(v, 'head', [(z, (z + by) % NHEAD) for z in range(NHEAD)])  11.6 us
    pallas_call x1, Pallas kernels, attend(): pl.pallas_call(attend_body, out_shape=sds((TOK, QH * DH), bf16), in_specs...  9.82 us
  transfers between devices with their start and end apart: 24, of which 12 were waited for; matrix products, arithmetic and copies ran while one was open for 3% of the time, Pallas kernels for 20%

profile of v1, /device:TPU:1, one launch (start us, length us, event | category | flops | bytes accessed | tf_op | source)
XLA Modules:
  0.0 206.5 jit_solution(15248844631103507362)
XLA Ops:
  0.6 3.8 %pack_first.1 = (bf16[32,288,128]{2,1,0:T(8,128)(2,1)}, s32[16]{0:T(128)}) custom-call(s32[1]{0:T(128)} %bitcast.me.refs_0_, s32[512]{0:T(512)} %refs_1_.3, s32[512]{0:T(512)} %slot.3, bf16[256,1024]{1,0:T(8,128)(2,1)} %q.1, bf16[256,256]{1,0:T(8,128)(2,1)} %kv.1, bf16[16,1024,128]{2,1,0:T(8,128)(2,1)} %bitcast.16), custom_call_target="tpu_custom_call" | custom-call | tf_op jit(solution)/shard_map/pack_first/pallas_call | solution.py:107
  4.5 8.7 %all-to-all-start = ((bf16[32,288,128]{2,1,0:T(8,128)(2,1)}), bf16[32,288,128]{2,1,0:T(8,128)(2,1)S(1)}, u32[]{:S(2)}, u32[]{:S(2)}) async-start(bf16[32,288,128]{2,1,0:T(8,128)(2,1)} %get-tuple-element.25), calls=%async_computation | async-start | bytes 4718592 | tf_op jit(solution)/shard_map/all_to_all | solution.py:526
  13.3 2.7 %collective-permute-start.2 = (bf16[512,128]{1,0:T(8,128)(2,1)S(1)}, bf16[512,128]{1,0:T(8,128)(2,1)S(1)}, u32[]{:S(2)}, u32[]{:S(2)}) collective-permute-start(bf16[512,128]{1,0:T(8,128)(2,1)S(1)} %get-tuple-element.46), channel_id=1, source_target_pairs={{0,192},{8,200},{16,208},{24,216},{32,224},{40,232},{48,240},{56,2... | collective-permute-start | bytes 393224 | tf_op jit(solution)/shard_map/ppermute | solution.py:541
  16.0 1.7 collective-permute-start.3
  17.7 2.4 %collective-permute-start.9 = (bf16[512,128]{1,0:T(8,128)(2,1)S(1)}, bf16[512,128]{1,0:T(8,128)(2,1)S(1)}, u32[]{:S(2)}, u32[]{:S(2)}) collective-permute-start(bf16[512,128]{1,0:T(8,128)(2,1)S(1)} %get-tuple-element.45), channel_id=1, source_target_pairs={{0,48},{8,56},{16,0},{24,8},{32,16},{40,24},{48,32},{56,40},{64,11... | collective-permute-start | bytes 393224 | tf_op jit(solution)/shard_map/ppermute | solution.py:541
  20.1 23.8 %collective-permute-done.2 = bf16[512,128]{1,0:T(8,128)(2,1)S(1)} collective-permute-done((bf16[512,128]{1,0:T(8,128)(2,1)S(1)}, bf16[512,128]{1,0:T(8,128)(2,1)S(1)}, u32[]{:S(2)}, u32[]{:S(2)}) %collective-permute-start.2) | collective-permute-done | bytes 131104 | tf_op jit(solution)/shard_map/ppermute | solution.py:541
  43.9 2.3 %collective-permute-start.10 = (bf16[512,128]{1,0:T(8,128)(2,1)S(1)}, bf16[512,128]{1,0:T(8,128)(2,1)S(1)}, u32[]{:S(2)}, u32[]{:S(2)}) collective-permute-start(bf16[512,128]{1,0:T(8,128)(2,1)S(1)} %get-tuple-element.45), channel_id=1, source_target_pairs={{0,32},{8,40},{16,48},{24,56},{32,0},{40,8},{48,16},{56,24},{64,96... | collective-permute-start | bytes 393224 | tf_op jit(solution)/shard_map/ppermute | solution.py:541
  46.2 1.8 collective-permute-done.3
  48.1 2.4 %collective-permute-start.5 = (bf16[4,512,128]{2,1,0:T(8,128)(2,1)S(1)}, bf16[4,512,128]{2,1,0:T(8,128)(2,1)S(1)}, u32[]{:S(2)}, u32[]{:S(2)}) collective-permute-start(bf16[4,512,128]{2,1,0:T(8,128)(2,1)S(1)} %pad_maximum_fusion.rest_0_), channel_id=1, source_target_pairs={{0,48},{8,56},{16,0},{24,8},{32,16},{40,24},{48,32},{56,40},{64,11... | collective-permute-start | bytes 1572872 | tf_op jit(solution)/shard_map/ppermute | solution.py:541
  52.2 9.3 %collective-permute-done.5.rest_2_ = bf16[4,512,128]{2,1,0:T(8,128)(2,1)S(1)} collective-permute-done((bf16[4,512,128]{2,1,0:T(8,128)(2,1)S(1)}, bf16[4,512,128]{2,1,0:T(8,128)(2,1)S(1)}, u32[]{:S(2)}, u32[]{:S(2)}) %collective-permute-start.5) | collective-permute-done | bytes 524320 | tf_op jit(solution)/shard_map/ppermute | solution.py:541
  62.2 2.8 %collective-permute-start.6 = (bf16[2,512,128]{2,1,0:T(8,128)(2,1)}, bf16[2,512,128]{2,1,0:T(8,128)(2,1)}, u32[]{:S(2)}, u32[]{:S(2)}) collective-permute-start(bf16[2,512,128]{2,1,0:T(8,128)(2,1)} %slice.32), channel_id=1, source_target_pairs={{0,48},{8,56},{16,0},{24,8},{32,16},{40,24},{48,32},{56,40},{64,11... | collective-permute-start | bytes 786440 | tf_op jit(solution)/shard_map/ppermute | solution.py:541
  68.8 5.0 %pack_s.1 = (bf16[32,768,128]{2,1,0:T(8,128)(2,1)}, bf16[32,192,128]{2,1,0:T(8,128)(2,1)}, s32[32]{0:T(128)}) custom-call(s32[1]{0:T(128)} %bitcast.me.refs_0_, s32[512]{0:T(512)} %refs_1_.3, s32[512]{0:T(512)} %slot.3, s32[16]{0:T(128)} %get-tuple-element.23.req, bf16[16,1024,128]{2,1,0:T(8,128)(2,1)} %bitcast.17), custom_call_target="tpu_custom_call" | custom-call | tf_op jit(solution)/shard_map/pack_s/pallas_call | solution.py:141
  73.8 1.4 collective-permute-done.14.rest_9_
  76.6 8.1 %all-to-all-start.2 = ((bf16[32,768,128]{2,1,0:T(8,128)(2,1)}), bf16[32,768,128]{2,1,0:T(8,128)(2,1)}, u32[]{:S(2)}, u32[]{:S(2)}) async-start(bf16[32,768,128]{2,1,0:T(8,128)(2,1)} %get-tuple-element.35), calls=%async_computation.2 | async-start | bytes 12582912 | tf_op jit(solution)/shard_map/all_to_all | solution.py:526
  85.6 9.8 %attend.1.mine = bf16[256,1024]{1,0:T(8,128)(2,1)} custom-call(s32[16]{0:T(128)} %get-tuple-element.23.req, s32[8192]{0:T(1024)} %reshape.32.pages, s32[512]{0:T(512)} %hit.1, s32[512]{0:T(512)} %tail.3, bf16[32,288,128]{2,1,0:T(8,128)(2,1)} %copy-done.1, bf16[256,16,256]{2,1,0:T(8,128)(2,1)} %pool.1), custom_call_target="tpu_custom_call" | custom-call | flops 8000000000 | bytes 4000000 | tf_op jit(solution)/shard_map/attend/pallas_call | solution.py:195
  95.8 1.8 collective-permute-done.other
  98.4 6.1 %project.1.terms = bf16[32,256,128]{2,1,0:T(8,128)(2,1)} custom-call(s32[1]{0:T(128)} %bitcast.me.refs_0_, s32[1]{0:T(128)} %bitcast.4.head, bf16[256,1024]{1,0:T(8,128)(2,1)} %attend.1.mine, bf16[256,1024]{1,0:T(8,128)(2,1)} %copy-done.15, bf16[4,512,128]{2,1,0:T(8,128)(2,1)} %copy-done.2, bf16[4,512,128]{2,1,0:T(8,128)(2,1)} %copy-done.10, ...), custom_call_target="tpu_custom_call" | custom-call | flops 8000000000 | bytes 11000000 | tf_op jit(solution)/shard_map/project/pallas_call | solution.py:240
  105.7 5.7 %collective-permute-start.16 = (bf16[6,256,128]{2,1,0:T(8,128)(2,1)S(1)}, bf16[6,256,128]{2,1,0:T(8,128)(2,1)S(1)}, u32[]{:S(2)}, u32[]{:S(2)}) collective-permute-start(bf16[6,256,128]{2,1,0:T(8,128)(2,1)S(1)} %get-tuple-element.41), channel_id=1, source_target_pairs={{0,7},{1,0},{2,1},{3,2},{4,3},{5,4},{6,5},{7,6},{8,15},{9,8},{10,9... | collective-permute-start | bytes 1179656 | tf_op jit(solution)/shard_map/ppermute | solution.py:558
  111.4 8.2 %collective-permute-done.16.down = bf16[6,256,128]{2,1,0:T(8,128)(2,1)S(1)} collective-permute-done((bf16[6,256,128]{2,1,0:T(8,128)(2,1)S(1)}, bf16[6,256,128]{2,1,0:T(8,128)(2,1)S(1)}, u32[]{:S(2)}, u32[]{:S(2)}) %collective-permute-start.16) | collective-permute-done | bytes 393248 | tf_op jit(solution)/shard_map/ppermute | solution.py:558
  119.5 3.2 %collective-permute-done.15.up = bf16[6,256,128]{2,1,0:T(8,128)(2,1)S(1)} collective-permute-done((bf16[6,256,128]{2,1,0:T(8,128)(2,1)S(1)}, bf16[6,256,128]{2,1,0:T(8,128)(2,1)S(1)}, u32[]{:S(2)}, u32[]{:S(2)}) %collective-permute-start.15) | collective-permute-done | bytes 393248 | tf_op jit(solution)/shard_map/ppermute | solution.py:558
  123.5 2.8 %relay.1 = (bf16[4,256,128]{2,1,0:T(8,128)(2,1)}, bf16[4,256,128]{2,1,0:T(8,128)(2,1)}, bf16[4,256,128]{2,1,0:T(8,128)(2,1)}, bf16[4,256,128]{2,1,0:T(8,128)(2,1)}) custom-call(bf16[32,256,128]{2,1,0:T(8,128)(2,1)} %project.1.terms, bf16[6,256,128]{2,1,0:T(8,128)(2,1)} %copy-done.17, bf16[6,256,128]{2,1,0:T(8,128)(2,1)} %copy-done.16), custom_call_target="tpu_custom_call" | custom-call | flops 1000000000 | bytes 3000000 | tf_op jit(solution)/shard_map/relay/pallas_call | solution.py:265
  126.3 2.0 collective-permute-start.18
  129.1 3.1 %collective-permute-start.20 = (bf16[4,256,128]{2,1,0:T(8,128)(2,1)}, bf16[4,256,128]{2,1,0:T(8,128)(2,1)S(1)}, u32[]{:S(2)}, u32[]{:S(2)}) collective-permute-start(bf16[4,256,128]{2,1,0:T(8,128)(2,1)} %get-tuple-element.29), channel_id=1, source_target_pairs={{0,5},{1,6},{2,7},{3,0},{4,1},{5,2},{6,3},{7,4},{8,13},{9,14},{10,... | collective-permute-start | bytes 786440 | tf_op jit(solution)/shard_map/ppermute | solution.py:558
  132.2 2.6 %collective-permute-done.17.rest_0_ = bf16[4,256,128]{2,1,0:T(8,128)(2,1)S(1)} collective-permute-done((bf16[4,256,128]{2,1,0:T(8,128)(2,1)}, bf16[4,256,128]{2,1,0:T(8,128)(2,1)S(1)}, u32[]{:S(2)}, u32[]{:S(2)}) %collective-permute-start.17) | collective-permute-done | bytes 262176 | tf_op jit(solution)/shard_map/ppermute | solution.py:558
  134.8 12.9 %collective-permute-done.18.rest_1_ = bf16[4,256,128]{2,1,0:T(8,128)(2,1)S(1)} collective-permute-done((bf16[4,256,128]{2,1,0:T(8,128)(2,1)}, bf16[4,256,128]{2,1,0:T(8,128)(2,1)S(1)}, u32[]{:S(2)}, u32[]{:S(2)}) %collective-permute-start.18) | collective-permute-done | bytes 262176 | tf_op jit(solution)/shard_map/ppermute | solution.py:558
  148.9 2.7 %total.1 = bf16[32,192,128]{2,1,0:T(8,128)(2,1)} custom-call(s32[32]{0:T(128)} %get-tuple-element.24.both, bf16[32,256,128]{2,1,0:T(8,128)(2,1)} %project.1.terms, bf16[4,256,128]{2,1,0:T(8,128)(2,1)} %copy-done.5, bf16[4,256,128]{2,1,0:T(8,128)(2,1)} %copy-done.6, bf16[4,256,128]{2,1,0:T(8,128)(2,1)} %copy-done.7, ...), custom_call_target="tpu_custom_call", output_to_operand_aliasing={{}: (6, {})} | custom-call | flops 1000000000 | bytes 3000000 | tf_op jit(solution)/shard_map/total/pallas_call | solution.py:297
  151.6 10.4 %all-to-all-done.2.refs_3_.refs_5_ = bf16[32,768,128]{2,1,0:T(8,128)(2,1)} async-done(((bf16[32,768,128]{2,1,0:T(8,128)(2,1)}), bf16[32,768,128]{2,1,0:T(8,128)(2,1)}, u32[]{:S(2)}, u32[]{:S(2)}) %all-to-all-start.2) | async-done | bytes 6291488 | tf_op jit(solution)/shard_map/all_to_all | solution.py:526
  162.1 14.7 %all-to-all-start.1 = ((bf16[32,192,128]{2,1,0:T(8,128)(2,1)}), bf16[32,192,128]{2,1,0:T(8,128)(2,1)S(1)}, u32[]{:S(2)}, u32[]{:S(2)}) async-start(bf16[32,192,128]{2,1,0:T(8,128)(2,1)} %total.1), calls=%async_computation.1 | async-start | bytes 3145728 | tf_op jit(solution)/shard_map/all_to_all | solution.py:526
  177.5 5.1 %prepare.1 = (f32[256,1024]{1,0:T(8,128)}, f32[256,1024]{1,0:T(8,128)}, bf16[2,1024,256]{2,1,0:T(8,128)(2,1)}, f32[16,16]{1,0:T(8,128)}) custom-call(s32[1]{0:T(128)} %bitcast.me.refs_0_, s32[512]{0:T(512)} %tail.3, bf16[256,1024]{1,0:T(8,128)(2,1)} %x_ref.1, bf16[256,1024]{1,0:T(8,128)(2,1)} %z_ref.1, bf16[256,128]{1,0:T(8,128)(2,1)} %refs_15_.1, ...), custom_call_target="tpu_custom_call" | custom-call | flops 8000000000 | bytes 5000000 | tf_op jit(solution)/shard_map/prepare/pallas_call | solution.py:362
  182.6 9.8 %shard_map.193 = (bf16[16,16,64,128]{3,2,1,0:T(8,128)(2,1)}, f32[256,896]{1,0:T(8,128)}) custom-call(s32[1]{0:T(128)} %bitcast.me.refs_0_, s32[512]{0:T(512)} %refs_1_.3, f32[16,16]{1,0:T(8,128)} %get-tuple-element.22.refs_2_, bf16[32,768,128]{2,1,0:T(8,128)(2,1)} %all-to-all-done.2.refs_3_.refs_5_, bf16[32,288,128]{2,1,0:T(8,128)(2,1)} %copy-done.1, ...), custom_call_target="tpu_custom_call" | custom-call | flops 4000000000 | bytes 8000000 | tf_op jit(solution)/shard_map/pallas_call | solution.py:508
  192.4 7.0 %all-to-all-done.1.refs_3_.refs_4_.refs_5_.refs_6_.refs_7_.refs_8_.refs_9_.refs_10_.refs_11_.refs_12_.refs_13_.refs_14_ = bf16[32,192,128]{2,1,0:T(8,128)(2,1)S(1)} async-done(((bf16[32,192,128]{2,1,0:T(8,128)(2,1)}), bf16[32,192,128]{2,1,0:T(8,128)(2,1)S(1)}, u32[]{:S(2)}, u32[]{:S(2)}) %all-to-all-start.1) | async-done | bytes 1572896 | tf_op jit(solution)/shard_map/all_to_all | solution.py:526
  200.6 5.8 %shard_map.194 = (bf16[16,16,64,128]{3,2,1,0:T(8,128)(2,1)}, bf16[256,1024]{1,0:T(8,128)(2,1)}, bf16[256,512]{1,0:T(8,128)(2,1)}) custom-call(s32[1]{0:T(128)} %bitcast.me.refs_0_, s32[512]{0:T(512)} %refs_1_.3, f32[16,16]{1,0:T(8,128)} %get-tuple-element.22.refs_2_, bf16[32,192,128]{2,1,0:T(8,128)(2,1)} %copy-done, ...), custom_call_target="tpu_custom_call", output_to_operand_aliasing={{0}: (20, {})} | custom-call | flops 4000000000 | bytes 8000000 | tf_op jit(solution)/shard_map/pallas_call | solution.py:508
  (72 shorter events, 15.5 us)
Async XLA Ops:
  4.4 8.7 %copy-start.4 = (bf16[1024,128]{1,0:T(8,128)(2,1)S(1)}, bf16[1024,128]{1,0:T(8,128)(2,1)}, u32[]{:S(2)}) copy-start(bf16[1024,128]{1,0:T(8,128)(2,1)} %param.27) | copy-start | bytes 786436
  4.5 70.8 %all-to-all-start = ((bf16[32,288,128]{2,1,0:T(8,128)(2,1)}), bf16[32,288,128]{2,1,0:T(8,128)(2,1)S(1)}, u32[]{:S(2)}, u32[]{:S(2)}) async-start(bf16[32,288,128]{2,1,0:T(8,128)(2,1)} %get-tuple-element.25), calls=%async_computation | async-start | bytes 4718592 | tf_op jit(solution)/shard_map/all_to_all | solution.py:526
  13.3 30.6 %collective-permute-start.2 = (bf16[512,128]{1,0:T(8,128)(2,1)S(1)}, bf16[512,128]{1,0:T(8,128)(2,1)S(1)}, u32[]{:S(2)}, u32[]{:S(2)}) collective-permute-start(bf16[512,128]{1,0:T(8,128)(2,1)S(1)} %get-tuple-element.46), channel_id=1, source_target_pairs={{0,192},{8,200},{16,208},{24,216},{32,224},{40,232},{48,240},{56,2... | collective-permute-start | bytes 393224 | tf_op jit(solution)/shard_map/ppermute | solution.py:541
  16.0 30.2 %collective-permute-start.1 = (bf16[512,128]{1,0:T(8,128)(2,1)S(1)}, bf16[512,128]{1,0:T(8,128)(2,1)S(1)}, u32[]{:S(2)}, u32[]{:S(2)}) collective-permute-start(bf16[512,128]{1,0:T(8,128)(2,1)S(1)} %get-tuple-element.46), channel_id=1, source_target_pairs={{0,64},{8,72},{16,80},{24,88},{32,96},{40,104},{48,112},{56,120},{... | collective-permute-start | bytes 393224 | tf_op jit(solution)/shard_map/ppermute | solution.py:541
  16.0 32.0 %collective-permute-start.3 = (bf16[512,128]{1,0:T(8,128)(2,1)S(1)}, bf16[512,128]{1,0:T(8,128)(2,1)S(1)}, u32[]{:S(2)}, u32[]{:S(2)}) collective-permute-start(bf16[512,128]{1,0:T(8,128)(2,1)S(1)} %get-tuple-element.46), channel_id=1, source_target_pairs={{0,128},{8,136},{16,144},{24,152},{32,160},{40,168},{48,176},{56,1... | collective-permute-start | bytes 393224 | tf_op jit(solution)/shard_map/ppermute | solution.py:541
  17.7 32.8 %collective-permute-start.9 = (bf16[512,128]{1,0:T(8,128)(2,1)S(1)}, bf16[512,128]{1,0:T(8,128)(2,1)S(1)}, u32[]{:S(2)}, u32[]{:S(2)}) collective-permute-start(bf16[512,128]{1,0:T(8,128)(2,1)S(1)} %get-tuple-element.45), channel_id=1, source_target_pairs={{0,48},{8,56},{16,0},{24,8},{32,16},{40,24},{48,32},{56,40},{64,11... | collective-permute-start | bytes 393224 | tf_op jit(solution)/shard_map/ppermute | solution.py:541
  20.1 30.4 %collective-permute-start.8 = (bf16[512,128]{1,0:T(8,128)(2,1)S(1)}, bf16[512,128]{1,0:T(8,128)(2,1)S(1)}, u32[]{:S(2)}, u32[]{:S(2)}) collective-permute-start(bf16[512,128]{1,0:T(8,128)(2,1)S(1)} %get-tuple-element.45), channel_id=1, source_target_pairs={{0,16},{8,24},{16,32},{24,40},{32,48},{40,56},{48,0},{56,8},{64,80... | collective-permute-start | bytes 393224 | tf_op jit(solution)/shard_map/ppermute | solution.py:541
  43.9 6.7 %collective-permute-start.10 = (bf16[512,128]{1,0:T(8,128)(2,1)S(1)}, bf16[512,128]{1,0:T(8,128)(2,1)S(1)}, u32[]{:S(2)}, u32[]{:S(2)}) collective-permute-start(bf16[512,128]{1,0:T(8,128)(2,1)S(1)} %get-tuple-element.45), channel_id=1, source_target_pairs={{0,32},{8,40},{16,48},{24,56},{32,0},{40,8},{48,16},{56,24},{64,96... | collective-permute-start | bytes 393224 | tf_op jit(solution)/shard_map/ppermute | solution.py:541
  48.1 25.7 %copy-start.2 = (bf16[4,512,128]{2,1,0:T(8,128)(2,1)}, bf16[4,512,128]{2,1,0:T(8,128)(2,1)S(1)}, u32[]{:S(2)}) copy-start(bf16[4,512,128]{2,1,0:T(8,128)(2,1)S(1)} %pad_maximum_fusion.rest_0_) | copy-start | bytes 1572868
  48.1 13.4 %collective-permute-start.5 = (bf16[4,512,128]{2,1,0:T(8,128)(2,1)S(1)}, bf16[4,512,128]{2,1,0:T(8,128)(2,1)S(1)}, u32[]{:S(2)}, u32[]{:S(2)}) collective-permute-start(bf16[4,512,128]{2,1,0:T(8,128)(2,1)S(1)} %pad_maximum_fusion.rest_0_), channel_id=1, source_target_pairs={{0,48},{8,56},{16,0},{24,8},{32,16},{40,24},{48,32},{56,40},{64,11... | collective-permute-start | bytes 1572872 | tf_op jit(solution)/shard_map/ppermute | solution.py:541
  50.5 14.5 %collective-permute-start.4 = (bf16[4,512,128]{2,1,0:T(8,128)(2,1)S(1)}, bf16[4,512,128]{2,1,0:T(8,128)(2,1)S(1)}, u32[]{:S(2)}, u32[]{:S(2)}) collective-permute-start(bf16[4,512,128]{2,1,0:T(8,128)(2,1)S(1)} %pad_maximum_fusion.rest_0_), channel_id=1, source_target_pairs={{0,16},{8,24},{16,32},{24,40},{32,48},{40,56},{48,0},{56,8},{64,80... | collective-permute-start | bytes 1572872 | tf_op jit(solution)/shard_map/ppermute | solution.py:541
  50.6 23.2 %copy-start.3 = (bf16[4,512,128]{2,1,0:T(8,128)(2,1)}, bf16[4,512,128]{2,1,0:T(8,128)(2,1)S(1)}, u32[]{:S(2)}) copy-start(bf16[4,512,128]{2,1,0:T(8,128)(2,1)S(1)} %pad_maximum_fusion.1.rest_5_) | copy-start | bytes 1572868
  50.6 15.2 %collective-permute-start.12 = (bf16[4,512,128]{2,1,0:T(8,128)(2,1)S(1)}, bf16[4,512,128]{2,1,0:T(8,128)(2,1)S(1)}, u32[]{:S(2)}, u32[]{:S(2)}) collective-permute-start(bf16[4,512,128]{2,1,0:T(8,128)(2,1)S(1)} %pad_maximum_fusion.1.rest_5_), channel_id=1, source_target_pairs={{0,192},{8,200},{16,208},{24,216},{32,224},{40,232},{48,240},{56,2... | collective-permute-start | bytes 1572872 | tf_op jit(solution)/shard_map/ppermute | solution.py:541
  51.6 15.9 %collective-permute-start.11 = (bf16[4,512,128]{2,1,0:T(8,128)(2,1)S(1)}, bf16[4,512,128]{2,1,0:T(8,128)(2,1)S(1)}, u32[]{:S(2)}, u32[]{:S(2)}) collective-permute-start(bf16[4,512,128]{2,1,0:T(8,128)(2,1)S(1)} %pad_maximum_fusion.1.rest_5_), channel_id=1, source_target_pairs={{0,64},{8,72},{16,80},{24,88},{32,96},{40,104},{48,112},{56,120},{... | collective-permute-start | bytes 1572872 | tf_op jit(solution)/shard_map/ppermute | solution.py:541
  61.4 6.0 %copy-start.9 = (bf16[4,512,128]{2,1,0:T(8,128)(2,1)}, bf16[4,512,128]{2,1,0:T(8,128)(2,1)S(1)}, u32[]{:S(2)}) copy-start(bf16[4,512,128]{2,1,0:T(8,128)(2,1)S(1)} %collective-permute-done.5.rest_2_) | copy-start | bytes 1572868
  62.2 11.6 %collective-permute-start.6 = (bf16[2,512,128]{2,1,0:T(8,128)(2,1)}, bf16[2,512,128]{2,1,0:T(8,128)(2,1)}, u32[]{:S(2)}, u32[]{:S(2)}) collective-permute-start(bf16[2,512,128]{2,1,0:T(8,128)(2,1)} %slice.32), channel_id=1, source_target_pairs={{0,48},{8,56},{16,0},{24,8},{32,16},{40,24},{48,32},{56,40},{64,11... | collective-permute-start | bytes 786440 | tf_op jit(solution)/shard_map/ppermute | solution.py:541
  65.8 8.0 %collective-permute-start.7 = (bf16[2,512,128]{2,1,0:T(8,128)(2,1)}, bf16[2,512,128]{2,1,0:T(8,128)(2,1)}, u32[]{:S(2)}, u32[]{:S(2)}) collective-permute-start(bf16[2,512,128]{2,1,0:T(8,128)(2,1)} %slice.33), channel_id=1, source_target_pairs={{0,16},{8,24},{16,32},{24,40},{32,48},{40,56},{48,0},{56,8},{64,80... | collective-permute-start | bytes 786440 | tf_op jit(solution)/shard_map/ppermute | solution.py:541
  66.6 7.3 %collective-permute-start.13 = (bf16[2,512,128]{2,1,0:T(8,128)(2,1)}, bf16[2,512,128]{2,1,0:T(8,128)(2,1)}, u32[]{:S(2)}, u32[]{:S(2)}) collective-permute-start(bf16[2,512,128]{2,1,0:T(8,128)(2,1)} %slice.34), channel_id=1, source_target_pairs={{0,192},{8,200},{16,208},{24,216},{32,224},{40,232},{48,240},{56,2... | collective-permute-start | bytes 786440 | tf_op jit(solution)/shard_map/ppermute | solution.py:541
  68.2 7.0 %collective-permute-start.14 = (bf16[2,512,128]{2,1,0:T(8,128)(2,1)}, bf16[2,512,128]{2,1,0:T(8,128)(2,1)}, u32[]{:S(2)}, u32[]{:S(2)}) collective-permute-start(bf16[2,512,128]{2,1,0:T(8,128)(2,1)} %slice.35), channel_id=1, source_target_pairs={{0,64},{8,72},{16,80},{24,88},{32,96},{40,104},{48,112},{56,120},{... | collective-permute-start | bytes 786440 | tf_op jit(solution)/shard_map/ppermute | solution.py:541
  75.3 9.5 %copy-start.13 = (s32[512,16]{0,1:T(8,128)S(1)}, s32[512,16]{0,1:T(8,128)}, u32[]{:S(2)}) copy-start(s32[512,16]{0,1:T(8,128)} %param.33) | copy-start | bytes 98308
  76.6 85.4 %all-to-all-start.2 = ((bf16[32,768,128]{2,1,0:T(8,128)(2,1)}), bf16[32,768,128]{2,1,0:T(8,128)(2,1)}, u32[]{:S(2)}, u32[]{:S(2)}) async-start(bf16[32,768,128]{2,1,0:T(8,128)(2,1)} %get-tuple-element.35), calls=%async_computation.2 | async-start | bytes 12582912 | tf_op jit(solution)/shard_map/all_to_all | solution.py:526
  95.5 2.1 %collective-permute-start = (bf16[256,1024]{1,0:T(8,128)(2,1)}, bf16[256,1024]{1,0:T(8,128)(2,1)S(1)}, u32[]{:S(2)}, u32[]{:S(2)}) collective-permute-start(bf16[256,1024]{1,0:T(8,128)(2,1)} %attend.1.mine), channel_id=1, source_target_pairs={{0,8},{8,0},{16,24},{24,16},{32,40},{40,32},{48,56},{56,48},{64,72... | collective-permute-start | bytes 1572872 | tf_op jit(solution)/shard_map/ppermute | solution.py:598
  105.7 13.8 %collective-permute-start.16 = (bf16[6,256,128]{2,1,0:T(8,128)(2,1)S(1)}, bf16[6,256,128]{2,1,0:T(8,128)(2,1)S(1)}, u32[]{:S(2)}, u32[]{:S(2)}) collective-permute-start(bf16[6,256,128]{2,1,0:T(8,128)(2,1)S(1)} %get-tuple-element.41), channel_id=1, source_target_pairs={{0,7},{1,0},{2,1},{3,2},{4,3},{5,4},{6,5},{7,6},{8,15},{9,8},{10,9... | collective-permute-start | bytes 1179656 | tf_op jit(solution)/shard_map/ppermute | solution.py:558
  111.3 11.4 %collective-permute-start.15 = (bf16[6,256,128]{2,1,0:T(8,128)(2,1)S(1)}, bf16[6,256,128]{2,1,0:T(8,128)(2,1)S(1)}, u32[]{:S(2)}, u32[]{:S(2)}) collective-permute-start(bf16[6,256,128]{2,1,0:T(8,128)(2,1)S(1)} %get-tuple-element.42), channel_id=1, source_target_pairs={{0,1},{1,2},{2,3},{3,4},{4,5},{5,6},{6,7},{7,0},{8,9},{9,10},{10,1... | collective-permute-start | bytes 1179656 | tf_op jit(solution)/shard_map/ppermute | solution.py:558
  119.5 3.2 %copy-start.16 = (bf16[6,256,128]{2,1,0:T(8,128)(2,1)}, bf16[6,256,128]{2,1,0:T(8,128)(2,1)S(1)}, u32[]{:S(2)}) copy-start(bf16[6,256,128]{2,1,0:T(8,128)(2,1)S(1)} %collective-permute-done.16.down) | copy-start | bytes 1179652
  126.3 8.5 %collective-permute-start.17 = (bf16[4,256,128]{2,1,0:T(8,128)(2,1)}, bf16[4,256,128]{2,1,0:T(8,128)(2,1)S(1)}, u32[]{:S(2)}, u32[]{:S(2)}) collective-permute-start(bf16[4,256,128]{2,1,0:T(8,128)(2,1)} %get-tuple-element.26), channel_id=1, source_target_pairs={{0,1},{1,2},{2,3},{3,4},{4,5},{5,6},{6,7},{7,0},{8,9},{9,10},{10,1... | collective-permute-start | bytes 786440 | tf_op jit(solution)/shard_map/ppermute | solution.py:558
  126.3 21.5 %collective-permute-start.18 = (bf16[4,256,128]{2,1,0:T(8,128)(2,1)}, bf16[4,256,128]{2,1,0:T(8,128)(2,1)S(1)}, u32[]{:S(2)}, u32[]{:S(2)}) collective-permute-start(bf16[4,256,128]{2,1,0:T(8,128)(2,1)} %get-tuple-element.27), channel_id=1, source_target_pairs={{0,3},{1,4},{2,5},{3,6},{4,7},{5,0},{6,1},{7,2},{8,11},{9,12},{10,... | collective-permute-start | bytes 786440 | tf_op jit(solution)/shard_map/ppermute | solution.py:558
  128.2 19.5 %collective-permute-start.19 = (bf16[4,256,128]{2,1,0:T(8,128)(2,1)}, bf16[4,256,128]{2,1,0:T(8,128)(2,1)S(1)}, u32[]{:S(2)}, u32[]{:S(2)}) collective-permute-start(bf16[4,256,128]{2,1,0:T(8,128)(2,1)} %get-tuple-element.28), channel_id=1, source_target_pairs={{0,7},{1,0},{2,1},{3,2},{4,3},{5,4},{6,5},{7,6},{8,15},{9,8},{10,9... | collective-permute-start | bytes 786440 | tf_op jit(solution)/shard_map/ppermute | solution.py:558
  129.1 19.1 %collective-permute-start.20 = (bf16[4,256,128]{2,1,0:T(8,128)(2,1)}, bf16[4,256,128]{2,1,0:T(8,128)(2,1)S(1)}, u32[]{:S(2)}, u32[]{:S(2)}) collective-permute-start(bf16[4,256,128]{2,1,0:T(8,128)(2,1)} %get-tuple-element.29), channel_id=1, source_target_pairs={{0,5},{1,6},{2,7},{3,0},{4,1},{5,2},{6,3},{7,4},{8,13},{9,14},{10,... | collective-permute-start | bytes 786440 | tf_op jit(solution)/shard_map/ppermute | solution.py:558
  134.8 13.4 %copy-start.5 = (bf16[4,256,128]{2,1,0:T(8,128)(2,1)}, bf16[4,256,128]{2,1,0:T(8,128)(2,1)S(1)}, u32[]{:S(2)}) copy-start(bf16[4,256,128]{2,1,0:T(8,128)(2,1)S(1)} %collective-permute-done.17.rest_0_) | copy-start | bytes 786436
  151.6 25.1 %copy-start.14 = (bf16[256,16]{0,1:T(8,128)(2,1)S(1)}, bf16[256,16]{0,1:T(8,128)(2,1)}, u32[]{:S(2)}) copy-start(bf16[256,16]{0,1:T(8,128)(2,1)} %param.22) | copy-start | bytes 24580
  162.1 37.3 %all-to-all-start.1 = ((bf16[32,192,128]{2,1,0:T(8,128)(2,1)}), bf16[32,192,128]{2,1,0:T(8,128)(2,1)S(1)}, u32[]{:S(2)}, u32[]{:S(2)}) async-start(bf16[32,192,128]{2,1,0:T(8,128)(2,1)} %total.1), calls=%async_computation.1 | async-start | bytes 3145728 | tf_op jit(solution)/shard_map/all_to_all | solution.py:526
  (10 other events, 13.8 us)

commit v2 on v1

--- a/solution.py
+++ b/solution.py
@@ -22,13 +22,13 @@
 WIDTH = HEADS * HD
 NHEAD = 8
 NEAR = (0, -1, 1, 2)
-SIZES = (14, 2)
-STARTS = (0, 14)
+SIZES = (12, 4)
+STARTS = (0, 12)
 STEPS = (2, 4)
 CHUNKS = len(SIZES)
 EARLY = 2 * HD
-MOST = 12 * HD
-LAST = 2 * HD
+MOST = 10 * HD
+LAST = 4 * HD
 SLAB = 4 * TAIL
 ASK = (QH + 2) * TAIL
 
@@ -213,16 +213,14 @@
 
 
 def project_body(me, head, mine, other, *rest):
-    a_ring, b_ring, out = rest[:5], rest[5:10], rest[10]
+    a_ring, b_ring, out = rest[:8], rest[8:16], rest[16]
     x = me[0] // 8
     y = (me[0] // 2) & 3
     par = me[0] & 1
     half = QH * DH // 2
 
     def block(ring, outer, inner):
-        if outer < 3:
-            return ring[outer][inner]
-        return ring[3 + inner // 2][inner % 2]
+        return ring[2 * outer + inner // 2][inner % 2]
 
     for dy in range(4):
         for dx in (0, 2):
@@ -240,7 +238,7 @@
     return pl.pallas_call(
         project_body,
         out_shape=sds((4 * NHEAD, TOK, DH), bf16),
-        in_specs=[SMEM, SMEM] + [VMEM] * 12,
+        in_specs=[SMEM, SMEM] + [VMEM] * 18,
         out_specs=VMEM,
         cost_estimate=pl.CostEstimate(
             flops=8_000_000_000, transcendentals=0, bytes_accessed=11_000_000
@@ -542,16 +540,18 @@
 
 
 def ring(v, axis):
-    return jnp.stack([v, hop(v, axis, 1), hop(v, axis, -1), hop(v, axis, 2)])
+    return (
+        jnp.stack([v, hop(v, axis, 1)]),
+        jnp.stack([hop(v, axis, -1), hop(v, axis, 2)]),
+    )
 
 
 def sides(v, axis):
-    return hop(v, axis, 1), hop(v, axis, -1)
-
-
-def across(v, axis, left, right):
-    n = v.shape[0] // 2
-    return v, left, right, hop(right[:n], axis, -1), hop(left[n:], axis, 1)
+    return [hop(p, axis, by) for by in (1, -1) for p in v]
+
+
+def across(v, axis, near):
+    return [*v, *near, hop(near[2], axis, -1), hop(near[1], axis, 1)]
 
 
 def turn(v, by):
@@ -589,10 +589,10 @@
     b_half = ring(w_out[half:], "y")
     a_side = sides(a_half, "y")
     b_side = sides(b_half, "x")
-    a_ring = across(a_half, "y", *a_side)
-    b_ring = across(b_half, "x", *b_side)
+    a_ring = across(a_half, "y", a_side)
+    b_ring = across(b_half, "x", b_side)
     most, packed, both = pack_s(me, owner, slot, req, ckpt)
-    most = lax.optimization_barrier((most, asked, a_ring[3], a_ring[4], b_ring[3], b_ring[4]))[0]
+    most = lax.optimization_barrier((most, asked))[0]
     got = exchange(most, "rep")
     attn = attend(req, page_table.reshape(-1), hit_len, tail_len, asked, kv_pool)
     other = lax.ppermute(attn, "rep", swap)

time: 207 us -> 266 us (1.29)
  waiting for transfers between devices: 82.9 us -> 135 us
  starting transfers between devices: 60.8 us -> 68.5 us
    ppermute x14 -> x18, waiting for transfers between devices: 36.3 us -> 67.4 us  [hop(): return lax.ppermute(v, 'rep', pairs)]
    all_to_all x3, waiting for transfers between devices: 17.4 us -> 45.2 us  [exchange(): return lax.all_to_all(x, axis, split_axis=0, concat_axis=0, tiled=True)]
    ppermute x14 -> x18, starting transfers between devices: 17.4 us -> 26.1 us  [hop(): return lax.ppermute(v, 'rep', pairs)]
    ppermute x6, waiting for transfers between devices: 27.4 us -> 22.9 us  [turn(): lax.ppermute(v, 'head', [(z, (z + by) % NHEAD) for z in range(NHEAD)])]
    all_to_all x3, starting transfers between devices: 31.5 us -> 27.5 us  [exchange(): return lax.all_to_all(x, axis, split_axis=0, concat_axis=0, tiled=True)]
    slice x4 -> x0, local copies, waits for them, and re-layouts: 3.07 us -> none  [across(): return (v, left, right, hop(right[:n], axis, -1), hop(left[n:], axis, 1))]
    ppermute x1, starting transfers between devices: 0.3 us -> 3.15 us  [step(): other = lax.ppermute(attn, 'rep', swap)]
    unnamed x38 -> x58, local copies, waits for them, and re-layouts: 5.69 us -> 6.95 us
  transfers between devices with their start and end apart: 24 -> 28, of which waited for: 12 -> 13; matrix products, arithmetic and copies ran while one was open for 3% -> 1% of each run, Pallas kernels for 20% -> 15%
where the time goes in v2:
time: 266 us; the launch traced here: 264 us
  waiting for transfers between devices  135 us (51%)
  starting transfers between devices  68.5 us (26%)
  Pallas kernels  50.3 us (19%)
  local copies, waits for them, and re-layouts  8.94 us (3%)
    ppermute x18, waiting for transfers between devices, hop(): return lax.ppermute(v, 'rep', pairs)  67.4 us
    all_to_all x3, waiting for transfers between devices, exchange(): return lax.all_to_all(x, axis, split_axis=0, concat_axis=0, tiled=True)  45.2 us
    all_to_all x3, starting transfers between devices, exchange(): return lax.all_to_all(x, axis, split_axis=0, concat_axis=0, tiled=True)  27.5 us
    ppermute x18, starting transfers between devices, hop(): return lax.ppermute(v, 'rep', pairs)  26.1 us
    ppermute x6, waiting for transfers between devices, turn(): lax.ppermute(v, 'head', [(z, (z + by) % NHEAD) for z in range(NHEAD)])  22.9 us
    pallas_call x2, Pallas kernels, scan(): pl.pallas_call(body, grid_spec=pltpu.PrefetchScalarGridSpec(num_scalar_pr...  14.9 us
    ppermute x6, starting transfers between devices, turn(): lax.ppermute(v, 'head', [(z, (z + by) % NHEAD) for z in range(NHEAD)])  11.7 us
    pallas_call x1, Pallas kernels, attend(): pl.pallas_call(attend_body, out_shape=sds((TOK, QH * DH), bf16), in_specs...  9.82 us
  transfers between devices with their start and end apart: 28, of which 13 were waited for; matrix products, arithmetic and copies ran while one was open for 1% of the time, Pallas kernels for 15%

profile of v2, /device:TPU:1, one launch (start us, length us, event | category | flops | bytes accessed | tf_op | source)
XLA Modules:
  0.0 264.4 jit_solution(13365407755198219594)
XLA Ops:
  0.6 3.8 %pack_first.1 = (bf16[32,288,128]{2,1,0:T(8,128)(2,1)}, s32[16]{0:T(128)}) custom-call(s32[1]{0:T(128)} %bitcast.me.refs_0_, s32[512]{0:T(512)} %refs_1_.3, s32[512]{0:T(512)} %slot.3, bf16[256,1024]{1,0:T(8,128)(2,1)} %q.1, bf16[256,256]{1,0:T(8,128)(2,1)} %kv.1, bf16[16,1024,128]{2,1,0:T(8,128)(2,1)} %bitcast.16), custom_call_target="tpu_custom_call" | custom-call | tf_op jit(solution)/shard_map/pack_first/pallas_call | solution.py:107
  4.4 8.6 %all-to-all-start = ((bf16[32,288,128]{2,1,0:T(8,128)(2,1)}), bf16[32,288,128]{2,1,0:T(8,128)(2,1)S(1)}, u32[]{:S(2)}, u32[]{:S(2)}) async-start(bf16[32,288,128]{2,1,0:T(8,128)(2,1)} %get-tuple-element.25), calls=%async_computation | async-start | bytes 4718592 | tf_op jit(solution)/shard_map/all_to_all | solution.py:524
  13.0 5.0 %pack_s.1 = (bf16[32,640,128]{2,1,0:T(8,128)(2,1)}, bf16[32,320,128]{2,1,0:T(8,128)(2,1)}, s32[32]{0:T(128)}) custom-call(s32[1]{0:T(128)} %bitcast.me.refs_0_, s32[512]{0:T(512)} %refs_1_.3, s32[512]{0:T(512)} %slot.3, s32[16]{0:T(128)} %get-tuple-element.23.req, bf16[16,1024,128]{2,1,0:T(8,128)(2,1)} %bitcast.17), custom_call_target="tpu_custom_call" | custom-call | tf_op jit(solution)/shard_map/pack_s/pallas_call | solution.py:141
  18.0 26.2 %all-to-all-done.qin.refs_4_.refs_6_ = bf16[32,288,128]{2,1,0:T(8,128)(2,1)S(1)} async-done(((bf16[32,288,128]{2,1,0:T(8,128)(2,1)}), bf16[32,288,128]{2,1,0:T(8,128)(2,1)S(1)}, u32[]{:S(2)}, u32[]{:S(2)}) %all-to-all-start) | async-done | bytes 2359328 | tf_op jit(solution)/shard_map/all_to_all | solution.py:524
  45.6 5.3 %all-to-all-start.2 = ((bf16[32,640,128]{2,1,0:T(8,128)(2,1)}), bf16[32,640,128]{2,1,0:T(8,128)(2,1)}, u32[]{:S(2)}, u32[]{:S(2)}) async-start(bf16[32,640,128]{2,1,0:T(8,128)(2,1)} %get-tuple-element.35), calls=%async_computation.2 | async-start | bytes 10485760 | tf_op jit(solution)/shard_map/all_to_all | solution.py:524
  51.0 2.7 %collective-permute-start.11 = (bf16[512,128]{1,0:T(8,128)(2,1)S(1)}, bf16[512,128]{1,0:T(8,128)(2,1)S(1)}, u32[]{:S(2)}, u32[]{:S(2)}) collective-permute-start(bf16[512,128]{1,0:T(8,128)(2,1)S(1)} %get-tuple-element.45), channel_id=1, source_target_pairs={{0,48},{8,56},{16,0},{24,8},{32,16},{40,24},{48,32},{56,40},{64,11... | collective-permute-start | bytes 393224 | tf_op jit(solution)/shard_map/ppermute | solution.py:539
  54.2 2.6 collective-permute-start.2
  57.8 57.0 %collective-permute-done.11 = bf16[512,128]{1,0:T(8,128)(2,1)S(1)} collective-permute-done((bf16[512,128]{1,0:T(8,128)(2,1)S(1)}, bf16[512,128]{1,0:T(8,128)(2,1)S(1)}, u32[]{:S(2)}, u32[]{:S(2)}) %collective-permute-start.11) | collective-permute-done | bytes 131104 | tf_op jit(solution)/shard_map/ppermute | solution.py:539
  118.1 7.2 %collective-permute-start.5 = (bf16[2,512,128]{2,1,0:T(8,128)(2,1)S(1)}, bf16[2,512,128]{2,1,0:T(8,128)(2,1)S(1)}, u32[]{:S(2)}, u32[]{:S(2)}) collective-permute-start(bf16[2,512,128]{2,1,0:T(8,128)(2,1)S(1)} %pad_maximum_fusion.1.rest_1_), channel_id=1, source_target_pairs={{0,16},{8,24},{16,32},{24,40},{32,48},{40,56},{48,0},{56,8},{64,80... | collective-permute-start | bytes 786440 | tf_op jit(solution)/shard_map/ppermute | solution.py:539
  127.6 2.6 collective-permute-done.1
  130.3 1.5 collective-permute-start.13
  131.9 2.2 collective-permute-start.6
  134.4 9.8 %attend.1.mine = bf16[256,1024]{1,0:T(8,128)(2,1)} custom-call(s32[16]{0:T(128)} %get-tuple-element.23.req, s32[8192]{0:T(1024)} %reshape.32.pages, s32[512]{0:T(512)} %hit.1, s32[512]{0:T(512)} %tail.3, bf16[32,288,128]{2,1,0:T(8,128)(2,1)} %copy-done.1, bf16[256,16,256]{2,1,0:T(8,128)(2,1)} %pool.1), custom_call_target="tpu_custom_call" | custom-call | flops 8000000000 | bytes 4000000 | tf_op jit(solution)/shard_map/attend/pallas_call | solution.py:195
  144.2 3.1 %collective-permute-start = (bf16[256,1024]{1,0:T(8,128)(2,1)}, bf16[256,1024]{1,0:T(8,128)(2,1)S(1)}, u32[]{:S(2)}, u32[]{:S(2)}) collective-permute-start(bf16[256,1024]{1,0:T(8,128)(2,1)} %attend.1.mine), channel_id=1, source_target_pairs={{0,8},{8,0},{16,24},{24,16},{32,40},{40,32},{48,56},{56,48},{64,72... | collective-permute-start | bytes 1572872 | tf_op jit(solution)/shard_map/ppermute | solution.py:598
  148.9 2.6 collective-permute-start.17
  152.9 3.6 %collective-permute-done.18.rest_15_ = bf16[2,512,128]{2,1,0:T(8,128)(2,1)S(1)} collective-permute-done((bf16[2,512,128]{2,1,0:T(8,128)(2,1)S(1)}, bf16[2,512,128]{2,1,0:T(8,128)(2,1)S(1)}, u32[]{:S(2)}, u32[]{:S(2)}) %collective-permute-start.18) | collective-permute-done | bytes 262176 | tf_op jit(solution)/shard_map/ppermute | solution.py:539
  156.8 1.7 collective-permute-done.8.rest_6_
  159.5 6.1 %project.1.terms = bf16[32,256,128]{2,1,0:T(8,128)(2,1)} custom-call(s32[1]{0:T(128)} %bitcast.me.refs_0_, s32[1]{0:T(128)} %bitcast.4.head, bf16[256,1024]{1,0:T(8,128)(2,1)} %attend.1.mine, bf16[256,1024]{1,0:T(8,128)(2,1)} %copy-done.13, bf16[2,512,128]{2,1,0:T(8,128)(2,1)} %copy-done.10, bf16[2,512,128]{2,1,0:T(8,128)(2,1)} %copy-done.8, ...), custom_call_target="tpu_custom_call" | custom-call | flops 8000000000 | bytes 11000000 | tf_op jit(solution)/shard_map/project/pallas_call | solution.py:238
  166.8 1.7 collective-permute-start.19
  168.5 4.0 %collective-permute-start.20 = (bf16[6,256,128]{2,1,0:T(8,128)(2,1)S(1)}, bf16[6,256,128]{2,1,0:T(8,128)(2,1)S(1)}, u32[]{:S(2)}, u32[]{:S(2)}) collective-permute-start(bf16[6,256,128]{2,1,0:T(8,128)(2,1)S(1)} %get-tuple-element.41), channel_id=1, source_target_pairs={{0,7},{1,0},{2,1},{3,2},{4,3},{5,4},{6,5},{7,6},{8,15},{9,8},{10,9... | collective-permute-start | bytes 1179656 | tf_op jit(solution)/shard_map/ppermute | solution.py:558
  172.5 7.7 %collective-permute-done.19.up = bf16[6,256,128]{2,1,0:T(8,128)(2,1)S(1)} collective-permute-done((bf16[6,256,128]{2,1,0:T(8,128)(2,1)S(1)}, bf16[6,256,128]{2,1,0:T(8,128)(2,1)S(1)}, u32[]{:S(2)}, u32[]{:S(2)}) %collective-permute-start.19) | collective-permute-done | bytes 393248 | tf_op jit(solution)/shard_map/ppermute | solution.py:558
  181.7 2.7 %relay.1 = (bf16[4,256,128]{2,1,0:T(8,128)(2,1)}, bf16[4,256,128]{2,1,0:T(8,128)(2,1)}, bf16[4,256,128]{2,1,0:T(8,128)(2,1)}, bf16[4,256,128]{2,1,0:T(8,128)(2,1)}) custom-call(bf16[32,256,128]{2,1,0:T(8,128)(2,1)} %project.1.terms, bf16[6,256,128]{2,1,0:T(8,128)(2,1)} %copy-done.14, bf16[6,256,128]{2,1,0:T(8,128)(2,1)} %copy-done.15), custom_call_target="tpu_custom_call" | custom-call | flops 1000000000 | bytes 3000000 | tf_op jit(solution)/shard_map/relay/pallas_call | solution.py:263
  184.5 4.0 %collective-permute-start.22 = (bf16[4,256,128]{2,1,0:T(8,128)(2,1)}, bf16[4,256,128]{2,1,0:T(8,128)(2,1)S(1)}, u32[]{:S(2)}, u32[]{:S(2)}) collective-permute-start(bf16[4,256,128]{2,1,0:T(8,128)(2,1)} %get-tuple-element.27), channel_id=1, source_target_pairs={{0,3},{1,4},{2,5},{3,6},{4,7},{5,0},{6,1},{7,2},{8,11},{9,12},{10,... | collective-permute-start | bytes 786440 | tf_op jit(solution)/shard_map/ppermute | solution.py:558
  188.5 1.7 collective-permute-start.23
  191.4 14.2 %collective-permute-done.22.rest_1_ = bf16[4,256,128]{2,1,0:T(8,128)(2,1)S(1)} collective-permute-done((bf16[4,256,128]{2,1,0:T(8,128)(2,1)}, bf16[4,256,128]{2,1,0:T(8,128)(2,1)S(1)}, u32[]{:S(2)}, u32[]{:S(2)}) %collective-permute-start.22) | collective-permute-done | bytes 262176 | tf_op jit(solution)/shard_map/ppermute | solution.py:558
  206.5 2.7 %total.1 = bf16[32,320,128]{2,1,0:T(8,128)(2,1)} custom-call(s32[32]{0:T(128)} %get-tuple-element.24.both, bf16[32,256,128]{2,1,0:T(8,128)(2,1)} %project.1.terms, bf16[4,256,128]{2,1,0:T(8,128)(2,1)} %copy-done.3, bf16[4,256,128]{2,1,0:T(8,128)(2,1)} %copy-done.4, bf16[4,256,128]{2,1,0:T(8,128)(2,1)} %copy-done.5, ...), custom_call_target="tpu_custom_call", output_to_operand_aliasing={{}: (6, {})} | custom-call | flops 1000000000 | bytes 3000000 | tf_op jit(solution)/shard_map/total/pallas_call | solution.py:295
  209.3 13.7 %all-to-all-start.1 = ((bf16[32,320,128]{2,1,0:T(8,128)(2,1)}), bf16[32,320,128]{2,1,0:T(8,128)(2,1)S(1)}, u32[]{:S(2)}, u32[]{:S(2)}) async-start(bf16[32,320,128]{2,1,0:T(8,128)(2,1)} %total.1), calls=%async_computation.1 | async-start | bytes 5242880 | tf_op jit(solution)/shard_map/all_to_all | solution.py:524
  223.7 5.2 %prepare.1 = (f32[256,1024]{1,0:T(8,128)}, f32[256,1024]{1,0:T(8,128)}, bf16[2,1024,256]{2,1,0:T(8,128)(2,1)}, f32[16,16]{1,0:T(8,128)}) custom-call(s32[1]{0:T(128)} %bitcast.me.refs_0_, s32[512]{0:T(512)} %tail.3, bf16[256,1024]{1,0:T(8,128)(2,1)} %x_ref.1, bf16[256,1024]{1,0:T(8,128)(2,1)} %z_ref.1, bf16[256,128]{1,0:T(8,128)(2,1)} %refs_15_.1, ...), custom_call_target="tpu_custom_call" | custom-call | flops 8000000000 | bytes 5000000 | tf_op jit(solution)/shard_map/prepare/pallas_call | solution.py:360
  228.9 9.0 %shard_map.193 = (bf16[16,16,64,128]{3,2,1,0:T(8,128)(2,1)}, f32[256,768]{1,0:T(8,128)}) custom-call(s32[1]{0:T(128)} %bitcast.me.refs_0_, s32[512]{0:T(512)} %refs_1_.3, f32[16,16]{1,0:T(8,128)} %get-tuple-element.22.refs_2_, bf16[32,640,128]{2,1,0:T(8,128)(2,1)} %all-to-all-done.2.refs_3_.refs_5_, bf16[32,288,128]{2,1,0:T(8,128)(2,1)} %copy-done.1, ...), custom_call_target="tpu_custom_call" | custom-call | flops 4000000000 | bytes 8000000 | tf_op jit(solution)/shard_map/pallas_call | solution.py:506
  237.9 19.0 %all-to-all-done.1.refs_3_.refs_4_.refs_5_.refs_6_.refs_7_.refs_8_.refs_9_.refs_10_.refs_11_.refs_12_.refs_13_.refs_14_ = bf16[32,320,128]{2,1,0:T(8,128)(2,1)S(1)} async-done(((bf16[32,320,128]{2,1,0:T(8,128)(2,1)}), bf16[32,320,128]{2,1,0:T(8,128)(2,1)S(1)}, u32[]{:S(2)}, u32[]{:S(2)}) %all-to-all-start.1) | async-done | bytes 2621472 | tf_op jit(solution)/shard_map/all_to_all | solution.py:524
  256.8 1.5 copy-done
  258.3 5.9 %shard_map.194 = (bf16[16,16,64,128]{3,2,1,0:T(8,128)(2,1)}, bf16[256,1024]{1,0:T(8,128)(2,1)}, bf16[256,512]{1,0:T(8,128)(2,1)}) custom-call(s32[1]{0:T(128)} %bitcast.me.refs_0_, s32[512]{0:T(512)} %refs_1_.3, f32[16,16]{1,0:T(8,128)} %get-tuple-element.22.refs_2_, bf16[32,320,128]{2,1,0:T(8,128)(2,1)} %copy-done, ...), custom_call_target="tpu_custom_call", output_to_operand_aliasing={{0}: (20, {})} | custom-call | flops 4000000000 | bytes 8000000 | tf_op jit(solution)/shard_map/pallas_call | solution.py:506
  (98 shorter events, 18.6 us)
Async XLA Ops:
  4.4 39.8 %all-to-all-start = ((bf16[32,288,128]{2,1,0:T(8,128)(2,1)}), bf16[32,288,128]{2,1,0:T(8,128)(2,1)S(1)}, u32[]{:S(2)}, u32[]{:S(2)}) async-start(bf16[32,288,128]{2,1,0:T(8,128)(2,1)} %get-tuple-element.25), calls=%async_computation | async-start | bytes 4718592 | tf_op jit(solution)/shard_map/all_to_all | solution.py:524
  44.2 82.5 %copy-start.11 = (s32[512,16]{0,1:T(8,128)S(1)}, s32[512,16]{0,1:T(8,128)}, u32[]{:S(2)}) copy-start(s32[512,16]{0,1:T(8,128)} %param.33) | copy-start | bytes 98308
  45.6 163.6 %all-to-all-start.2 = ((bf16[32,640,128]{2,1,0:T(8,128)(2,1)}), bf16[32,640,128]{2,1,0:T(8,128)(2,1)}, u32[]{:S(2)}, u32[]{:S(2)}) async-start(bf16[32,640,128]{2,1,0:T(8,128)(2,1)} %get-tuple-element.35), calls=%async_computation.2 | async-start | bytes 10485760 | tf_op jit(solution)/shard_map/all_to_all | solution.py:524
  51.0 63.9 %collective-permute-start.11 = (bf16[512,128]{1,0:T(8,128)(2,1)S(1)}, bf16[512,128]{1,0:T(8,128)(2,1)S(1)}, u32[]{:S(2)}, u32[]{:S(2)}) collective-permute-start(bf16[512,128]{1,0:T(8,128)(2,1)S(1)} %get-tuple-element.45), channel_id=1, source_target_pairs={{0,48},{8,56},{16,0},{24,8},{32,16},{40,24},{48,32},{56,40},{64,11... | collective-permute-start | bytes 393224 | tf_op jit(solution)/shard_map/ppermute | solution.py:539
  53.7 61.4 %collective-permute-start.12 = (bf16[512,128]{1,0:T(8,128)(2,1)S(1)}, bf16[512,128]{1,0:T(8,128)(2,1)S(1)}, u32[]{:S(2)}, u32[]{:S(2)}) collective-permute-start(bf16[512,128]{1,0:T(8,128)(2,1)S(1)} %get-tuple-element.45), channel_id=1, source_target_pairs={{0,32},{8,40},{16,48},{24,56},{32,0},{40,8},{48,16},{56,24},{64,96... | collective-permute-start | bytes 393224 | tf_op jit(solution)/shard_map/ppermute | solution.py:539
  54.2 63.2 %collective-permute-start.2 = (bf16[512,128]{1,0:T(8,128)(2,1)S(1)}, bf16[512,128]{1,0:T(8,128)(2,1)S(1)}, u32[]{:S(2)}, u32[]{:S(2)}) collective-permute-start(bf16[512,128]{1,0:T(8,128)(2,1)S(1)} %get-tuple-element.46), channel_id=1, source_target_pairs={{0,192},{8,200},{16,208},{24,216},{32,224},{40,232},{48,240},{56,2... | collective-permute-start | bytes 393224 | tf_op jit(solution)/shard_map/ppermute | solution.py:539
  56.8 61.2 %collective-permute-start.3 = (bf16[512,128]{1,0:T(8,128)(2,1)S(1)}, bf16[512,128]{1,0:T(8,128)(2,1)S(1)}, u32[]{:S(2)}, u32[]{:S(2)}) collective-permute-start(bf16[512,128]{1,0:T(8,128)(2,1)S(1)} %get-tuple-element.46), channel_id=1, source_target_pairs={{0,128},{8,136},{16,144},{24,152},{32,160},{40,168},{48,176},{56,1... | collective-permute-start | bytes 393224 | tf_op jit(solution)/shard_map/ppermute | solution.py:539
  57.3 70.3 %collective-permute-start.10 = (bf16[512,128]{1,0:T(8,128)(2,1)S(1)}, bf16[512,128]{1,0:T(8,128)(2,1)S(1)}, u32[]{:S(2)}, u32[]{:S(2)}) collective-permute-start(bf16[512,128]{1,0:T(8,128)(2,1)S(1)} %get-tuple-element.45), channel_id=1, source_target_pairs={{0,16},{8,24},{16,32},{24,40},{32,48},{40,56},{48,0},{56,8},{64,80... | collective-permute-start | bytes 393224 | tf_op jit(solution)/shard_map/ppermute | solution.py:539
  115.1 29.1 %copy-start.7 = (bf16[2,512,128]{2,1,0:T(8,128)(2,1)}, bf16[2,512,128]{2,1,0:T(8,128)(2,1)S(1)}, u32[]{:S(2)}) copy-start(bf16[2,512,128]{2,1,0:T(8,128)(2,1)S(1)} %pad_maximum_fusion.3.rest_9_) | copy-start | bytes 786436
  115.1 15.2 %collective-permute-start.14 = (bf16[2,512,128]{2,1,0:T(8,128)(2,1)S(1)}, bf16[2,512,128]{2,1,0:T(8,128)(2,1)S(1)}, u32[]{:S(2)}, u32[]{:S(2)}) collective-permute-start(bf16[2,512,128]{2,1,0:T(8,128)(2,1)S(1)} %pad_maximum_fusion.3.rest_9_), channel_id=1, source_target_pairs={{0,64},{8,72},{16,80},{24,88},{32,96},{40,104},{48,112},{56,120},{... | collective-permute-start | bytes 786440 | tf_op jit(solution)/shard_map/ppermute | solution.py:539
  118.0 26.1 %copy-start.8 = (bf16[2,512,128]{2,1,0:T(8,128)(2,1)}, bf16[2,512,128]{2,1,0:T(8,128)(2,1)S(1)}, u32[]{:S(2)}) copy-start(bf16[2,512,128]{2,1,0:T(8,128)(2,1)S(1)} %pad_maximum_fusion.1.rest_1_) | copy-start | bytes 786436
  118.1 13.8 %collective-permute-start.5 = (bf16[2,512,128]{2,1,0:T(8,128)(2,1)S(1)}, bf16[2,512,128]{2,1,0:T(8,128)(2,1)S(1)}, u32[]{:S(2)}, u32[]{:S(2)}) collective-permute-start(bf16[2,512,128]{2,1,0:T(8,128)(2,1)S(1)} %pad_maximum_fusion.1.rest_1_), channel_id=1, source_target_pairs={{0,16},{8,24},{16,32},{24,40},{32,48},{40,56},{48,0},{56,8},{64,80... | collective-permute-start | bytes 786440 | tf_op jit(solution)/shard_map/ppermute | solution.py:539
  125.2 8.9 %collective-permute-start.16 = (bf16[2,512,128]{2,1,0:T(8,128)(2,1)S(1)}, bf16[2,512,128]{2,1,0:T(8,128)(2,1)S(1)}, u32[]{:S(2)}, u32[]{:S(2)}) collective-permute-start(bf16[2,512,128]{2,1,0:T(8,128)(2,1)S(1)} %pad_maximum_fusion.3.rest_9_), channel_id=1, source_target_pairs={{0,192},{8,200},{16,208},{24,216},{32,224},{40,232},{48,240},{56,2... | collective-permute-start | bytes 786440 | tf_op jit(solution)/shard_map/ppermute | solution.py:539
  125.2 5.0 %collective-permute-start.1 = (bf16[512,128]{1,0:T(8,128)(2,1)S(1)}, bf16[512,128]{1,0:T(8,128)(2,1)S(1)}, u32[]{:S(2)}, u32[]{:S(2)}) collective-permute-start(bf16[512,128]{1,0:T(8,128)(2,1)S(1)} %get-tuple-element.46), channel_id=1, source_target_pairs={{0,64},{8,72},{16,80},{24,88},{32,96},{40,104},{48,112},{56,120},{... | collective-permute-start | bytes 393224 | tf_op jit(solution)/shard_map/ppermute | solution.py:539
  127.6 16.6 %collective-permute-start.7 = (bf16[2,512,128]{2,1,0:T(8,128)(2,1)S(1)}, bf16[2,512,128]{2,1,0:T(8,128)(2,1)S(1)}, u32[]{:S(2)}, u32[]{:S(2)}) collective-permute-start(bf16[2,512,128]{2,1,0:T(8,128)(2,1)S(1)} %pad_maximum_fusion.1.rest_1_), channel_id=1, source_target_pairs={{0,48},{8,56},{16,0},{24,8},{32,16},{40,24},{48,32},{56,40},{64,11... | collective-permute-start | bytes 786440 | tf_op jit(solution)/shard_map/ppermute | solution.py:539
  130.3 17.1 %collective-permute-start.15 = (bf16[2,512,128]{2,1,0:T(8,128)(2,1)S(1)}, bf16[2,512,128]{2,1,0:T(8,128)(2,1)S(1)}, u32[]{:S(2)}, u32[]{:S(2)}) collective-permute-start(bf16[2,512,128]{2,1,0:T(8,128)(2,1)S(1)} %pad_maximum_fusion.2.rest_8_), channel_id=1, source_target_pairs={{0,192},{8,200},{16,208},{24,216},{32,224},{40,232},{48,240},{56,2... | collective-permute-start | bytes 786440 | tf_op jit(solution)/shard_map/ppermute | solution.py:539
  130.3 17.1 %copy-start.16 = (bf16[2,512,128]{2,1,0:T(8,128)(2,1)}, bf16[2,512,128]{2,1,0:T(8,128)(2,1)S(1)}, u32[]{:S(2)}) copy-start(bf16[2,512,128]{2,1,0:T(8,128)(2,1)S(1)} %collective-permute-done.14.rest_11_) | copy-start | bytes 786436
  130.3 18.6 %collective-permute-start.13 = (bf16[2,512,128]{2,1,0:T(8,128)(2,1)S(1)}, bf16[2,512,128]{2,1,0:T(8,128)(2,1)S(1)}, u32[]{:S(2)}, u32[]{:S(2)}) collective-permute-start(bf16[2,512,128]{2,1,0:T(8,128)(2,1)S(1)} %pad_maximum_fusion.2.rest_8_), channel_id=1, source_target_pairs={{0,64},{8,72},{16,80},{24,88},{32,96},{40,104},{48,112},{56,120},{... | collective-permute-start | bytes 786440 | tf_op jit(solution)/shard_map/ppermute | solution.py:539
  131.9 16.1 %collective-permute-start.6 = (bf16[2,512,128]{2,1,0:T(8,128)(2,1)S(1)}, bf16[2,512,128]{2,1,0:T(8,128)(2,1)S(1)}, u32[]{:S(2)}, u32[]{:S(2)}) collective-permute-start(bf16[2,512,128]{2,1,0:T(8,128)(2,1)S(1)} %pad_maximum_fusion.rest_0_), channel_id=1, source_target_pairs={{0,48},{8,56},{16,0},{24,8},{32,16},{40,24},{48,32},{56,40},{64,11... | collective-permute-start | bytes 786440 | tf_op jit(solution)/shard_map/ppermute | solution.py:539
  134.1 17.5 %collective-permute-start.4 = (bf16[2,512,128]{2,1,0:T(8,128)(2,1)S(1)}, bf16[2,512,128]{2,1,0:T(8,128)(2,1)S(1)}, u32[]{:S(2)}, u32[]{:S(2)}) collective-permute-start(bf16[2,512,128]{2,1,0:T(8,128)(2,1)S(1)} %pad_maximum_fusion.rest_0_), channel_id=1, source_target_pairs={{0,16},{8,24},{16,32},{24,40},{32,48},{40,56},{48,0},{56,8},{64,80... | collective-permute-start | bytes 786440 | tf_op jit(solution)/shard_map/ppermute | solution.py:539
  144.2 14.3 %collective-permute-start = (bf16[256,1024]{1,0:T(8,128)(2,1)}, bf16[256,1024]{1,0:T(8,128)(2,1)S(1)}, u32[]{:S(2)}, u32[]{:S(2)}) collective-permute-start(bf16[256,1024]{1,0:T(8,128)(2,1)} %attend.1.mine), channel_id=1, source_target_pairs={{0,8},{8,0},{16,24},{24,16},{32,40},{40,32},{48,56},{56,48},{64,72... | collective-permute-start | bytes 1572872 | tf_op jit(solution)/shard_map/ppermute | solution.py:598
  147.4 9.1 %collective-permute-start.18 = (bf16[2,512,128]{2,1,0:T(8,128)(2,1)S(1)}, bf16[2,512,128]{2,1,0:T(8,128)(2,1)S(1)}, u32[]{:S(2)}, u32[]{:S(2)}) collective-permute-start(bf16[2,512,128]{2,1,0:T(8,128)(2,1)S(1)} %collective-permute-done.14.rest_11_), channel_id=1, source_target_pairs={{0,64},{8,72},{16,80},{24,88},{32,96},{40,104},{48,112},{56,120},{... | collective-permute-start | bytes 786440 | tf_op jit(solution)/shard_map/ppermute | solution.py:539
  148.0 8.8 %collective-permute-start.9 = (bf16[2,512,128]{2,1,0:T(8,128)(2,1)S(1)}, bf16[2,512,128]{2,1,0:T(8,128)(2,1)S(1)}, u32[]{:S(2)}, u32[]{:S(2)}) collective-permute-start(bf16[2,512,128]{2,1,0:T(8,128)(2,1)S(1)} %collective-permute-done.5.rest_3_), channel_id=1, source_target_pairs={{0,16},{8,24},{16,32},{24,40},{32,48},{40,56},{48,0},{56,8},{64,80... | collective-permute-start | bytes 786440 | tf_op jit(solution)/shard_map/ppermute | solution.py:539
  148.9 7.9 %collective-permute-start.17 = (bf16[2,512,128]{2,1,0:T(8,128)(2,1)S(1)}, bf16[2,512,128]{2,1,0:T(8,128)(2,1)S(1)}, u32[]{:S(2)}, u32[]{:S(2)}) collective-permute-start(bf16[2,512,128]{2,1,0:T(8,128)(2,1)S(1)} %collective-permute-done.15.rest_12_), channel_id=1, source_target_pairs={{0,192},{8,200},{16,208},{24,216},{32,224},{40,232},{48,240},{56,2... | collective-permute-start | bytes 786440 | tf_op jit(solution)/shard_map/ppermute | solution.py:539
  151.6 7.0 %collective-permute-start.8 = (bf16[2,512,128]{2,1,0:T(8,128)(2,1)S(1)}, bf16[2,512,128]{2,1,0:T(8,128)(2,1)S(1)}, u32[]{:S(2)}, u32[]{:S(2)}) collective-permute-start(bf16[2,512,128]{2,1,0:T(8,128)(2,1)S(1)} %collective-permute-done.6.rest_4_), channel_id=1, source_target_pairs={{0,48},{8,56},{16,0},{24,8},{32,16},{40,24},{48,32},{56,40},{64,11... | collective-permute-start | bytes 786440 | tf_op jit(solution)/shard_map/ppermute | solution.py:539
  166.8 13.4 %collective-permute-start.19 = (bf16[6,256,128]{2,1,0:T(8,128)(2,1)S(1)}, bf16[6,256,128]{2,1,0:T(8,128)(2,1)S(1)}, u32[]{:S(2)}, u32[]{:S(2)}) collective-permute-start(bf16[6,256,128]{2,1,0:T(8,128)(2,1)S(1)} %get-tuple-element.42), channel_id=1, source_target_pairs={{0,1},{1,2},{2,3},{3,4},{4,5},{5,6},{6,7},{7,0},{8,9},{9,10},{10,1... | collective-permute-start | bytes 1179656 | tf_op jit(solution)/shard_map/ppermute | solution.py:558
  168.5 11.7 %collective-permute-start.20 = (bf16[6,256,128]{2,1,0:T(8,128)(2,1)S(1)}, bf16[6,256,128]{2,1,0:T(8,128)(2,1)S(1)}, u32[]{:S(2)}, u32[]{:S(2)}) collective-permute-start(bf16[6,256,128]{2,1,0:T(8,128)(2,1)S(1)} %get-tuple-element.41), channel_id=1, source_target_pairs={{0,7},{1,0},{2,1},{3,2},{4,3},{5,4},{6,5},{7,6},{8,15},{9,8},{10,9... | collective-permute-start | bytes 1179656 | tf_op jit(solution)/shard_map/ppermute | solution.py:558
  184.4 7.0 %collective-permute-start.21 = (bf16[4,256,128]{2,1,0:T(8,128)(2,1)}, bf16[4,256,128]{2,1,0:T(8,128)(2,1)S(1)}, u32[]{:S(2)}, u32[]{:S(2)}) collective-permute-start(bf16[4,256,128]{2,1,0:T(8,128)(2,1)} %get-tuple-element.26), channel_id=1, source_target_pairs={{0,1},{1,2},{2,3},{3,4},{4,5},{5,6},{6,7},{7,0},{8,9},{9,10},{10,1... | collective-permute-start | bytes 786440 | tf_op jit(solution)/shard_map/ppermute | solution.py:558
  184.5 21.2 %collective-permute-start.22 = (bf16[4,256,128]{2,1,0:T(8,128)(2,1)}, bf16[4,256,128]{2,1,0:T(8,128)(2,1)S(1)}, u32[]{:S(2)}, u32[]{:S(2)}) collective-permute-start(bf16[4,256,128]{2,1,0:T(8,128)(2,1)} %get-tuple-element.27), channel_id=1, source_target_pairs={{0,3},{1,4},{2,5},{3,6},{4,7},{5,0},{6,1},{7,2},{8,11},{9,12},{10,... | collective-permute-start | bytes 786440 | tf_op jit(solution)/shard_map/ppermute | solution.py:558
  188.5 17.2 %collective-permute-start.23 = (bf16[4,256,128]{2,1,0:T(8,128)(2,1)}, bf16[4,256,128]{2,1,0:T(8,128)(2,1)S(1)}, u32[]{:S(2)}, u32[]{:S(2)}) collective-permute-start(bf16[4,256,128]{2,1,0:T(8,128)(2,1)} %get-tuple-element.28), channel_id=1, source_target_pairs={{0,7},{1,0},{2,1},{3,2},{4,3},{5,4},{6,5},{7,6},{8,15},{9,8},{10,9... | collective-permute-start | bytes 786440 | tf_op jit(solution)/shard_map/ppermute | solution.py:558
  190.1 15.5 %collective-permute-start.24 = (bf16[4,256,128]{2,1,0:T(8,128)(2,1)}, bf16[4,256,128]{2,1,0:T(8,128)(2,1)S(1)}, u32[]{:S(2)}, u32[]{:S(2)}) collective-permute-start(bf16[4,256,128]{2,1,0:T(8,128)(2,1)} %get-tuple-element.29), channel_id=1, source_target_pairs={{0,5},{1,6},{2,7},{3,0},{4,1},{5,2},{6,3},{7,4},{8,13},{9,14},{10,... | collective-permute-start | bytes 786440 | tf_op jit(solution)/shard_map/ppermute | solution.py:558
  209.3 47.6 %all-to-all-start.1 = ((bf16[32,320,128]{2,1,0:T(8,128)(2,1)}), bf16[32,320,128]{2,1,0:T(8,128)(2,1)S(1)}, u32[]{:S(2)}, u32[]{:S(2)}) async-start(bf16[32,320,128]{2,1,0:T(8,128)(2,1)} %total.1), calls=%async_computation.1 | async-start | bytes 5242880 | tf_op jit(solution)/shard_map/all_to_all | solution.py:524
  (24 other events, 158.3 us)

commit v3 on v2

--- a/solution.py
+++ b/solution.py
@@ -381,9 +381,13 @@
     count = STEPS[chunk]
     final_chunk = chunk == CHUNKS - 1
     me, owner, dl = refs[:3]
-    per = 3 if final_chunk else 2
-    held = [refs[3 + per * k : 3 + per * (k + 1)] for k in range(count)]
-    refs = refs[3 + per * count :]
+    i = pl.program_id(0)
+    if final_chunk:
+        got = refs[3]
+        refs = refs[4:]
+    else:
+        held = [refs[3 + 2 * k : 5 + 2 * k] for k in range(count)]
+        refs = refs[3 + 2 * count :]
     b_ref, c_ref, xt, base, ecx = refs[:5]
     refs = refs[5:]
     prev = []
@@ -394,9 +398,9 @@
         gain, fin, out, proj = refs
     else:
         fin, gated_ref = refs
-    i = pl.program_id(0)
     if final_chunk:
-        states = [h[0][0] for h in held]
+        hosts = [owner[me[0] * REQ + count * i + k] for k in range(count)]
+        states = [got[o, :LAST] for o in hosts]
     else:
         states = [jnp.concatenate([h[0][0], h[1][0]], axis=0) for h in held]
     seen = jnp.concatenate(
@@ -417,14 +421,14 @@
             cols = slice(STARTS[c] * HD, (STARTS[c] + SIZES[c]) * HD)
             out[:, cols] = (parts[c] / denom * gain[:, cols]).astype(bf16)
         for k in range(count):
-            upper = (owner[me[0] * REQ + count * i + k] & 1) == 1
+            slabs = [got[hosts[k] // 2 * 2 + c, LAST:] for c in range(2)]
+            upper = (hosts[k] & 1) == 1
             for c in range(4):
-                slab = held[k][1 + c % 2]
                 at = (c // 2) * TAIL
                 proj[k * TAIL : (k + 1) * TAIL, c * DH : (c + 1) * DH] = jnp.where(
                     upper,
-                    slab[0, 2 * TAIL + at : 3 * TAIL + at, :],
-                    slab[0, at : TAIL + at, :],
+                    slabs[c % 2][2 * TAIL + at : 3 * TAIL + at],
+                    slabs[c % 2][at : TAIL + at],
                 )
     else:
         gated_ref[...] = gated
@@ -456,17 +460,6 @@
         return o[m[0] * REQ + count * i + k]
 
     def held(k):
-        if final_chunk:
-            return [
-                pl.BlockSpec((1, LAST, STATE), lambda i, m, o: (who(i, m, o, k), 0, 0)),
-                pl.BlockSpec(
-                    (1, SLAB, STATE), lambda i, m, o: (who(i, m, o, k) // 2 * 2, LAST // SLAB, 0)
-                ),
-                pl.BlockSpec(
-                    (1, SLAB, STATE),
-                    lambda i, m, o: (who(i, m, o, k) // 2 * 2 + 1, LAST // SLAB, 0),
-                ),
-            ]
         return [
             pl.BlockSpec((1, MOST, STATE), lambda i, m, o: (who(i, m, o, k), 0, 0)),
             pl.BlockSpec((1, EARLY, STATE), lambda i, m, o: (who(i, m, o, k), 0, 0)),
@@ -475,7 +468,13 @@
     def span(w, col=0):
         return pl.BlockSpec((rows, w), lambda i, m, o: (i, col))
 
-    in_specs = [SMEM] + [spec for k in range(count) for spec in held(k)]
+    in_specs = [SMEM]
+    if final_chunk:
+        in_specs.append(VMEM)
+        args = [dl, got]
+    else:
+        in_specs += [spec for k in range(count) for spec in held(k)]
+        args = [dl] + list(got) * count
     in_specs += [
         pl.BlockSpec((128, STATE), lambda i, m, o: (i * count // 8, 0)),
         span(STATE),
@@ -483,7 +482,7 @@
         span(width, at),
         span(width, at),
     ]
-    args = [dl] + list(got) * count + [b, c, xt, base, ecx]
+    args += [b, c, xt, base, ecx]
     alias = {}
     if chunk > 0:
         alias = {2 + len(args): 0}
@@ -612,11 +611,12 @@
     )
     gain = norm_gain.reshape(1, -1)
     last = exchange(total(both, terms, parts, packed), "rep")
+    last = pltpu.with_memory_space_constraint(last, pltpu.VMEM)
     fin, rows = scan(
         0, me, owner, dl, (got, asked), group_b, group_c, xt, base, ecx, None, [], gain
     )
     fin, out, projected = scan(
-        1, me, owner, dl, (last,) * 3, group_b, group_c, xt, base, ecx, fin, [rows], gain
+        1, me, owner, dl, last, group_b, group_c, xt, base, ecx, fin, [rows], gain
     )
     return out, projected, fin
 

time: 266 us -> 263 us (0.989)
    unnamed x58 -> x56, local copies, waits for them, and re-layouts: 6.95 us -> 5.51 us
  transfers between devices with their start and end apart: 28 -> 28, of which waited for: 13 -> 13; matrix products, arithmetic and copies ran while one was open for 1% -> 1% of each run, Pallas kernels for 15% -> 16%
where the time goes in v3:
time: 263 us; the launch traced here: 262 us
  waiting for transfers between devices  135 us (51%)
  starting transfers between devices  68.4 us (26%)
  Pallas kernels  49.5 us (19%)
  local copies, waits for them, and re-layouts  7.5 us (3%)
    ppermute x18, waiting for transfers between devices, hop(): return lax.ppermute(v, 'rep', pairs)  67.4 us
    all_to_all x3, waiting for transfers between devices, exchange(): return lax.all_to_all(x, axis, split_axis=0, concat_axis=0, tiled=True)  45.2 us
    all_to_all x3, starting transfers between devices, exchange(): return lax.all_to_all(x, axis, split_axis=0, concat_axis=0, tiled=True)  27.5 us
    ppermute x18, starting transfers between devices, hop(): return lax.ppermute(v, 'rep', pairs)  26.1 us
    ppermute x6, waiting for transfers between devices, turn(): lax.ppermute(v, 'head', [(z, (z + by) % NHEAD) for z in range(NHEAD)])  22.9 us
    pallas_call x2, Pallas kernels, scan(): pl.pallas_call(body, grid_spec=pltpu.PrefetchScalarGridSpec(num_scalar_pr...  14 us
    ppermute x6, starting transfers between devices, turn(): lax.ppermute(v, 'head', [(z, (z + by) % NHEAD) for z in range(NHEAD)])  11.7 us
    pallas_call x1, Pallas kernels, attend(): pl.pallas_call(attend_body, out_shape=sds((TOK, QH * DH), bf16), in_specs...  9.82 us
  transfers between devices with their start and end apart: 28, of which 13 were waited for; matrix products, arithmetic and copies ran while one was open for 1% of the time, Pallas kernels for 16%

profile of v3, /device:TPU:1, one launch (start us, length us, event | category | flops | bytes accessed | tf_op | source)
XLA Modules:
  0.0 262.0 jit_solution(2973555313574404744)
XLA Ops:
  0.6 3.8 %pack_first.1 = (bf16[32,288,128]{2,1,0:T(8,128)(2,1)}, s32[16]{0:T(128)}) custom-call(s32[1]{0:T(128)} %bitcast.me.refs_0_, s32[512]{0:T(512)} %refs_1_.3, s32[512]{0:T(512)} %slot.3, bf16[256,1024]{1,0:T(8,128)(2,1)} %q.1, bf16[256,256]{1,0:T(8,128)(2,1)} %kv.1, bf16[16,1024,128]{2,1,0:T(8,128)(2,1)} %bitcast.16), custom_call_target="tpu_custom_call" | custom-call | tf_op jit(solution)/shard_map/pack_first/pallas_call | solution.py:107
  4.4 8.6 %all-to-all-start = ((bf16[32,288,128]{2,1,0:T(8,128)(2,1)}), bf16[32,288,128]{2,1,0:T(8,128)(2,1)S(1)}, u32[]{:S(2)}, u32[]{:S(2)}) async-start(bf16[32,288,128]{2,1,0:T(8,128)(2,1)} %get-tuple-element.25), calls=%async_computation | async-start | bytes 4718592 | tf_op jit(solution)/shard_map/all_to_all | solution.py:523
  13.0 5.0 %pack_s.1 = (bf16[32,640,128]{2,1,0:T(8,128)(2,1)}, bf16[32,320,128]{2,1,0:T(8,128)(2,1)}, s32[32]{0:T(128)}) custom-call(s32[1]{0:T(128)} %bitcast.me.refs_0_, s32[512]{0:T(512)} %refs_1_.3, s32[512]{0:T(512)} %slot.3, s32[16]{0:T(128)} %get-tuple-element.23.req, bf16[16,1024,128]{2,1,0:T(8,128)(2,1)} %bitcast.17), custom_call_target="tpu_custom_call" | custom-call | tf_op jit(solution)/shard_map/pack_s/pallas_call | solution.py:141
  18.0 26.2 %all-to-all-done.qin.refs_4_.refs_6_ = bf16[32,288,128]{2,1,0:T(8,128)(2,1)S(1)} async-done(((bf16[32,288,128]{2,1,0:T(8,128)(2,1)}), bf16[32,288,128]{2,1,0:T(8,128)(2,1)S(1)}, u32[]{:S(2)}, u32[]{:S(2)}) %all-to-all-start) | async-done | bytes 2359328 | tf_op jit(solution)/shard_map/all_to_all | solution.py:523
  45.6 5.3 %all-to-all-start.2 = ((bf16[32,640,128]{2,1,0:T(8,128)(2,1)}), bf16[32,640,128]{2,1,0:T(8,128)(2,1)}, u32[]{:S(2)}, u32[]{:S(2)}) async-start(bf16[32,640,128]{2,1,0:T(8,128)(2,1)} %get-tuple-element.35), calls=%async_computation.2 | async-start | bytes 10485760 | tf_op jit(solution)/shard_map/all_to_all | solution.py:523
  51.0 2.7 %collective-permute-start.11 = (bf16[512,128]{1,0:T(8,128)(2,1)S(1)}, bf16[512,128]{1,0:T(8,128)(2,1)S(1)}, u32[]{:S(2)}, u32[]{:S(2)}) collective-permute-start(bf16[512,128]{1,0:T(8,128)(2,1)S(1)} %get-tuple-element.45), channel_id=1, source_target_pairs={{0,48},{8,56},{16,0},{24,8},{32,16},{40,24},{48,32},{56,40},{64,11... | collective-permute-start | bytes 393224 | tf_op jit(solution)/shard_map/ppermute | solution.py:538
  54.2 2.6 collective-permute-start.2
  57.8 57.0 %collective-permute-done.11 = bf16[512,128]{1,0:T(8,128)(2,1)S(1)} collective-permute-done((bf16[512,128]{1,0:T(8,128)(2,1)S(1)}, bf16[512,128]{1,0:T(8,128)(2,1)S(1)}, u32[]{:S(2)}, u32[]{:S(2)}) %collective-permute-start.11) | collective-permute-done | bytes 131104 | tf_op jit(solution)/shard_map/ppermute | solution.py:538
  118.1 7.2 %collective-permute-start.5 = (bf16[2,512,128]{2,1,0:T(8,128)(2,1)S(1)}, bf16[2,512,128]{2,1,0:T(8,128)(2,1)S(1)}, u32[]{:S(2)}, u32[]{:S(2)}) collective-permute-start(bf16[2,512,128]{2,1,0:T(8,128)(2,1)S(1)} %pad_maximum_fusion.1.rest_1_), channel_id=1, source_target_pairs={{0,16},{8,24},{16,32},{24,40},{32,48},{40,56},{48,0},{56,8},{64,80... | collective-permute-start | bytes 786440 | tf_op jit(solution)/shard_map/ppermute | solution.py:538
  125.2 1.5 collective-permute-start.1
  127.6 2.6 %collective-permute-done.1 = bf16[512,128]{1,0:T(8,128)(2,1)S(1)} collective-permute-done((bf16[512,128]{1,0:T(8,128)(2,1)S(1)}, bf16[512,128]{1,0:T(8,128)(2,1)S(1)}, u32[]{:S(2)}, u32[]{:S(2)}) %collective-permute-start.1) | collective-permute-done | bytes 131104 | tf_op jit(solution)/shard_map/ppermute | solution.py:538
  130.3 1.5 collective-permute-start.13
  131.9 2.2 collective-permute-start.6
  134.4 9.8 %attend.1.mine = bf16[256,1024]{1,0:T(8,128)(2,1)} custom-call(s32[16]{0:T(128)} %get-tuple-element.23.req, s32[8192]{0:T(1024)} %reshape.32.pages, s32[512]{0:T(512)} %hit.1, s32[512]{0:T(512)} %tail.3, bf16[32,288,128]{2,1,0:T(8,128)(2,1)} %copy-done, bf16[256,16,256]{2,1,0:T(8,128)(2,1)} %pool.1), custom_call_target="tpu_custom_call" | custom-call | flops 8000000000 | bytes 4000000 | tf_op jit(solution)/shard_map/attend/pallas_call | solution.py:195
  144.2 3.1 %collective-permute-start = (bf16[256,1024]{1,0:T(8,128)(2,1)}, bf16[256,1024]{1,0:T(8,128)(2,1)S(1)}, u32[]{:S(2)}, u32[]{:S(2)}) collective-permute-start(bf16[256,1024]{1,0:T(8,128)(2,1)} %attend.1.mine), channel_id=1, source_target_pairs={{0,8},{8,0},{16,24},{24,16},{32,40},{40,32},{48,56},{56,48},{64,72... | collective-permute-start | bytes 1572872 | tf_op jit(solution)/shard_map/ppermute | solution.py:597
  148.9 2.6 %collective-permute-start.17 = (bf16[2,512,128]{2,1,0:T(8,128)(2,1)S(1)}, bf16[2,512,128]{2,1,0:T(8,128)(2,1)S(1)}, u32[]{:S(2)}, u32[]{:S(2)}) collective-permute-start(bf16[2,512,128]{2,1,0:T(8,128)(2,1)S(1)} %collective-permute-done.15.rest_12_), channel_id=1, source_target_pairs={{0,192},{8,200},{16,208},{24,216},{32,224},{40,232},{48,240},{56,2... | collective-permute-start | bytes 786440 | tf_op jit(solution)/shard_map/ppermute | solution.py:538
  152.9 3.6 %collective-permute-done.18.rest_15_ = bf16[2,512,128]{2,1,0:T(8,128)(2,1)S(1)} collective-permute-done((bf16[2,512,128]{2,1,0:T(8,128)(2,1)S(1)}, bf16[2,512,128]{2,1,0:T(8,128)(2,1)S(1)}, u32[]{:S(2)}, u32[]{:S(2)}) %collective-permute-start.18) | collective-permute-done | bytes 262176 | tf_op jit(solution)/shard_map/ppermute | solution.py:538
  156.8 1.7 collective-permute-done.8.rest_6_
  159.5 6.1 %project.1.terms = bf16[32,256,128]{2,1,0:T(8,128)(2,1)} custom-call(s32[1]{0:T(128)} %bitcast.me.refs_0_, s32[1]{0:T(128)} %bitcast.4.head, bf16[256,1024]{1,0:T(8,128)(2,1)} %attend.1.mine, bf16[256,1024]{1,0:T(8,128)(2,1)} %copy-done.12, bf16[2,512,128]{2,1,0:T(8,128)(2,1)} %copy-done.9, bf16[2,512,128]{2,1,0:T(8,128)(2,1)} %copy-done.7, ...), custom_call_target="tpu_custom_call" | custom-call | flops 8000000000 | bytes 11000000 | tf_op jit(solution)/shard_map/project/pallas_call | solution.py:238
  166.8 1.7 collective-permute-start.19
  168.5 4.0 %collective-permute-start.20 = (bf16[6,256,128]{2,1,0:T(8,128)(2,1)S(1)}, bf16[6,256,128]{2,1,0:T(8,128)(2,1)S(1)}, u32[]{:S(2)}, u32[]{:S(2)}) collective-permute-start(bf16[6,256,128]{2,1,0:T(8,128)(2,1)S(1)} %get-tuple-element.41), channel_id=1, source_target_pairs={{0,7},{1,0},{2,1},{3,2},{4,3},{5,4},{6,5},{7,6},{8,15},{9,8},{10,9... | collective-permute-start | bytes 1179656 | tf_op jit(solution)/shard_map/ppermute | solution.py:557
  172.5 7.7 %collective-permute-done.19.up = bf16[6,256,128]{2,1,0:T(8,128)(2,1)S(1)} collective-permute-done((bf16[6,256,128]{2,1,0:T(8,128)(2,1)S(1)}, bf16[6,256,128]{2,1,0:T(8,128)(2,1)S(1)}, u32[]{:S(2)}, u32[]{:S(2)}) %collective-permute-start.19) | collective-permute-done | bytes 393248 | tf_op jit(solution)/shard_map/ppermute | solution.py:557
  181.7 2.7 %relay.1 = (bf16[4,256,128]{2,1,0:T(8,128)(2,1)}, bf16[4,256,128]{2,1,0:T(8,128)(2,1)}, bf16[4,256,128]{2,1,0:T(8,128)(2,1)}, bf16[4,256,128]{2,1,0:T(8,128)(2,1)}) custom-call(bf16[32,256,128]{2,1,0:T(8,128)(2,1)} %project.1.terms, bf16[6,256,128]{2,1,0:T(8,128)(2,1)} %copy-done.13, bf16[6,256,128]{2,1,0:T(8,128)(2,1)} %copy-done.14), custom_call_target="tpu_custom_call" | custom-call | flops 1000000000 | bytes 3000000 | tf_op jit(solution)/shard_map/relay/pallas_call | solution.py:263
  184.5 4.0 %collective-permute-start.22 = (bf16[4,256,128]{2,1,0:T(8,128)(2,1)}, bf16[4,256,128]{2,1,0:T(8,128)(2,1)S(1)}, u32[]{:S(2)}, u32[]{:S(2)}) collective-permute-start(bf16[4,256,128]{2,1,0:T(8,128)(2,1)} %get-tuple-element.27), channel_id=1, source_target_pairs={{0,3},{1,4},{2,5},{3,6},{4,7},{5,0},{6,1},{7,2},{8,11},{9,12},{10,... | collective-permute-start | bytes 786440 | tf_op jit(solution)/shard_map/ppermute | solution.py:557
  188.5 1.7 collective-permute-start.23
  191.4 14.2 %collective-permute-done.22.rest_1_ = bf16[4,256,128]{2,1,0:T(8,128)(2,1)S(1)} collective-permute-done((bf16[4,256,128]{2,1,0:T(8,128)(2,1)}, bf16[4,256,128]{2,1,0:T(8,128)(2,1)S(1)}, u32[]{:S(2)}, u32[]{:S(2)}) %collective-permute-start.22) | collective-permute-done | bytes 262176 | tf_op jit(solution)/shard_map/ppermute | solution.py:557
  206.5 2.8 %total.1 = bf16[32,320,128]{2,1,0:T(8,128)(2,1)} custom-call(s32[32]{0:T(128)} %get-tuple-element.24.both, bf16[32,256,128]{2,1,0:T(8,128)(2,1)} %project.1.terms, bf16[4,256,128]{2,1,0:T(8,128)(2,1)} %copy-done.2, bf16[4,256,128]{2,1,0:T(8,128)(2,1)} %copy-done.3, bf16[4,256,128]{2,1,0:T(8,128)(2,1)} %copy-done.4, ...), custom_call_target="tpu_custom_call", output_to_operand_aliasing={{}: (6, {})} | custom-call | flops 1000000000 | bytes 3000000 | tf_op jit(solution)/shard_map/total/pallas_call | solution.py:295
  209.3 13.6 %all-to-all-start.1 = ((bf16[32,320,128]{2,1,0:T(8,128)(2,1)}), bf16[32,320,128]{2,1,0:T(8,128)(2,1)S(1)}, u32[]{:S(2)}, u32[]{:S(2)}) async-start(bf16[32,320,128]{2,1,0:T(8,128)(2,1)} %total.1), calls=%async_computation.1 | async-start | bytes 5242880 | tf_op jit(solution)/shard_map/all_to_all | solution.py:523
  223.7 5.2 %prepare.1 = (f32[256,1024]{1,0:T(8,128)}, f32[256,1024]{1,0:T(8,128)}, bf16[2,1024,256]{2,1,0:T(8,128)(2,1)}, f32[16,16]{1,0:T(8,128)}) custom-call(s32[1]{0:T(128)} %bitcast.me.refs_0_, s32[512]{0:T(512)} %tail.3, bf16[256,1024]{1,0:T(8,128)(2,1)} %x_ref.1, bf16[256,1024]{1,0:T(8,128)(2,1)} %z_ref.1, bf16[256,128]{1,0:T(8,128)(2,1)} %refs_4_.1, ...), custom_call_target="tpu_custom_call" | custom-call | flops 8000000000 | bytes 5000000 | tf_op jit(solution)/shard_map/prepare/pallas_call | solution.py:360
  228.9 9.0 %shard_map.193 = (bf16[16,16,64,128]{3,2,1,0:T(8,128)(2,1)}, f32[256,768]{1,0:T(8,128)}) custom-call(s32[1]{0:T(128)} %bitcast.me.refs_0_, s32[512]{0:T(512)} %refs_1_.3, f32[16,16]{1,0:T(8,128)} %get-tuple-element.22.refs_2_, bf16[32,640,128]{2,1,0:T(8,128)(2,1)} %all-to-all-done.2.refs_3_.refs_5_, bf16[32,288,128]{2,1,0:T(8,128)(2,1)} %copy-done, ...), custom_call_target="tpu_custom_call" | custom-call | flops 4000000000 | bytes 8000000 | tf_op jit(solution)/shard_map/pallas_call | solution.py:505
  237.9 19.0 %all-to-all-done.1.refs_3_ = bf16[32,320,128]{2,1,0:T(8,128)(2,1)S(1)} async-done(((bf16[32,320,128]{2,1,0:T(8,128)(2,1)}), bf16[32,320,128]{2,1,0:T(8,128)(2,1)S(1)}, u32[]{:S(2)}, u32[]{:S(2)}) %all-to-all-start.1) | async-done | bytes 2621472 | tf_op jit(solution)/shard_map/all_to_all | solution.py:523
  256.8 5.0 %shard_map.194 = (bf16[16,16,64,128]{3,2,1,0:T(8,128)(2,1)}, bf16[256,1024]{1,0:T(8,128)(2,1)}, bf16[256,512]{1,0:T(8,128)(2,1)}) custom-call(s32[1]{0:T(128)} %bitcast.me.refs_0_, s32[512]{0:T(512)} %refs_1_.3, f32[16,16]{1,0:T(8,128)} %get-tuple-element.22.refs_2_, ...), custom_call_target="tpu_custom_call", output_to_operand_aliasing={{0}: (9, {})} | custom-call | flops 4000000000 | bytes 8000000 | tf_op jit(solution)/shard_map/pallas_call | solution.py:505
  (96 shorter events, 17.1 us)
Async XLA Ops:
  4.4 39.8 %all-to-all-start = ((bf16[32,288,128]{2,1,0:T(8,128)(2,1)}), bf16[32,288,128]{2,1,0:T(8,128)(2,1)S(1)}, u32[]{:S(2)}, u32[]{:S(2)}) async-start(bf16[32,288,128]{2,1,0:T(8,128)(2,1)} %get-tuple-element.25), calls=%async_computation | async-start | bytes 4718592 | tf_op jit(solution)/shard_map/all_to_all | solution.py:523
  44.2 82.5 %copy-start.10 = (s32[512,16]{0,1:T(8,128)S(1)}, s32[512,16]{0,1:T(8,128)}, u32[]{:S(2)}) copy-start(s32[512,16]{0,1:T(8,128)} %param.33) | copy-start | bytes 98308
  45.6 163.7 %all-to-all-start.2 = ((bf16[32,640,128]{2,1,0:T(8,128)(2,1)}), bf16[32,640,128]{2,1,0:T(8,128)(2,1)}, u32[]{:S(2)}, u32[]{:S(2)}) async-start(bf16[32,640,128]{2,1,0:T(8,128)(2,1)} %get-tuple-element.35), calls=%async_computation.2 | async-start | bytes 10485760 | tf_op jit(solution)/shard_map/all_to_all | solution.py:523
  51.0 63.9 %collective-permute-start.11 = (bf16[512,128]{1,0:T(8,128)(2,1)S(1)}, bf16[512,128]{1,0:T(8,128)(2,1)S(1)}, u32[]{:S(2)}, u32[]{:S(2)}) collective-permute-start(bf16[512,128]{1,0:T(8,128)(2,1)S(1)} %get-tuple-element.45), channel_id=1, source_target_pairs={{0,48},{8,56},{16,0},{24,8},{32,16},{40,24},{48,32},{56,40},{64,11... | collective-permute-start | bytes 393224 | tf_op jit(solution)/shard_map/ppermute | solution.py:538
  53.7 61.4 %collective-permute-start.12 = (bf16[512,128]{1,0:T(8,128)(2,1)S(1)}, bf16[512,128]{1,0:T(8,128)(2,1)S(1)}, u32[]{:S(2)}, u32[]{:S(2)}) collective-permute-start(bf16[512,128]{1,0:T(8,128)(2,1)S(1)} %get-tuple-element.45), channel_id=1, source_target_pairs={{0,32},{8,40},{16,48},{24,56},{32,0},{40,8},{48,16},{56,24},{64,96... | collective-permute-start | bytes 393224 | tf_op jit(solution)/shard_map/ppermute | solution.py:538
  54.2 63.2 %collective-permute-start.2 = (bf16[512,128]{1,0:T(8,128)(2,1)S(1)}, bf16[512,128]{1,0:T(8,128)(2,1)S(1)}, u32[]{:S(2)}, u32[]{:S(2)}) collective-permute-start(bf16[512,128]{1,0:T(8,128)(2,1)S(1)} %get-tuple-element.46), channel_id=1, source_target_pairs={{0,192},{8,200},{16,208},{24,216},{32,224},{40,232},{48,240},{56,2... | collective-permute-start | bytes 393224 | tf_op jit(solution)/shard_map/ppermute | solution.py:538
  56.8 61.2 %collective-permute-start.3 = (bf16[512,128]{1,0:T(8,128)(2,1)S(1)}, bf16[512,128]{1,0:T(8,128)(2,1)S(1)}, u32[]{:S(2)}, u32[]{:S(2)}) collective-permute-start(bf16[512,128]{1,0:T(8,128)(2,1)S(1)} %get-tuple-element.46), channel_id=1, source_target_pairs={{0,128},{8,136},{16,144},{24,152},{32,160},{40,168},{48,176},{56,1... | collective-permute-start | bytes 393224 | tf_op jit(solution)/shard_map/ppermute | solution.py:538
  57.3 70.3 %collective-permute-start.10 = (bf16[512,128]{1,0:T(8,128)(2,1)S(1)}, bf16[512,128]{1,0:T(8,128)(2,1)S(1)}, u32[]{:S(2)}, u32[]{:S(2)}) collective-permute-start(bf16[512,128]{1,0:T(8,128)(2,1)S(1)} %get-tuple-element.45), channel_id=1, source_target_pairs={{0,16},{8,24},{16,32},{24,40},{32,48},{40,56},{48,0},{56,8},{64,80... | collective-permute-start | bytes 393224 | tf_op jit(solution)/shard_map/ppermute | solution.py:538
  115.1 29.1 %copy-start.6 = (bf16[2,512,128]{2,1,0:T(8,128)(2,1)}, bf16[2,512,128]{2,1,0:T(8,128)(2,1)S(1)}, u32[]{:S(2)}) copy-start(bf16[2,512,128]{2,1,0:T(8,128)(2,1)S(1)} %pad_maximum_fusion.3.rest_9_) | copy-start | bytes 786436
  115.1 15.2 %collective-permute-start.14 = (bf16[2,512,128]{2,1,0:T(8,128)(2,1)S(1)}, bf16[2,512,128]{2,1,0:T(8,128)(2,1)S(1)}, u32[]{:S(2)}, u32[]{:S(2)}) collective-permute-start(bf16[2,512,128]{2,1,0:T(8,128)(2,1)S(1)} %pad_maximum_fusion.3.rest_9_), channel_id=1, source_target_pairs={{0,64},{8,72},{16,80},{24,88},{32,96},{40,104},{48,112},{56,120},{... | collective-permute-start | bytes 786440 | tf_op jit(solution)/shard_map/ppermute | solution.py:538
  118.0 26.1 %copy-start.7 = (bf16[2,512,128]{2,1,0:T(8,128)(2,1)}, bf16[2,512,128]{2,1,0:T(8,128)(2,1)S(1)}, u32[]{:S(2)}) copy-start(bf16[2,512,128]{2,1,0:T(8,128)(2,1)S(1)} %pad_maximum_fusion.1.rest_1_) | copy-start | bytes 786436
  118.1 13.8 %collective-permute-start.5 = (bf16[2,512,128]{2,1,0:T(8,128)(2,1)S(1)}, bf16[2,512,128]{2,1,0:T(8,128)(2,1)S(1)}, u32[]{:S(2)}, u32[]{:S(2)}) collective-permute-start(bf16[2,512,128]{2,1,0:T(8,128)(2,1)S(1)} %pad_maximum_fusion.1.rest_1_), channel_id=1, source_target_pairs={{0,16},{8,24},{16,32},{24,40},{32,48},{40,56},{48,0},{56,8},{64,80... | collective-permute-start | bytes 786440 | tf_op jit(solution)/shard_map/ppermute | solution.py:538
  125.2 8.9 %collective-permute-start.16 = (bf16[2,512,128]{2,1,0:T(8,128)(2,1)S(1)}, bf16[2,512,128]{2,1,0:T(8,128)(2,1)S(1)}, u32[]{:S(2)}, u32[]{:S(2)}) collective-permute-start(bf16[2,512,128]{2,1,0:T(8,128)(2,1)S(1)} %pad_maximum_fusion.3.rest_9_), channel_id=1, source_target_pairs={{0,192},{8,200},{16,208},{24,216},{32,224},{40,232},{48,240},{56,2... | collective-permute-start | bytes 786440 | tf_op jit(solution)/shard_map/ppermute | solution.py:538
  125.2 5.0 %collective-permute-start.1 = (bf16[512,128]{1,0:T(8,128)(2,1)S(1)}, bf16[512,128]{1,0:T(8,128)(2,1)S(1)}, u32[]{:S(2)}, u32[]{:S(2)}) collective-permute-start(bf16[512,128]{1,0:T(8,128)(2,1)S(1)} %get-tuple-element.46), channel_id=1, source_target_pairs={{0,64},{8,72},{16,80},{24,88},{32,96},{40,104},{48,112},{56,120},{... | collective-permute-start | bytes 393224 | tf_op jit(solution)/shard_map/ppermute | solution.py:538
  127.6 16.6 %collective-permute-start.7 = (bf16[2,512,128]{2,1,0:T(8,128)(2,1)S(1)}, bf16[2,512,128]{2,1,0:T(8,128)(2,1)S(1)}, u32[]{:S(2)}, u32[]{:S(2)}) collective-permute-start(bf16[2,512,128]{2,1,0:T(8,128)(2,1)S(1)} %pad_maximum_fusion.1.rest_1_), channel_id=1, source_target_pairs={{0,48},{8,56},{16,0},{24,8},{32,16},{40,24},{48,32},{56,40},{64,11... | collective-permute-start | bytes 786440 | tf_op jit(solution)/shard_map/ppermute | solution.py:538
  130.3 17.1 %collective-permute-start.15 = (bf16[2,512,128]{2,1,0:T(8,128)(2,1)S(1)}, bf16[2,512,128]{2,1,0:T(8,128)(2,1)S(1)}, u32[]{:S(2)}, u32[]{:S(2)}) collective-permute-start(bf16[2,512,128]{2,1,0:T(8,128)(2,1)S(1)} %pad_maximum_fusion.2.rest_8_), channel_id=1, source_target_pairs={{0,192},{8,200},{16,208},{24,216},{32,224},{40,232},{48,240},{56,2... | collective-permute-start | bytes 786440 | tf_op jit(solution)/shard_map/ppermute | solution.py:538
  130.3 17.1 %copy-start.15 = (bf16[2,512,128]{2,1,0:T(8,128)(2,1)}, bf16[2,512,128]{2,1,0:T(8,128)(2,1)S(1)}, u32[]{:S(2)}) copy-start(bf16[2,512,128]{2,1,0:T(8,128)(2,1)S(1)} %collective-permute-done.14.rest_11_) | copy-start | bytes 786436
  130.3 18.6 %collective-permute-start.13 = (bf16[2,512,128]{2,1,0:T(8,128)(2,1)S(1)}, bf16[2,512,128]{2,1,0:T(8,128)(2,1)S(1)}, u32[]{:S(2)}, u32[]{:S(2)}) collective-permute-start(bf16[2,512,128]{2,1,0:T(8,128)(2,1)S(1)} %pad_maximum_fusion.2.rest_8_), channel_id=1, source_target_pairs={{0,64},{8,72},{16,80},{24,88},{32,96},{40,104},{48,112},{56,120},{... | collective-permute-start | bytes 786440 | tf_op jit(solution)/shard_map/ppermute | solution.py:538
  131.9 16.1 %collective-permute-start.6 = (bf16[2,512,128]{2,1,0:T(8,128)(2,1)S(1)}, bf16[2,512,128]{2,1,0:T(8,128)(2,1)S(1)}, u32[]{:S(2)}, u32[]{:S(2)}) collective-permute-start(bf16[2,512,128]{2,1,0:T(8,128)(2,1)S(1)} %pad_maximum_fusion.rest_0_), channel_id=1, source_target_pairs={{0,48},{8,56},{16,0},{24,8},{32,16},{40,24},{48,32},{56,40},{64,11... | collective-permute-start | bytes 786440 | tf_op jit(solution)/shard_map/ppermute | solution.py:538
  134.1 17.5 %collective-permute-start.4 = (bf16[2,512,128]{2,1,0:T(8,128)(2,1)S(1)}, bf16[2,512,128]{2,1,0:T(8,128)(2,1)S(1)}, u32[]{:S(2)}, u32[]{:S(2)}) collective-permute-start(bf16[2,512,128]{2,1,0:T(8,128)(2,1)S(1)} %pad_maximum_fusion.rest_0_), channel_id=1, source_target_pairs={{0,16},{8,24},{16,32},{24,40},{32,48},{40,56},{48,0},{56,8},{64,80... | collective-permute-start | bytes 786440 | tf_op jit(solution)/shard_map/ppermute | solution.py:538
  144.2 14.3 %collective-permute-start = (bf16[256,1024]{1,0:T(8,128)(2,1)}, bf16[256,1024]{1,0:T(8,128)(2,1)S(1)}, u32[]{:S(2)}, u32[]{:S(2)}) collective-permute-start(bf16[256,1024]{1,0:T(8,128)(2,1)} %attend.1.mine), channel_id=1, source_target_pairs={{0,8},{8,0},{16,24},{24,16},{32,40},{40,32},{48,56},{56,48},{64,72... | collective-permute-start | bytes 1572872 | tf_op jit(solution)/shard_map/ppermute | solution.py:597
  147.4 9.1 %collective-permute-start.18 = (bf16[2,512,128]{2,1,0:T(8,128)(2,1)S(1)}, bf16[2,512,128]{2,1,0:T(8,128)(2,1)S(1)}, u32[]{:S(2)}, u32[]{:S(2)}) collective-permute-start(bf16[2,512,128]{2,1,0:T(8,128)(2,1)S(1)} %collective-permute-done.14.rest_11_), channel_id=1, source_target_pairs={{0,64},{8,72},{16,80},{24,88},{32,96},{40,104},{48,112},{56,120},{... | collective-permute-start | bytes 786440 | tf_op jit(solution)/shard_map/ppermute | solution.py:538
  148.0 8.8 %collective-permute-start.9 = (bf16[2,512,128]{2,1,0:T(8,128)(2,1)S(1)}, bf16[2,512,128]{2,1,0:T(8,128)(2,1)S(1)}, u32[]{:S(2)}, u32[]{:S(2)}) collective-permute-start(bf16[2,512,128]{2,1,0:T(8,128)(2,1)S(1)} %collective-permute-done.5.rest_3_), channel_id=1, source_target_pairs={{0,16},{8,24},{16,32},{24,40},{32,48},{40,56},{48,0},{56,8},{64,80... | collective-permute-start | bytes 786440 | tf_op jit(solution)/shard_map/ppermute | solution.py:538
  148.9 7.9 %collective-permute-start.17 = (bf16[2,512,128]{2,1,0:T(8,128)(2,1)S(1)}, bf16[2,512,128]{2,1,0:T(8,128)(2,1)S(1)}, u32[]{:S(2)}, u32[]{:S(2)}) collective-permute-start(bf16[2,512,128]{2,1,0:T(8,128)(2,1)S(1)} %collective-permute-done.15.rest_12_), channel_id=1, source_target_pairs={{0,192},{8,200},{16,208},{24,216},{32,224},{40,232},{48,240},{56,2... | collective-permute-start | bytes 786440 | tf_op jit(solution)/shard_map/ppermute | solution.py:538
  151.6 7.0 %collective-permute-start.8 = (bf16[2,512,128]{2,1,0:T(8,128)(2,1)S(1)}, bf16[2,512,128]{2,1,0:T(8,128)(2,1)S(1)}, u32[]{:S(2)}, u32[]{:S(2)}) collective-permute-start(bf16[2,512,128]{2,1,0:T(8,128)(2,1)S(1)} %collective-permute-done.6.rest_4_), channel_id=1, source_target_pairs={{0,48},{8,56},{16,0},{24,8},{32,16},{40,24},{48,32},{56,40},{64,11... | collective-permute-start | bytes 786440 | tf_op jit(solution)/shard_map/ppermute | solution.py:538
  166.8 13.4 %collective-permute-start.19 = (bf16[6,256,128]{2,1,0:T(8,128)(2,1)S(1)}, bf16[6,256,128]{2,1,0:T(8,128)(2,1)S(1)}, u32[]{:S(2)}, u32[]{:S(2)}) collective-permute-start(bf16[6,256,128]{2,1,0:T(8,128)(2,1)S(1)} %get-tuple-element.42), channel_id=1, source_target_pairs={{0,1},{1,2},{2,3},{3,4},{4,5},{5,6},{6,7},{7,0},{8,9},{9,10},{10,1... | collective-permute-start | bytes 1179656 | tf_op jit(solution)/shard_map/ppermute | solution.py:557
  168.5 11.7 %collective-permute-start.20 = (bf16[6,256,128]{2,1,0:T(8,128)(2,1)S(1)}, bf16[6,256,128]{2,1,0:T(8,128)(2,1)S(1)}, u32[]{:S(2)}, u32[]{:S(2)}) collective-permute-start(bf16[6,256,128]{2,1,0:T(8,128)(2,1)S(1)} %get-tuple-element.41), channel_id=1, source_target_pairs={{0,7},{1,0},{2,1},{3,2},{4,3},{5,4},{6,5},{7,6},{8,15},{9,8},{10,9... | collective-permute-start | bytes 1179656 | tf_op jit(solution)/shard_map/ppermute | solution.py:557
  184.5 7.0 %collective-permute-start.21 = (bf16[4,256,128]{2,1,0:T(8,128)(2,1)}, bf16[4,256,128]{2,1,0:T(8,128)(2,1)S(1)}, u32[]{:S(2)}, u32[]{:S(2)}) collective-permute-start(bf16[4,256,128]{2,1,0:T(8,128)(2,1)} %get-tuple-element.26), channel_id=1, source_target_pairs={{0,1},{1,2},{2,3},{3,4},{4,5},{5,6},{6,7},{7,0},{8,9},{9,10},{10,1... | collective-permute-start | bytes 786440 | tf_op jit(solution)/shard_map/ppermute | solution.py:557
  184.5 21.2 %collective-permute-start.22 = (bf16[4,256,128]{2,1,0:T(8,128)(2,1)}, bf16[4,256,128]{2,1,0:T(8,128)(2,1)S(1)}, u32[]{:S(2)}, u32[]{:S(2)}) collective-permute-start(bf16[4,256,128]{2,1,0:T(8,128)(2,1)} %get-tuple-element.27), channel_id=1, source_target_pairs={{0,3},{1,4},{2,5},{3,6},{4,7},{5,0},{6,1},{7,2},{8,11},{9,12},{10,... | collective-permute-start | bytes 786440 | tf_op jit(solution)/shard_map/ppermute | solution.py:557
  188.5 17.2 %collective-permute-start.23 = (bf16[4,256,128]{2,1,0:T(8,128)(2,1)}, bf16[4,256,128]{2,1,0:T(8,128)(2,1)S(1)}, u32[]{:S(2)}, u32[]{:S(2)}) collective-permute-start(bf16[4,256,128]{2,1,0:T(8,128)(2,1)} %get-tuple-element.28), channel_id=1, source_target_pairs={{0,7},{1,0},{2,1},{3,2},{4,3},{5,4},{6,5},{7,6},{8,15},{9,8},{10,9... | collective-permute-start | bytes 786440 | tf_op jit(solution)/shard_map/ppermute | solution.py:557
  190.1 15.5 %collective-permute-start.24 = (bf16[4,256,128]{2,1,0:T(8,128)(2,1)}, bf16[4,256,128]{2,1,0:T(8,128)(2,1)S(1)}, u32[]{:S(2)}, u32[]{:S(2)}) collective-permute-start(bf16[4,256,128]{2,1,0:T(8,128)(2,1)} %get-tuple-element.29), channel_id=1, source_target_pairs={{0,5},{1,6},{2,7},{3,0},{4,1},{5,2},{6,3},{7,4},{8,13},{9,14},{10,... | collective-permute-start | bytes 786440 | tf_op jit(solution)/shard_map/ppermute | solution.py:557
  209.3 47.5 %all-to-all-start.1 = ((bf16[32,320,128]{2,1,0:T(8,128)(2,1)}), bf16[32,320,128]{2,1,0:T(8,128)(2,1)S(1)}, u32[]{:S(2)}, u32[]{:S(2)}) async-start(bf16[32,320,128]{2,1,0:T(8,128)(2,1)} %total.1), calls=%async_computation.1 | async-start | bytes 5242880 | tf_op jit(solution)/shard_map/all_to_all | solution.py:523
  (23 other events, 156.8 us)
